TPU v7x, 256 devices: a 8x8x2 block of a 8x8x16 slice. The times are simulated.
256 devices in a mesh: grp: 2 (over z), tp: 128 (over y, x, core).
Axes of the slice: x: 8, y: 8, z: 2, core: 2. Of those that a mesh axis runs over, the one named last changes fastest.
The devices are a block of a 8x8x16 slice.
Arguments:
- hidden: bfloat16 [1024, 16384], P('grp', 'tp'), parts along dimension 0, may hold values from -36 to 36
- norm_gain: float32 [16384], P('tp'), may hold values from 0.3 to 10, as said below
- prefix: int32 [2], P('grp'), parts along dimension 0, may hold values from 0 to 8192
- w_query: bfloat16 [16384, 16384], P(None, 'tp'), may hold values from -0.046875 to 0.046875
- w_kv: bfloat16 [2048, 16384], P('tp'), may hold values from -0.046875 to 0.046875
- w_scale: float32 [18432], P('tp'), may hold values from 0.25 to 4
Outputs:
- queries: bfloat16 [1024, 16384], P('grp', 'tp'), parts along dimension 0
- keys: bfloat16 [1024, 16384], P('grp', 'tp'), parts along dimension 0
- values: bfloat16 [1024, 16384], P('grp', 'tp'), parts along dimension 0
- payload: bfloat16 [1024, 16384], P('grp', 'tp'), parts along dimension 0
- row_scale: float32 [1024], P('grp'), parts along dimension 0
There are 2 independent parts, one for each index of `grp`. A program takes and returns all parts, laid end to end along the dimension named above; an argument that names none is the same for every part. Nothing has to cross between parts.
Inputs may be any that keep to these rules, and one draw needn't show every extreme that they name: `norm_gain`: positive.
All inputs are finite; a program needn't handle non-finite values. Where the computation divides by a largest or mean magnitude, that divisor is 1e-20 or more.
Results may differ from a plain program's by a relative error of at most 0.012.
Values may be sent and summed in bfloat16 or wider, within the bound.
No kernel may reach another device: no remote copies, remote signals or barrier semaphores. Data moves between devices by JAX's collectives and lax.ppermute only.
A program may use at most 64 MiB of HBM per device.

v0:
```python
import math

import jax
import jax.numpy as jnp
from jax import lax
from jax.experimental import pallas as pl
from jax.experimental.pallas import tpu as pltpu
from jax.sharding import PartitionSpec as P


HD = 128
KV_COLS_DEV = 8
norm_eps = 1e-05
tiny_eps = 1e-06
rope_base = 500000.0

VMEM = 24 * 2**20

F32 = jnp.float32
BF16 = jnp.bfloat16
STAT = 16


def split2(v):
    hi = v.astype(BF16)
    return hi, (v - hi.astype(F32)).astype(BF16)


def prep_kernel(core, hidden, gain, keep, send):
    half = keep.shape[0] - STAT
    for out, which in ((keep, core[0]), (send, 1 - core[0])):
        h = hidden[pl.ds(pl.multiple_of(which * half, half), half), :].astype(F32)
        weighted = h * gain[...]
        out[:half, :] = weighted.astype(BF16)
        squares = jnp.sum(jnp.transpose(h * h), axis=0, keepdims=True)
        largest = jnp.max(jnp.transpose(jnp.abs(weighted)), axis=0, keepdims=True)
        rows = []
        for v in (squares, largest):
            for part in split2(v):
                part = part.astype(F32)
                rows += [part[:, :128], part[:, 128:]]
        rows.append(jnp.zeros((STAT - len(rows), 128), F32))
        out[half:, :] = jnp.concatenate(rows, axis=0).astype(BF16)


def combine_kernel(core, keep, recv, out):
    half = keep.shape[0] - STAT
    first = core[0] == 0
    mine, other = keep[:half, :], recv[:half, :]
    left = jnp.where(first, mine.astype(F32), other.astype(F32)).astype(BF16)
    right = jnp.where(first, other.astype(F32), mine.astype(F32)).astype(BF16)
    a, b = keep[half:, :].astype(F32), recv[half:, :].astype(F32)

    def wide(s, r):
        return jnp.concatenate([s[r : r + 1], s[r + 1 : r + 2]], axis=1)

    squares = (wide(a, 0) + wide(a, 2)) + (wide(b, 0) + wide(b, 2))
    largest = jnp.maximum(wide(a, 4) + wide(a, 6), wide(b, 4) + wide(b, 6))
    rows = [p.astype(F32) for v in (squares, largest) for p in split2(v)]
    rows.append(jnp.zeros((STAT - len(rows), rows[0].shape[1]), F32))
    stats = jnp.concatenate(rows, axis=0).astype(BF16)
    for s in range(out.shape[0]):
        out[s, :half, :128] = left
        out[s, :half, 128:] = right
        out[s, half:, :] = stats


def weights_kernel(core, wq, wo, kv, ko, w_all, kv_all, w_buf, kv_buf, sems):
    n = w_buf.shape[0]
    kb = w_buf.shape[1]
    hw = wq.shape[2]
    rows = kv.shape[0]
    side = math.isqrt(n)

    def fetches(i):
        b = jnp.where(core[0] == 0, i, (i % side) * side + i // side)
        at = pl.ds(pl.multiple_of(b * kb, kb), kb)
        return (
            pltpu.make_async_copy(wq.at[b], w_buf.at[i, :, pl.ds(0, hw)], sems.at[0, i]),
            pltpu.make_async_copy(wo.at[b], w_buf.at[i, :, pl.ds(hw, hw)], sems.at[1, i]),
            pltpu.make_async_copy(kv.at[:, at], kv_buf.at[i, pl.ds(0, rows), :], sems.at[2, i]),
            pltpu.make_async_copy(ko.at[:, at], kv_buf.at[i, pl.ds(rows, rows), :], sems.at[3, i]),
        )

    def stores(i):
        return (
            pltpu.make_async_copy(w_buf.at[i], w_all.at[i], sems.at[4, i]),
            pltpu.make_async_copy(kv_buf.at[i], kv_all.at[i], sems.at[5, i]),
        )

    @pl.loop(0, n)
    def _(i):
        for c in fetches(i):
            c.start()

    @pl.loop(0, n)
    def _(i):
        for c in fetches(i):
            c.wait()
        for c in stores(i):
            c.start()

    @pl.loop(0, n)
    def _(i):
        for c in stores(i):
            c.wait()


def arrange_weights(core, wq, wo, kv, ko):
    n, kb, hw = wq.shape
    hbm = pl.BlockSpec(memory_space=pltpu.HBM)
    out_shape = (
        jax.ShapeDtypeStruct((n, kb, 2 * hw), BF16),
        jax.ShapeDtypeStruct((n, 2 * kv.shape[0], kb), BF16),
    )
    return pl.pallas_call(
        weights_kernel,
        out_shape=out_shape,
        in_specs=[pl.BlockSpec(memory_space=pltpu.SMEM), hbm, hbm, hbm, hbm],
        out_specs=(hbm, hbm),
        scratch_shapes=[pltpu.VMEM(o.shape, o.dtype) for o in out_shape]
        + [pltpu.SemaphoreType.DMA((6, n))],
        compiler_params=pltpu.CompilerParams(vmem_limit_bytes=VMEM),
        cost_estimate=pl.CostEstimate(flops=10**9, bytes_accessed=2 * 10**7, transcendentals=0),
    )(core, wq, wo, kv, ko)


def high_kernel(gathered, high):
    n = gathered.shape[0] // 2
    half = gathered.shape[1] - STAT
    squares, largest = 0.0, 0.0
    for i in range(2 * n):
        s = gathered[i, half:, :].astype(F32)
        squares = squares + (s[0:1] + s[1:2])
        largest = jnp.maximum(largest, s[2:3] + s[3:4])
        if i >= n:
            high[(i - n) * half : (i - n + 1) * half, :] = gathered[i, :half, :]
    rows = [p.astype(F32) for v in (squares, largest) for p in split2(v)]
    rows.append(jnp.zeros((STAT - len(rows), rows[0].shape[1]), F32))
    high[n * half :, :] = jnp.concatenate(rows, axis=0).astype(BF16)


def kv_rows(xs, kvs, kv_in, st_in):
    half = kv_in.shape[1]
    total = kv_in[...]
    squares, largest = st_in[0:1, :], st_in[1:2, :]
    for x, w in zip(xs, kvs):
        n = w.shape[0]
        for i in range(n):
            total = total + lax.dot_general(
                w[i],
                x[i * half : (i + 1) * half, :],
                (((1,), (1,)), ((), ())),
                preferred_element_type=F32,
            )
        if x.shape[0] > n * half:
            s = x[n * half :, :].astype(F32)
            squares = squares + (s[0:1] + s[1:2])
            largest = jnp.maximum(largest, s[2:3] + s[3:4])
    return total, squares, largest


def q_sum(xs, ws, q_in):
    half = q_in.shape[0]
    total = q_in[...]
    for x, w in zip(xs, ws):
        for i in range(w.shape[0]):
            total = total + jnp.dot(
                x[i * half : (i + 1) * half, :], w[i], preferred_element_type=F32
            )
    return total


def fetch(table, m, pairs, sems):
    copies = []
    for i in range(m):
        for j, (whole, buf) in enumerate(pairs):
            n = buf.shape[1]
            at = pl.ds(pl.multiple_of(table[i] * n, n), n)
            copies.append(pltpu.make_async_copy(whole.at[at], buf.at[i], sems.at[j, i]))
    for c in copies:
        c.start()
    for c in copies:
        c.wait()


def matmul_kernel(m, table, *refs):
    xs, w_all, kv_all = refs[:m], refs[m], refs[m + 1]
    q_in, kv_in, st_in, q_out, kv_out, st_out, w_buf, kv_buf, sems = refs[m + 2 :]
    fetch(table, m, ((w_all, w_buf), (kv_all, kv_buf)), sems)
    ws, kvs = [w_buf.at[i] for i in range(m)], [kv_buf.at[i] for i in range(m)]
    q_out[...] = q_sum(xs, ws, q_in)
    total, squares, largest = kv_rows(xs, kvs, kv_in, st_in)
    kv_out[...] = total
    st_out[0:1, :] = squares
    st_out[1:2, :] = largest


def arrivals_call(kernel, out_shape, table, xs, weights, rest, flops, aliases=None):
    m = len(xs)
    n = xs[0].shape[0] // xs[0].shape[1]
    hbm = pl.BlockSpec(memory_space=pltpu.HBM)
    vmem = pl.BlockSpec(memory_space=pltpu.VMEM)
    smem = pl.BlockSpec(memory_space=pltpu.SMEM)
    specs = [smem] + [vmem] * m + [hbm] * len(weights)
    specs += [smem if a.dtype == jnp.int32 else vmem for a in rest]
    return pl.pallas_call(
        kernel,
        out_shape=out_shape,
        in_specs=specs,
        out_specs=tuple(vmem for _ in out_shape),
        scratch_shapes=[pltpu.VMEM((m, n) + w.shape[1:], w.dtype) for w in weights]
        + [pltpu.SemaphoreType.DMA((len(weights), m))],
        input_output_aliases=aliases or {},
        compiler_params=pltpu.CompilerParams(vmem_limit_bytes=VMEM),
        cost_estimate=pl.CostEstimate(flops=flops, bytes_accessed=10**6, transcendentals=0),
    )(table, *xs, *weights, *rest)


def matmul(table, xs, w_all, kv_all, acc):
    m = len(xs)
    out_shape = tuple(jax.ShapeDtypeStruct(a.shape, a.dtype) for a in acc)
    return arrivals_call(
        lambda *refs: matmul_kernel(m, *refs),
        out_shape,
        table,
        xs,
        (w_all, kv_all),
        acc,
        2 * m * xs[0].shape[0] * xs[0].shape[1] * 288,
        {3 + m + i: i for i in range(3)},
    )


def last_kv_kernel(d, m, table, *refs):
    xs, kv_all = refs[:m], refs[m]
    core, kv_in, st_in, kvscale, kcos, ksin, kvt, st_out, kv_buf, sems = refs[m + 1 :]
    fetch(table, m, ((kv_all, kv_buf),), sems)
    t, squares, largest = kv_rows(xs, [kv_buf.at[i] for i in range(m)], kv_in, st_in)
    st_out[0:1, :] = squares
    st_out[1:2, :] = largest
    t = t * (1.0 / jnp.sqrt(squares / d + norm_eps))
    first = core[0] == 0
    mk, mv, ok, ov = t[0:8], t[8:16], t[16:24], t[24:32]
    a = jnp.concatenate([jnp.where(first, mk, ok), jnp.where(first, ok, mk)], axis=0)
    b = jnp.concatenate([jnp.where(first, mv, ov), jnp.where(first, ov, mv)], axis=0)
    a = a * kvscale[:16, :]
    b = b * kvscale[16:, :]
    row = lax.broadcasted_iota(jnp.int32, a.shape, 0)
    swapped = jnp.where(row % 2 == 0, -pltpu.roll(a, a.shape[0] - 1, 0), pltpu.roll(a, 1, 0))
    a = a * kcos[...] + swapped * ksin[...]
    both = jnp.concatenate([a, b], axis=0).astype(BF16)
    for s in range(kvt.shape[0]):
        kvt[s] = both


def last_kv(d, copies, table, core, xs, kv_all, kv, st, kvscale, kcos, ksin):
    m = len(xs)
    out_shape = (
        jax.ShapeDtypeStruct((copies,) + kv.shape, BF16),
        jax.ShapeDtypeStruct(st.shape, F32),
    )
    return arrivals_call(
        lambda *refs: last_kv_kernel(d, m, *refs),
        out_shape,
        table,
        xs,
        (kv_all,),
        [core, kv, st, kvscale, kcos, ksin],
        10**9,
    )


def last_q_kernel(d, m, table, *refs):
    xs, w_all = refs[:m], refs[m]
    q_in, st, wscale, cosine, sine, mine, msg, w_buf, sems = refs[m + 1 :]
    fetch(table, m, ((w_all, w_buf),), sems)
    q = q_sum(xs, [w_buf.at[i] for i in range(m)], q_in)
    half = q.shape[0]
    squares, largest = st[0:1, :], st[1:2, :]
    inv = columns_of(1.0 / jnp.sqrt(squares / d + norm_eps), 128)
    mine[...] = turn(q[:, :128] * inv * wscale[...], cosine[...], sine[...]).astype(BF16)
    msg[:half, :] = q[:, 128:] * inv
    msg[half:, :] = jnp.concatenate(
        [
            squares[:, :128],
            squares[:, 128:],
            largest[:, :128],
            largest[:, 128:],
            jnp.zeros((4, 128), F32),
        ],
        axis=0,
    )


def last_q(d, table, xs, w_all, q, st, wscale, cosine, sine):
    m = len(xs)
    half = q.shape[0]
    out_shape = (
        jax.ShapeDtypeStruct((half, HD), BF16),
        jax.ShapeDtypeStruct((half + 8, HD), F32),
    )
    return arrivals_call(
        lambda *refs: last_q_kernel(d, m, *refs),
        out_shape,
        table,
        xs,
        (w_all,),
        [q, st, wscale, cosine, sine],
        10**9,
    )


def turn(v, cosine, sine):
    lane = lax.broadcasted_iota(jnp.int32, v.shape, 1)
    width = v.shape[1]
    swapped = jnp.where(
        lane % 2 == 0, -pltpu.roll(v, width - 1, 1), pltpu.roll(v, 1, 1)
    )
    return v * cosine + swapped * sine


def columns_of(row, width):
    return jnp.transpose(jnp.broadcast_to(row, (width, row.shape[1])))


def token_kernel(d, core, mine, msg, st, hidden, gain, wscale, cosine, sine, queries, payload, scale):
    half = mine.shape[0]
    c = core[0]
    own = pl.ds(pl.multiple_of(c * half, half), half)
    far = pl.ds(pl.multiple_of((1 - c) * half, half), half)
    queries[own, :] = mine[...]
    queries[far, :] = turn(msg[:half, :] * wscale[...], cosine[...], sine[...]).astype(BF16)
    wide = lambda r: jnp.concatenate(
        [msg[half + r : half + r + 1], msg[half + r + 1 : half + r + 2]], axis=1
    )
    for rows, squares, largest, place in (
        (own, st[0:1, :], st[1:2, :], c),
        (far, wide(0), wide(2), 1 - c),
    ):
        inverse = 1.0 / jnp.sqrt(squares / d + norm_eps)
        row_scale = largest * inverse + tiny_eps
        scale[pl.ds(2 * place, 1), :] = row_scale[:, :128]
        scale[pl.ds(2 * place + 1, 1), :] = row_scale[:, 128:]
        inv = columns_of(inverse, 128)
        rs = columns_of(row_scale, 128)
        normed = hidden[rows, :].astype(F32) * gain[...] * inv
        payload[rows, :] = (normed / rs).astype(BF16)


def head_kernel(core, kvr, keys, values):
    half = kvr.shape[2]
    pieces = kvr.shape[0] // 2
    for part in range(2):
        at = slice(part * half, (part + 1) * half)
        for out, lo in ((keys, 0), (values, 16)):
            t = jnp.concatenate(
                [kvr[2 * i + part, lo : lo + 16, :] for i in range(pieces)], axis=0
            )
            out[at, :] = jnp.transpose(t.astype(F32)).astype(BF16)


def call(kernel, out_shape, core, *args, flops=0):
    return pl.pallas_call(
        kernel,
        out_shape=out_shape,
        in_specs=[pl.BlockSpec(memory_space=pltpu.SMEM)]
        + [pl.BlockSpec(memory_space=pltpu.VMEM)] * len(args),
        compiler_params=pltpu.CompilerParams(vmem_limit_bytes=VMEM),
        cost_estimate=pl.CostEstimate(flops=flops or 10**8, bytes_accessed=10**6, transcendentals=0),
    )(core, *args)


def solution(mesh):
    tp = mesh.shape["tp"]
    side = math.isqrt(tp // 2)
    row = 2 * side

    def index(y, x, c):
        return (y % side) * row + (x % side) * 2 + c

    everyone = [(y, x, c) for y in range(side) for x in range(side) for c in range(2)]
    to_partner = [(index(y, x, c), index(y, x, 1 - c)) for y, x, c in everyone]
    to_row = [(p * side + g, g * row + p) for p in range(row) for g in range(side)]
    first_groups = [[index(y, x, 0) for x in range(side)] for y in range(side)]
    first_groups += [[index(y, x, 1) for y in range(side)] for x in range(side)]
    rows = [[y * row + i for i in range(row)] for y in range(side)]

    def second(v, s):
        pairs = [
            (index(y, x, c), index(y + s, x, c) if c == 0 else index(y, x + s, c))
            for y, x, c in everyone
        ]
        return lax.ppermute(v, "tp", pairs)

    def swap(v):
        return lax.ppermute(v, "tp", to_partner)

    def body(hidden, norm_gain, prefix, w_query, w_kv, w_scale):
        count, width = hidden.shape
        d = width * tp
        half = count // 2
        me = lax.axis_index("tp")
        core = me % 2
        x = (me // 2) % side
        y = me // row
        core1 = core[None].astype(jnp.int32)
        gain = norm_gain[None, :]

        kv_mine = lax.ppermute(w_kv, "tp", to_row)
        wq_other = swap(w_query)
        kvs_mine = lax.ppermute(w_scale[None, HD:], "tp", to_row)

        blk = jax.ShapeDtypeStruct((half + STAT, width), BF16)
        keep, send = call(prep_kernel, (blk, blk), core1, hidden, gain)
        recv = swap(send)
        slots = call(
            combine_kernel,
            jax.ShapeDtypeStruct((side, half + STAT, 2 * width), BF16),
            core1,
            keep,
            recv,
        )
        gathered = lax.all_to_all(
            slots, "tp", split_axis=0, concat_axis=0, tiled=False, axis_index_groups=first_groups
        )
        kv_other = swap(kv_mine)
        kvs_other = swap(kvs_mine)
        w_all, kv_all = arrange_weights(
            core1, w_query.reshape(-1, 2 * width, HD), wq_other.reshape(-1, 2 * width, HD), kv_mine, kv_other
        )

        positions = (prefix[0] + jnp.arange(count, dtype=jnp.int32)).astype(F32)
        pos_own = lax.dynamic_slice_in_dim(positions, core * half, half)
        pos_far = lax.dynamic_slice_in_dim(positions, (1 - core) * half, half)

        def freq(columns):
            pair = (columns % HD // 2).astype(F32)
            return jnp.power(F32(rope_base), -(2.0 * pair) / HD)

        fq = freq(jnp.arange(HD, dtype=jnp.int32))
        ang_own = pos_own[:, None] * fq[None, :]
        ang_far = pos_far[:, None] * fq[None, :]
        fk = freq(x * 2 * KV_COLS_DEV + jnp.arange(2 * KV_COLS_DEV, dtype=jnp.int32))
        ang_k = fk[:, None] * pos_own[None, :]
        ordered = jnp.where(
            core == 0,
            jnp.concatenate([kvs_mine, kvs_other], 0),
            jnp.concatenate([kvs_other, kvs_mine], 0),
        )
        kvscale = jnp.broadcast_to(
            jnp.concatenate(
                [ordered[:, :KV_COLS_DEV].reshape(-1), ordered[:, KV_COLS_DEV:].reshape(-1)]
            )[:, None],
            (4 * KV_COLS_DEV, half),
        )
        qscale = w_scale[None, :HD]
        tables = (
            jnp.cos(ang_own),
            jnp.sin(ang_own),
            jnp.cos(ang_far),
            jnp.sin(ang_far),
            jnp.cos(ang_k),
            jnp.sin(ang_k),
            kvscale,
        )
        zeros = (
            jnp.zeros((half, 2 * HD), F32),
            jnp.zeros((4 * KV_COLS_DEV, half), F32),
            jnp.zeros((8, half), F32),
        )
        coord = jnp.where(core == 0, y, x)

        def table_of(items):
            return jnp.stack([(coord - s) % side * 2 + k for s, k, _ in items]).astype(jnp.int32)

        shifts = [(s, k) for s in range(side) for k in range(2)]
        places = {sk: table_of([(*sk, None)]) for sk in shifts}
        gathered, w_all, kv_all, tables, zeros, places = lax.optimization_barrier(
            (gathered, w_all, kv_all, tables, zeros, places)
        )
        cos_own, sin_own, cos_far, sin_far, cos_k, sin_k, kvscale = tables

        n = side // 2
        low = gathered[:n, :half].reshape(n * half, -1)
        high = pl.pallas_call(
            high_kernel,
            out_shape=jax.ShapeDtypeStruct((n * half + STAT, gathered.shape[2]), BF16),
            compiler_params=pltpu.CompilerParams(vmem_limit_bytes=VMEM),
            cost_estimate=pl.CostEstimate(flops=10**8, bytes_accessed=10**6, transcendentals=0),
        )(gathered)

        def mm(acc, items):
            table = jnp.concatenate([places[s % side, k] for s, k, _ in items])
            return matmul(table, [v for _, _, v in items], w_all, kv_all, acc)

        up = [second(low, 1), second(high, 1)]
        down = [second(low, -1), second(high, -1)]
        acc = mm(zeros, [(0, 0, low), (0, 1, high)])
        last_round = side // 2
        for r in range(1, last_round):
            for k in range(2):
                items = [(r, k, up[k]), (-r, k, down[k])]
                up[k], down[k], acc = lax.optimization_barrier((up[k], down[k], acc))
                if r + 1 < last_round:
                    up[k], down[k] = second(up[k], 1), second(down[k], -1)
                elif k == 0:
                    up[k] = second(up[k], 1)
                else:
                    down[k] = second(down[k], -1)
                acc = mm(acc, items)
        items = [(last_round, 0, up[0]), (-last_round, 1, down[1])]
        xs = [v for _, _, v in items]
        table = jnp.concatenate([places[s % side, k] for s, k, _ in items])
        kvt, st = last_kv(
            d, row, table, core1, xs, kv_all, acc[1], acc[2], kvscale, cos_k, sin_k
        )
        kvr = lax.all_to_all(
            kvt, "tp", split_axis=0, concat_axis=0, tiled=False, axis_index_groups=rows
        )
        mine, msg = last_q(d, table, xs, w_all, acc[0], st, qscale, cos_own, sin_own)
        far = swap(msg)
        out = jax.ShapeDtypeStruct((count, HD), BF16)
        queries, payload, scale = call(
            lambda *r: token_kernel(d, *r),
            (out, out, jax.ShapeDtypeStruct((count // HD, HD), F32)),
            core1,
            mine,
            far,
            st,
            hidden,
            gain,
            qscale,
            cos_far,
            sin_far,
        )
        keys, values = call(head_kernel, (out, out), core1, kvr)
        return queries, keys, values, payload, scale.reshape(count)

    return jax.shard_map(
        body,
        mesh=mesh,
        in_specs=(P("grp", "tp"), P("tp"), P("grp"), P(None, "tp"), P("tp", None), P("tp")),
        out_specs=(P("grp", "tp"), P("grp", "tp"), P("grp", "tp"), P("grp", "tp"), P("grp")),
        check_vma=False,
    )
```

profile of v0, /device:TPU:513, one launch (start us, length us, event | category | flops | bytes accessed | tf_op | source)
XLA Modules:
  0.0 191.0 jit_solution(961684985691874717)
XLA Ops:
  0.6 20.5 %collective-permute-start.1 = (bf16[16384,128]{1,0:T(8,128)(2,1)}, bf16[16384,128]{1,0:T(8,128)(2,1)}, u32[]{:S(2)}, u32[]{:S(2)}) collective-permute-start(bf16[16384,128]{1,0:T(8,128)(2,1)} %param.9), channel_id=1, source_target_pairs={{0,1},{1,0},{2,3},{3,2},{4,5},{5,4},{6,7},{7,6},{8,9},{9,8},{10,11... | collective-permute-start | bytes 12582920 | tf_op jit(solution)/shard_map/ppermute | solution.py:397
  21.2 0.9 copy-done.7
  22.1 0.7 copy-done.9
  22.7 0.2 shard_map.101
  22.9 0.2 collective-permute-start
  23.1 5.2 %collective-permute-done.recv = bf16[272,128]{1,0:T(8,128)(2,1)S(1)} collective-permute-done((bf16[272,128]{1,0:T(8,128)(2,1)S(1)}, bf16[272,128]{1,0:T(8,128)(2,1)S(1)}, u32[]{:S(2)}, u32[]{:S(2)}) %collective-permute-start) | collective-permute-done | bytes 69664 | tf_op jit(solution)/shard_map/ppermute | solution.py:397
  28.3 1.1 shard_map.102
  29.4 3.8 %all-to-all-start = ((bf16[8,272,256]{2,1,0:T(8,128)(2,1)}), bf16[8,272,256]{2,1,0:T(8,128)(2,1)S(1)}, u32[]{:S(2)}, u32[]{:S(2)}) async-start(bf16[8,272,256]{2,1,0:T(8,128)(2,1)} %shard_map.102), calls=%async_computation | async-start | bytes 2228224 | tf_op jit(solution)/shard_map/all_to_all | solution.py:424
  33.2 2.0 %collective-permute-start.2 = (bf16[16,16384]{1,0:T(8,128)(2,1)}, bf16[16,16384]{1,0:T(8,128)(2,1)S(1)}, u32[]{:S(2)}, u32[]{:S(2)}) collective-permute-start(bf16[16,16384]{1,0:T(8,128)(2,1)} %param.10), channel_id=1, source_target_pairs={{0,0},{1,16},{2,32},{3,48},{4,64},{5,80},{6,96},{7,112},{8,1},{9,1... | collective-permute-start | bytes 1572872 | tf_op jit(solution)/shard_map/ppermute | solution.py:410
  35.2 0.7 slice_bitcast_fusion.1
  35.8 5.1 %collective-permute-start.4 = (f32[1,16]{1,0:T(1,128)S(1)}, f32[1,16]{1,0:T(1,128)S(1)}, u32[]{:S(2)}, u32[]{:S(2)}) collective-permute-start(f32[1,16]{1,0:T(1,128)S(1)} %slice_bitcast_fusion.1), channel_id=1, source_target_pairs={{0,0},{1,16},{2,32},{3,48},{4,64},{5,80},{6,96},{7,112},{8,1},{9,1... | collective-permute-start | bytes 200 | tf_op jit(solution)/shard_map/ppermute | solution.py:412
  41.7 0.1 fusion.1
  41.8 1.5 multiply_sine_fusion
  43.3 20.3 %collective-permute-done.2.kv = bf16[16,16384]{1,0:T(8,128)(2,1)S(1)} collective-permute-done((bf16[16,16384]{1,0:T(8,128)(2,1)}, bf16[16,16384]{1,0:T(8,128)(2,1)S(1)}, u32[]{:S(2)}, u32[]{:S(2)}) %collective-permute-start.2) | collective-permute-done | bytes 524320 | tf_op jit(solution)/shard_map/ppermute | solution.py:410
  63.6 0.1 multiply_sine_fusion.2
  63.9 0.6 collective-permute-start.5
  64.5 1.0 collective-permute-done.5
  65.5 0.1 fusion.2
  65.6 0.1 reshape.99
  65.7 0.1 reshape.98
  65.7 0.1 pad_maximum_fusion
  65.8 2.2 %copy-done.4 = bf16[16384,128]{1,0:T(8,128)(2,1)S(1)} copy-done((bf16[16384,128]{1,0:T(8,128)(2,1)S(1)}, bf16[16384,128]{1,0:T(8,128)(2,1)}, u32[]{:S(2)}) %copy-start.4) | copy-done | bytes 4194328
  68.0 19.4 %shard_map.103 = (bf16[64,256,256]{2,1,0:T(8,128)(2,1)S(1)}, bf16[64,32,256]{2,1,0:T(8,128)(2,1)S(1)}) custom-call(s32[1]{0:T(128)} %bitcast.core.refs_4_.r_0_, bf16[64,256,128]{2,1,0:T(8,128)(2,1)S(1)} %bitcast.28, bf16[64,256,128]{2,1,0:T(8,128)(2,1)} %bitcast.3.wo, bf16[16,16384]{1,0:T(8,128)(2,1)S(1)} %collective-permute-done.2.kv, ...), custom_call_target="tpu_custom_call" | custom-call | flops 1000000000 | bytes 20000000 | tf_op jit(solution)/shard_map/pallas_call | solution.py:116
  87.4 3.3 %copy-done = bf16[64,256,256]{2,1,0:T(8,128)(2,1)} copy-done((bf16[64,256,256]{2,1,0:T(8,128)(2,1)}, bf16[64,256,256]{2,1,0:T(8,128)(2,1)S(1)}, u32[]{:S(2)}) %copy-start) | copy-done | bytes 8388632
  90.8 20.4 %collective-permute-start.6 = (bf16[1024,256]{1,0:T(8,128)(2,1)S(1)}, bf16[1024,256]{1,0:T(8,128)(2,1)S(1)}, u32[]{:S(2)}, u32[]{:S(2)}) collective-permute-start(bf16[1024,256]{1,0:T(8,128)(2,1)S(1)} %bitcast.29), channel_id=1, source_target_pairs={{0,16},{1,3},{2,18},{3,5},{4,20},{5,7},{6,22},{7,9},{8,24},{9,11},... | collective-permute-start | bytes 1572872 | tf_op jit(solution)/shard_map/ppermute | solution.py:394
  111.2 10.6 %collective-permute-start.7 = (bf16[1024,256]{1,0:T(8,128)(2,1)S(1)}, bf16[1024,256]{1,0:T(8,128)(2,1)S(1)}, u32[]{:S(2)}, u32[]{:S(2)}) collective-permute-start(bf16[1024,256]{1,0:T(8,128)(2,1)S(1)} %bitcast.30), channel_id=1, source_target_pairs={{0,112},{1,15},{2,114},{3,1},{4,116},{5,3},{6,118},{7,5},{8,120},{... | collective-permute-start | bytes 1572872 | tf_op jit(solution)/shard_map/ppermute | solution.py:394
  121.9 0.1 collective-permute-start.10
  122.1 2.6 %collective-permute-start.11 = (bf16[1040,256]{1,0:T(8,128)(2,1)S(1)}, bf16[1040,256]{1,0:T(8,128)(2,1)S(1)}, u32[]{:S(2)}, u32[]{:S(2)}) collective-permute-start(bf16[1040,256]{1,0:T(8,128)(2,1)S(1)} %shard_map.104.refs_2_), channel_id=1, source_target_pairs={{0,112},{1,15},{2,114},{3,1},{4,116},{5,3},{6,118},{7,5},{8,120},{... | collective-permute-start | bytes 1597448 | tf_op jit(solution)/shard_map/ppermute | solution.py:394
  124.7 0.1 pad_add_fusion.1
  124.9 3.4 %copy-done.1 = bf16[64,256,256]{2,1,0:T(8,128)(2,1)S(1)} copy-done((bf16[64,256,256]{2,1,0:T(8,128)(2,1)S(1)}, bf16[64,256,256]{2,1,0:T(8,128)(2,1)}, u32[]{:S(2)}) %copy-start.1) | copy-done | bytes 8388632
  128.2 1.5 shard_map.105
  129.8 0.1 pad_add_fusion.3.refs_0_
  129.9 0.1 collective-permute-start.8
  130.0 2.6 %collective-permute-start.9 = (bf16[1024,256]{1,0:T(8,128)(2,1)S(1)}, bf16[1024,256]{1,0:T(8,128)(2,1)S(1)}, u32[]{:S(2)}, u32[]{:S(2)}) collective-permute-start(bf16[1024,256]{1,0:T(8,128)(2,1)S(1)} %collective-permute-done.7.refs_2_), channel_id=1, source_target_pairs={{0,112},{1,15},{2,114},{3,1},{4,116},{5,3},{6,118},{7,5},{8,120},{... | collective-permute-start | bytes 1572872 | tf_op jit(solution)/shard_map/ppermute | solution.py:394
  132.6 1.5 shard_map.106
  134.2 0.3 collective-permute-start.14
  134.5 2.6 %collective-permute-start.15 = (bf16[1040,256]{1,0:T(8,128)(2,1)S(1)}, bf16[1040,256]{1,0:T(8,128)(2,1)S(1)}, u32[]{:S(2)}, u32[]{:S(2)}) collective-permute-start(bf16[1040,256]{1,0:T(8,128)(2,1)S(1)} %collective-permute-done.11.refs_2_), channel_id=1, source_target_pairs={{0,112},{1,15},{2,114},{3,1},{4,116},{5,3},{6,118},{7,5},{8,120},{... | collective-permute-start | bytes 1597448 | tf_op jit(solution)/shard_map/ppermute | solution.py:394
  137.1 0.1 pad_add_fusion.5.refs_0_
  137.2 1.5 shard_map.107
  138.8 1.2 collective-permute-done.8.refs_1_
  139.9 2.8 %collective-permute-start.13 = (bf16[1024,256]{1,0:T(8,128)(2,1)S(1)}, bf16[1024,256]{1,0:T(8,128)(2,1)S(1)}, u32[]{:S(2)}, u32[]{:S(2)}) collective-permute-start(bf16[1024,256]{1,0:T(8,128)(2,1)S(1)} %collective-permute-done.9.refs_2_), channel_id=1, source_target_pairs={{0,112},{1,15},{2,114},{3,1},{4,116},{5,3},{6,118},{7,5},{8,120},{... | collective-permute-start | bytes 1572872 | tf_op jit(solution)/shard_map/ppermute | solution.py:394
  142.7 1.5 shard_map.108
  144.3 1.4 collective-permute-done.14.refs_1_
  145.7 2.8 %collective-permute-start.18 = (bf16[1040,256]{1,0:T(8,128)(2,1)S(1)}, bf16[1040,256]{1,0:T(8,128)(2,1)S(1)}, u32[]{:S(2)}, u32[]{:S(2)}) collective-permute-start(bf16[1040,256]{1,0:T(8,128)(2,1)S(1)} %collective-permute-done.15.refs_2_), channel_id=1, source_target_pairs={{0,112},{1,15},{2,114},{3,1},{4,116},{5,3},{6,118},{7,5},{8,120},{... | collective-permute-start | bytes 1597448 | tf_op jit(solution)/shard_map/ppermute | solution.py:394
  148.4 0.1 pad_add_fusion.4.refs_0_
  148.5 0.1 pad_add_fusion.6.refs_0_
  148.6 1.5 shard_map.109
  150.1 1.1 collective-permute-done.12.refs_1_
  151.3 1.5 shard_map.110
  152.8 4.2 %collective-permute-done.17.refs_1_ = bf16[1040,256]{1,0:T(8,128)(2,1)S(1)} collective-permute-done((bf16[1040,256]{1,0:T(8,128)(2,1)S(1)}, bf16[1040,256]{1,0:T(8,128)(2,1)S(1)}, u32[]{:S(2)}, u32[]{:S(2)}) %collective-permute-start.17) | collective-permute-done | bytes 532512 | tf_op jit(solution)/shard_map/ppermute | solution.py:394
  157.0 2.8 %collective-permute-start.19 = (bf16[1040,256]{1,0:T(8,128)(2,1)S(1)}, bf16[1040,256]{1,0:T(8,128)(2,1)S(1)}, u32[]{:S(2)}, u32[]{:S(2)}) collective-permute-start(bf16[1040,256]{1,0:T(8,128)(2,1)S(1)} %collective-permute-done.18.refs_2_), channel_id=1, source_target_pairs={{0,112},{1,15},{2,114},{3,1},{4,116},{5,3},{6,118},{7,5},{8,120},{... | collective-permute-start | bytes 1597448 | tf_op jit(solution)/shard_map/ppermute | solution.py:394
  159.8 0.1 pad_add_fusion.refs_0_
  159.8 0.1 pad_add_fusion.7.refs_0_
  159.9 1.5 shard_map.111
  161.5 7.8 %collective-permute-done.16.refs_1_ = bf16[1024,256]{1,0:T(8,128)(2,1)S(1)} collective-permute-done((bf16[1024,256]{1,0:T(8,128)(2,1)S(1)}, bf16[1024,256]{1,0:T(8,128)(2,1)S(1)}, u32[]{:S(2)}, u32[]{:S(2)}) %collective-permute-start.16) | collective-permute-done | bytes 524320 | tf_op jit(solution)/shard_map/ppermute | solution.py:394
  169.3 1.9 shard_map.112
  171.2 7.2 %all-to-all-start.1 = ((bf16[16,32,256]{2,1,0:T(8,128)(2,1)}), bf16[16,32,256]{2,1,0:T(8,128)(2,1)S(1)}, u32[]{:S(2)}, u32[]{:S(2)}) async-start(bf16[16,32,256]{2,1,0:T(8,128)(2,1)} %get-tuple-element.182), calls=%async_computation.1 | async-start | bytes 524288 | tf_op jit(solution)/shard_map/all_to_all | solution.py:518
  178.5 3.4 %copy-done.3 = bf16[64,256,256]{2,1,0:T(8,128)(2,1)S(1)} copy-done((bf16[64,256,256]{2,1,0:T(8,128)(2,1)S(1)}, bf16[64,256,256]{2,1,0:T(8,128)(2,1)}, u32[]{:S(2)}) %copy-start.3) | copy-done | bytes 8388632
  181.9 1.2 shard_map.113
  183.0 0.6 collective-permute-start.20
  183.6 1.0 collective-permute-done.20.r_2_
  184.6 1.0 shard_map.114
  185.6 4.6 %all-to-all-done.1.kvr = bf16[16,32,256]{2,1,0:T(8,128)(2,1)S(1)} async-done(((bf16[16,32,256]{2,1,0:T(8,128)(2,1)}), bf16[16,32,256]{2,1,0:T(8,128)(2,1)S(1)}, u32[]{:S(2)}, u32[]{:S(2)}) %all-to-all-start.1) | async-done | bytes 262176 | tf_op jit(solution)/shard_map/all_to_all | solution.py:518
  190.2 0.8 shard_map.115
  (46 shorter events, 0.3 us)
Async XLA Ops:
  0.6 65.2 %collective-permute-start.1 = (bf16[16384,128]{1,0:T(8,128)(2,1)}, bf16[16384,128]{1,0:T(8,128)(2,1)}, u32[]{:S(2)}, u32[]{:S(2)}) collective-permute-start(bf16[16384,128]{1,0:T(8,128)(2,1)} %param.9), channel_id=1, source_target_pairs={{0,1},{1,0},{2,3},{3,2},{4,5},{5,4},{6,7},{7,6},{8,9},{9,8},{10,11... | collective-permute-start | bytes 12582920 | tf_op jit(solution)/shard_map/ppermute | solution.py:397
  21.2 0.9 copy-start.7
  22.1 0.7 copy-start.9
  22.9 5.3 %collective-permute-start = (bf16[272,128]{1,0:T(8,128)(2,1)S(1)}, bf16[272,128]{1,0:T(8,128)(2,1)S(1)}, u32[]{:S(2)}, u32[]{:S(2)}) collective-permute-start(bf16[272,128]{1,0:T(8,128)(2,1)S(1)} %get-tuple-element.97), channel_id=1, source_target_pairs={{0,1},{1,0},{2,3},{3,2},{4,5},{5,4},{6,7},{7,6},{8,9},{9,8},{10,11... | collective-permute-start | bytes 208904 | tf_op jit(solution)/shard_map/ppermute | solution.py:397
  29.4 61.3 %all-to-all-start = ((bf16[8,272,256]{2,1,0:T(8,128)(2,1)}), bf16[8,272,256]{2,1,0:T(8,128)(2,1)S(1)}, u32[]{:S(2)}, u32[]{:S(2)}) async-start(bf16[8,272,256]{2,1,0:T(8,128)(2,1)} %shard_map.102), calls=%async_computation | async-start | bytes 2228224 | tf_op jit(solution)/shard_map/all_to_all | solution.py:424
  33.2 30.4 %collective-permute-start.2 = (bf16[16,16384]{1,0:T(8,128)(2,1)}, bf16[16,16384]{1,0:T(8,128)(2,1)S(1)}, u32[]{:S(2)}, u32[]{:S(2)}) collective-permute-start(bf16[16,16384]{1,0:T(8,128)(2,1)} %param.10), channel_id=1, source_target_pairs={{0,0},{1,16},{2,32},{3,48},{4,64},{5,80},{6,96},{7,112},{8,1},{9,1... | collective-permute-start | bytes 1572872 | tf_op jit(solution)/shard_map/ppermute | solution.py:410
  35.8 28.0 %collective-permute-start.4 = (f32[1,16]{1,0:T(1,128)S(1)}, f32[1,16]{1,0:T(1,128)S(1)}, u32[]{:S(2)}, u32[]{:S(2)}) collective-permute-start(f32[1,16]{1,0:T(1,128)S(1)} %slice_bitcast_fusion.1), channel_id=1, source_target_pairs={{0,0},{1,16},{2,32},{3,48},{4,64},{5,80},{6,96},{7,112},{8,1},{9,1... | collective-permute-start | bytes 200 | tf_op jit(solution)/shard_map/ppermute | solution.py:412
  63.6 2.2 %collective-permute-start.3 = (bf16[16,16384]{1,0:T(8,128)(2,1)S(1)}, bf16[16,16384]{1,0:T(8,128)(2,1)S(1)}, u32[]{:S(2)}, u32[]{:S(2)}) collective-permute-start(bf16[16,16384]{1,0:T(8,128)(2,1)S(1)} %collective-permute-done.2.kv), channel_id=1, source_target_pairs={{0,1},{1,0},{2,3},{3,2},{4,5},{5,4},{6,7},{7,6},{8,9},{9,8},{10,11... | collective-permute-start | bytes 1572872 | tf_op jit(solution)/shard_map/ppermute | solution.py:397
  63.9 1.6 collective-permute-start.5
  65.8 2.2 %copy-start.4 = (bf16[16384,128]{1,0:T(8,128)(2,1)S(1)}, bf16[16384,128]{1,0:T(8,128)(2,1)}, u32[]{:S(2)}) copy-start(bf16[16384,128]{1,0:T(8,128)(2,1)} %param.9) | copy-start | bytes 12582916
  87.4 3.3 %copy-start = (bf16[64,256,256]{2,1,0:T(8,128)(2,1)}, bf16[64,256,256]{2,1,0:T(8,128)(2,1)S(1)}, u32[]{:S(2)}) copy-start(bf16[64,256,256]{2,1,0:T(8,128)(2,1)S(1)} %get-tuple-element.105.refs_3_) | copy-start | bytes 25165828
  90.8 39.0 %collective-permute-start.6 = (bf16[1024,256]{1,0:T(8,128)(2,1)S(1)}, bf16[1024,256]{1,0:T(8,128)(2,1)S(1)}, u32[]{:S(2)}, u32[]{:S(2)}) collective-permute-start(bf16[1024,256]{1,0:T(8,128)(2,1)S(1)} %bitcast.29), channel_id=1, source_target_pairs={{0,16},{1,3},{2,18},{3,5},{4,20},{5,7},{6,22},{7,9},{8,24},{9,11},... | collective-permute-start | bytes 1572872 | tf_op jit(solution)/shard_map/ppermute | solution.py:394
  111.2 18.6 %collective-permute-start.7 = (bf16[1024,256]{1,0:T(8,128)(2,1)S(1)}, bf16[1024,256]{1,0:T(8,128)(2,1)S(1)}, u32[]{:S(2)}, u32[]{:S(2)}) collective-permute-start(bf16[1024,256]{1,0:T(8,128)(2,1)S(1)} %bitcast.30), channel_id=1, source_target_pairs={{0,112},{1,15},{2,114},{3,1},{4,116},{5,3},{6,118},{7,5},{8,120},{... | collective-permute-start | bytes 1572872 | tf_op jit(solution)/shard_map/ppermute | solution.py:394
  121.9 12.2 %collective-permute-start.10 = (bf16[1040,256]{1,0:T(8,128)(2,1)S(1)}, bf16[1040,256]{1,0:T(8,128)(2,1)S(1)}, u32[]{:S(2)}, u32[]{:S(2)}) collective-permute-start(bf16[1040,256]{1,0:T(8,128)(2,1)S(1)} %shard_map.104.refs_2_), channel_id=1, source_target_pairs={{0,16},{1,3},{2,18},{3,5},{4,20},{5,7},{6,22},{7,9},{8,24},{9,11},... | collective-permute-start | bytes 1597448 | tf_op jit(solution)/shard_map/ppermute | solution.py:394
  122.1 12.1 %collective-permute-start.11 = (bf16[1040,256]{1,0:T(8,128)(2,1)S(1)}, bf16[1040,256]{1,0:T(8,128)(2,1)S(1)}, u32[]{:S(2)}, u32[]{:S(2)}) collective-permute-start(bf16[1040,256]{1,0:T(8,128)(2,1)S(1)} %shard_map.104.refs_2_), channel_id=1, source_target_pairs={{0,112},{1,15},{2,114},{3,1},{4,116},{5,3},{6,118},{7,5},{8,120},{... | collective-permute-start | bytes 1597448 | tf_op jit(solution)/shard_map/ppermute | solution.py:394
  124.8 3.4 %copy-start.1 = (bf16[64,256,256]{2,1,0:T(8,128)(2,1)S(1)}, bf16[64,256,256]{2,1,0:T(8,128)(2,1)}, u32[]{:S(2)}) copy-start(bf16[64,256,256]{2,1,0:T(8,128)(2,1)} %copy-done) | copy-start | bytes 25165828
  128.2 4.4 %copy-start.2 = (bf16[64,256,256]{2,1,0:T(8,128)(2,1)S(1)}, bf16[64,256,256]{2,1,0:T(8,128)(2,1)}, u32[]{:S(2)}) copy-start(bf16[64,256,256]{2,1,0:T(8,128)(2,1)} %copy-done) | copy-start | bytes 25165828
  129.9 10.1 %collective-permute-start.8 = (bf16[1024,256]{1,0:T(8,128)(2,1)S(1)}, bf16[1024,256]{1,0:T(8,128)(2,1)S(1)}, u32[]{:S(2)}, u32[]{:S(2)}) collective-permute-start(bf16[1024,256]{1,0:T(8,128)(2,1)S(1)} %collective-permute-done.6.refs_1_), channel_id=1, source_target_pairs={{0,16},{1,3},{2,18},{3,5},{4,20},{5,7},{6,22},{7,9},{8,24},{9,11},... | collective-permute-start | bytes 1572872 | tf_op jit(solution)/shard_map/ppermute | solution.py:394
  130.0 10.0 %collective-permute-start.9 = (bf16[1024,256]{1,0:T(8,128)(2,1)S(1)}, bf16[1024,256]{1,0:T(8,128)(2,1)S(1)}, u32[]{:S(2)}, u32[]{:S(2)}) collective-permute-start(bf16[1024,256]{1,0:T(8,128)(2,1)S(1)} %collective-permute-done.7.refs_2_), channel_id=1, source_target_pairs={{0,112},{1,15},{2,114},{3,1},{4,116},{5,3},{6,118},{7,5},{8,120},{... | collective-permute-start | bytes 1572872 | tf_op jit(solution)/shard_map/ppermute | solution.py:394
  134.2 11.5 %collective-permute-start.14 = (bf16[1040,256]{1,0:T(8,128)(2,1)S(1)}, bf16[1040,256]{1,0:T(8,128)(2,1)S(1)}, u32[]{:S(2)}, u32[]{:S(2)}) collective-permute-start(bf16[1040,256]{1,0:T(8,128)(2,1)S(1)} %collective-permute-done.10.refs_1_), channel_id=1, source_target_pairs={{0,16},{1,3},{2,18},{3,5},{4,20},{5,7},{6,22},{7,9},{8,24},{9,11},... | collective-permute-start | bytes 1597448 | tf_op jit(solution)/shard_map/ppermute | solution.py:394
  134.5 11.2 %collective-permute-start.15 = (bf16[1040,256]{1,0:T(8,128)(2,1)S(1)}, bf16[1040,256]{1,0:T(8,128)(2,1)S(1)}, u32[]{:S(2)}, u32[]{:S(2)}) collective-permute-start(bf16[1040,256]{1,0:T(8,128)(2,1)S(1)} %collective-permute-done.11.refs_2_), channel_id=1, source_target_pairs={{0,112},{1,15},{2,114},{3,1},{4,116},{5,3},{6,118},{7,5},{8,120},{... | collective-permute-start | bytes 1597448 | tf_op jit(solution)/shard_map/ppermute | solution.py:394
  139.9 11.3 %collective-permute-start.12 = (bf16[1024,256]{1,0:T(8,128)(2,1)S(1)}, bf16[1024,256]{1,0:T(8,128)(2,1)S(1)}, u32[]{:S(2)}, u32[]{:S(2)}) collective-permute-start(bf16[1024,256]{1,0:T(8,128)(2,1)S(1)} %collective-permute-done.8.refs_1_), channel_id=1, source_target_pairs={{0,16},{1,3},{2,18},{3,5},{4,20},{5,7},{6,22},{7,9},{8,24},{9,11},... | collective-permute-start | bytes 1572872 | tf_op jit(solution)/shard_map/ppermute | solution.py:394
  139.9 11.3 %collective-permute-start.13 = (bf16[1024,256]{1,0:T(8,128)(2,1)S(1)}, bf16[1024,256]{1,0:T(8,128)(2,1)S(1)}, u32[]{:S(2)}, u32[]{:S(2)}) collective-permute-start(bf16[1024,256]{1,0:T(8,128)(2,1)S(1)} %collective-permute-done.9.refs_2_), channel_id=1, source_target_pairs={{0,112},{1,15},{2,114},{3,1},{4,116},{5,3},{6,118},{7,5},{8,120},{... | collective-permute-start | bytes 1572872 | tf_op jit(solution)/shard_map/ppermute | solution.py:394
  145.7 11.3 %collective-permute-start.17 = (bf16[1040,256]{1,0:T(8,128)(2,1)S(1)}, bf16[1040,256]{1,0:T(8,128)(2,1)S(1)}, u32[]{:S(2)}, u32[]{:S(2)}) collective-permute-start(bf16[1040,256]{1,0:T(8,128)(2,1)S(1)} %collective-permute-done.14.refs_1_), channel_id=1, source_target_pairs={{0,16},{1,3},{2,18},{3,5},{4,20},{5,7},{6,22},{7,9},{8,24},{9,11},... | collective-permute-start | bytes 1597448 | tf_op jit(solution)/shard_map/ppermute | solution.py:394
  145.7 11.3 %collective-permute-start.18 = (bf16[1040,256]{1,0:T(8,128)(2,1)S(1)}, bf16[1040,256]{1,0:T(8,128)(2,1)S(1)}, u32[]{:S(2)}, u32[]{:S(2)}) collective-permute-start(bf16[1040,256]{1,0:T(8,128)(2,1)S(1)} %collective-permute-done.15.refs_2_), channel_id=1, source_target_pairs={{0,112},{1,15},{2,114},{3,1},{4,116},{5,3},{6,118},{7,5},{8,120},{... | collective-permute-start | bytes 1597448 | tf_op jit(solution)/shard_map/ppermute | solution.py:394
  157.0 12.3 %collective-permute-start.19 = (bf16[1040,256]{1,0:T(8,128)(2,1)S(1)}, bf16[1040,256]{1,0:T(8,128)(2,1)S(1)}, u32[]{:S(2)}, u32[]{:S(2)}) collective-permute-start(bf16[1040,256]{1,0:T(8,128)(2,1)S(1)} %collective-permute-done.18.refs_2_), channel_id=1, source_target_pairs={{0,112},{1,15},{2,114},{3,1},{4,116},{5,3},{6,118},{7,5},{8,120},{... | collective-permute-start | bytes 1597448 | tf_op jit(solution)/shard_map/ppermute | solution.py:394
  159.8 9.5 %collective-permute-start.16 = (bf16[1024,256]{1,0:T(8,128)(2,1)S(1)}, bf16[1024,256]{1,0:T(8,128)(2,1)S(1)}, u32[]{:S(2)}, u32[]{:S(2)}) collective-permute-start(bf16[1024,256]{1,0:T(8,128)(2,1)S(1)} %collective-permute-done.12.refs_1_), channel_id=1, source_target_pairs={{0,16},{1,3},{2,18},{3,5},{4,20},{5,7},{6,22},{7,9},{8,24},{9,11},... | collective-permute-start | bytes 1572872 | tf_op jit(solution)/shard_map/ppermute | solution.py:394
  161.5 17.0 %copy-start.11 = (f32[144]{0:T(256)S(1)}, f32[144]{0:T(256)}, u32[]{:S(2)}) copy-start(f32[144]{0:T(256)} %param.11) | copy-start | bytes 1732
  171.2 18.9 %all-to-all-start.1 = ((bf16[16,32,256]{2,1,0:T(8,128)(2,1)}), bf16[16,32,256]{2,1,0:T(8,128)(2,1)S(1)}, u32[]{:S(2)}, u32[]{:S(2)}) async-start(bf16[16,32,256]{2,1,0:T(8,128)(2,1)} %get-tuple-element.182), calls=%async_computation.1 | async-start | bytes 524288 | tf_op jit(solution)/shard_map/all_to_all | solution.py:518
  178.5 3.4 %copy-start.3 = (bf16[64,256,256]{2,1,0:T(8,128)(2,1)S(1)}, bf16[64,256,256]{2,1,0:T(8,128)(2,1)}, u32[]{:S(2)}) copy-start(bf16[64,256,256]{2,1,0:T(8,128)(2,1)} %copy-done) | copy-start | bytes 25165828
  181.9 2.8 %copy-start.5 = (f32[256,128]{1,0:T(8,128)S(1)}, f32[256,128]{1,0:T(8,128)}, u32[]{:S(2)}) copy-start(f32[256,128]{1,0:T(8,128)} %get-tuple-element.180.r_8_) | copy-start | bytes 393220
  181.9 2.8 %copy-start.6 = (f32[256,128]{1,0:T(8,128)S(1)}, f32[256,128]{1,0:T(8,128)}, u32[]{:S(2)}) copy-start(f32[256,128]{1,0:T(8,128)} %get-tuple-element.179.r_7_) | copy-start | bytes 393220
  181.9 2.8 %copy-start.8 = (bf16[512,128]{1,0:T(8,128)(2,1)S(1)}, bf16[512,128]{1,0:T(8,128)(2,1)}, u32[]{:S(2)}) copy-start(bf16[512,128]{1,0:T(8,128)(2,1)} %r_4_.1) | copy-start | bytes 393220
  181.9 2.8 %copy-start.10 = (f32[128]{0:T(128)S(1)}, f32[128]{0:T(128)}, u32[]{:S(2)}) copy-start(f32[128]{0:T(128)} %param.7) | copy-start | bytes 1540
  183.0 1.6 collective-permute-start.20
where the time goes:
time: 191 us
  starting transfers between devices  87.9 us (46%)
  waiting for transfers between devices  47.7 us (25%)
  Pallas kernels  36.4 us (19%)
  local copies, waits for them, and re-layouts  15 us (8%)
  other arithmetic  2.35 us (1%)
    ppermute x14, starting transfers between devices, second(): return lax.ppermute(v, 'tp', pairs)  47.9 us
    ppermute x5, starting transfers between devices, swap(): return lax.ppermute(v, 'tp', to_partner)  21.9 us
    ppermute x1, waiting for transfers between devices, body(): kv_mine = lax.ppermute(w_kv, 'tp', to_row)  20.3 us
    pallas_call x1, Pallas kernels, arrange_weights(): pl.pallas_call(weights_kernel, out_shape=out_shape, in_specs=[pl.BlockSpe...  19.4 us
    ppermute x14, waiting for transfers between devices, second(): return lax.ppermute(v, 'tp', pairs)  15.7 us
    unnamed x24, local copies, waits for them, and re-layouts  13.8 us
    pallas_call x9, Pallas kernels, arrivals_call(): pl.pallas_call(kernel, out_shape=out_shape, in_specs=specs, out_specs=tup...  13.8 us
    all_to_all x1, starting transfers between devices, body(): lax.all_to_all(kvt, 'tp', split_axis=0, concat_axis=0, tiled=False, axis_...  7.24 us
  transfers between devices with their start and end apart: 23, of which 10 were waited for; matrix products, arithmetic and copies ran while one was open for 2% of the time, Pallas kernels for 18%

commit v1 on v0

--- a/solution.py
+++ b/solution.py
@@ -120,7 +120,7 @@
         out_specs=(hbm, hbm),
         scratch_shapes=[pltpu.VMEM(o.shape, o.dtype) for o in out_shape]
         + [pltpu.SemaphoreType.DMA((6, n))],
-        compiler_params=pltpu.CompilerParams(vmem_limit_bytes=VMEM),
+        compiler_params=pltpu.CompilerParams(vmem_limit_bytes=60 * 2**20),
         cost_estimate=pl.CostEstimate(flops=10**9, bytes_accessed=2 * 10**7, transcendentals=0),
     )(core, wq, wo, kv, ko)
 
@@ -348,24 +348,30 @@
         payload[rows, :] = (normed / rs).astype(BF16)
 
 
-def head_kernel(core, kvr, keys, values):
+def head_kernel(order, kvr, keys, values, whole):
     half = kvr.shape[2]
-    pieces = kvr.shape[0] // 2
+    chips = kvr.shape[0] // 2
+    n = KV_COLS_DEV
     for part in range(2):
         at = slice(part * half, (part + 1) * half)
-        for out, lo in ((keys, 0), (values, 16)):
-            t = jnp.concatenate(
-                [kvr[2 * i + part, lo : lo + 16, :] for i in range(pieces)], axis=0
-            )
-            out[at, :] = jnp.transpose(t.astype(F32)).astype(BF16)
-
-
-def call(kernel, out_shape, core, *args, flops=0):
+        for i in range(chips):
+            rows = kvr[2 * i + part].astype(F32)
+            for which in range(2):
+                for slot in range(2):
+                    to = pl.ds(pl.multiple_of(order[2 * i + slot] * n, n), n)
+                    lo = (2 * which + slot) * n
+                    whole[which, to, :] = rows[lo : lo + n]
+        for which, out in enumerate((keys, values)):
+            out[at, :] = jnp.transpose(whole[which]).astype(BF16)
+
+
+def call(kernel, out_shape, core, *args, flops=0, scratch=()):
     return pl.pallas_call(
         kernel,
         out_shape=out_shape,
         in_specs=[pl.BlockSpec(memory_space=pltpu.SMEM)]
         + [pl.BlockSpec(memory_space=pltpu.VMEM)] * len(args),
+        scratch_shapes=list(scratch),
         compiler_params=pltpu.CompilerParams(vmem_limit_bytes=VMEM),
         cost_estimate=pl.CostEstimate(flops=flops or 10**8, bytes_accessed=10**6, transcendentals=0),
     )(core, *args)
@@ -381,7 +387,14 @@
 
     everyone = [(y, x, c) for y in range(side) for x in range(side) for c in range(2)]
     to_partner = [(index(y, x, c), index(y, x, 1 - c)) for y, x, c in everyone]
-    to_row = [(p * side + g, g * row + p) for p in range(row) for g in range(side)]
+    heads = tp * KV_COLS_DEV // HD
+    columns = side // 2
+
+    def home(j):
+        y, x = j // row, (j // 2) % side
+        return index(j % heads, x - 1 + (y + x) % columns, y // columns)
+
+    to_row = [(j, home(j)) for j in range(tp)]
     first_groups = [[index(y, x, 0) for x in range(side)] for y in range(side)]
     first_groups += [[index(y, x, 1) for y in range(side)] for x in range(side)]
     rows = [[y * row + i for i in range(row)] for y in range(side)]
@@ -407,6 +420,13 @@
         core1 = core[None].astype(jnp.int32)
         gain = norm_gain[None, :]
 
+        def piece_at(xs, slot):
+            base = y // 2
+            h = jnp.where((xs - base + 1) % side < columns, 0, 1)
+            source = base + columns * h
+            o = (xs - source + 1) % side
+            return 2 * ((o - source) % columns + columns * slot) + h
+
         kv_mine = lax.ppermute(w_kv, "tp", to_row)
         wq_other = swap(w_query)
         kvs_mine = lax.ppermute(w_scale[None, HD:], "tp", to_row)
@@ -441,7 +461,10 @@
         fq = freq(jnp.arange(HD, dtype=jnp.int32))
         ang_own = pos_own[:, None] * fq[None, :]
         ang_far = pos_far[:, None] * fq[None, :]
-        fk = freq(x * 2 * KV_COLS_DEV + jnp.arange(2 * KV_COLS_DEV, dtype=jnp.int32))
+        slots_of = jnp.arange(2 * KV_COLS_DEV, dtype=jnp.int32)
+        fk = freq(piece_at(x, slots_of // KV_COLS_DEV) * KV_COLS_DEV + slots_of % KV_COLS_DEV)
+        seats = jnp.arange(row, dtype=jnp.int32)
+        order = piece_at(seats // 2, seats % 2).astype(jnp.int32)
         ang_k = fk[:, None] * pos_own[None, :]
         ordered = jnp.where(
             core == 0,
@@ -476,8 +499,8 @@
 
         shifts = [(s, k) for s in range(side) for k in range(2)]
         places = {sk: table_of([(*sk, None)]) for sk in shifts}
-        gathered, w_all, kv_all, tables, zeros, places = lax.optimization_barrier(
-            (gathered, w_all, kv_all, tables, zeros, places)
+        gathered, w_all, kv_all, tables, zeros, places, order = lax.optimization_barrier(
+            (gathered, w_all, kv_all, tables, zeros, places, order)
         )
         cos_own, sin_own, cos_far, sin_far, cos_k, sin_k, kvscale = tables
 
@@ -534,7 +557,9 @@
             cos_far,
             sin_far,
         )
-        keys, values = call(head_kernel, (out, out), core1, kvr)
+        keys, values = call(
+            head_kernel, (out, out), order, kvr, scratch=[pltpu.VMEM((2, HD, half), F32)]
+        )
         return queries, keys, values, payload, scale.reshape(count)
 
     return jax.shard_map(

time: 191 us -> 153 us (0.80)
  starting transfers between devices: 87.9 us -> 56 us
  Pallas kernels: 36.4 us -> 28.6 us
  waiting for transfers between devices: 47.7 us -> 53.3 us
  local copies, waits for them, and re-layouts: 15 us -> 11.5 us
    ppermute x14, starting transfers between devices: 47.9 us -> 18.8 us  [second(): return lax.ppermute(v, 'tp', pairs)]
    pallas_call x1, Pallas kernels: 19.4 us -> 11 us  [arrange_weights(): pl.pallas_call(weights_kernel, out_shape=out_shape, in_specs=[pl.BlockSpe...]
    ppermute x1, waiting for transfers between devices: 20.3 us -> 25.5 us  [body(): kv_mine = lax.ppermute(w_kv, 'tp', to_row)]
    ppermute x1, starting transfers between devices: 5.07 us -> 0.88 us  [body(): kvs_mine = lax.ppermute(w_scale[None, HD:], 'tp', to_row)]
    unnamed x24, local copies, waits for them, and re-layouts: 13.8 us -> 10.4 us
  transfers between devices with their start and end apart: 23 -> 23, of which waited for: 10 -> 10; matrix products, arithmetic and copies ran while one was open for 2% -> 2% of each run, Pallas kernels for 18% -> 17%
where the time goes in v1:
time: 153 us
  starting transfers between devices  56 us (37%)
  waiting for transfers between devices  53.3 us (35%)
  Pallas kernels  28.6 us (19%)
  local copies, waits for them, and re-layouts  11.5 us (8%)
  other arithmetic  1.83 us (1%)
  between operations  1.66 us (1%)
    ppermute x1, waiting for transfers between devices, body(): kv_mine = lax.ppermute(w_kv, 'tp', to_row)  25.5 us
    ppermute x5, starting transfers between devices, swap(): return lax.ppermute(v, 'tp', to_partner)  23.3 us
    ppermute x14, starting transfers between devices, second(): return lax.ppermute(v, 'tp', pairs)  18.8 us
    ppermute x14, waiting for transfers between devices, second(): return lax.ppermute(v, 'tp', pairs)  15.6 us
    pallas_call x9, Pallas kernels, arrivals_call(): pl.pallas_call(kernel, out_shape=out_shape, in_specs=specs, out_specs=tup...  13.8 us
    pallas_call x1, Pallas kernels, arrange_weights(): pl.pallas_call(weights_kernel, out_shape=out_shape, in_specs=[pl.BlockSpe...  11 us
    unnamed x24, local copies, waits for them, and re-layouts  10.4 us
    all_to_all x1, starting transfers between devices, body(): lax.all_to_all(kvt, 'tp', split_axis=0, concat_axis=0, tiled=False, axis_...  9.12 us
  transfers between devices with their start and end apart: 23, of which 10 were waited for; matrix products, arithmetic and copies ran while one was open for 2% of the time, Pallas kernels for 17%

profile of v1, /device:TPU:513, one launch (start us, length us, event | category | flops | bytes accessed | tf_op | source)
XLA Modules:
  0.0 152.8 jit_solution(16603499707444012164)
XLA Ops:
  0.6 20.5 %collective-permute-start.1 = (bf16[16384,128]{1,0:T(8,128)(2,1)}, bf16[16384,128]{1,0:T(8,128)(2,1)}, u32[]{:S(2)}, u32[]{:S(2)}) collective-permute-start(bf16[16384,128]{1,0:T(8,128)(2,1)} %param.9), channel_id=1, source_target_pairs={{0,1},{1,0},{2,3},{3,2},{4,5},{5,4},{6,7},{7,6},{8,9},{9,8},{10,11... | collective-permute-start | bytes 12582920 | tf_op jit(solution)/shard_map/ppermute | solution.py:410
  21.2 0.9 copy-done.5
  22.1 0.7 copy-done.7
  22.7 0.2 shard_map.101
  22.9 0.2 collective-permute-start
  23.1 5.2 %collective-permute-done.recv = bf16[272,128]{1,0:T(8,128)(2,1)S(1)} collective-permute-done((bf16[272,128]{1,0:T(8,128)(2,1)S(1)}, bf16[272,128]{1,0:T(8,128)(2,1)S(1)}, u32[]{:S(2)}, u32[]{:S(2)}) %collective-permute-start) | collective-permute-done | bytes 69664 | tf_op jit(solution)/shard_map/ppermute | solution.py:410
  28.3 1.1 shard_map.102
  29.4 3.8 %all-to-all-start = ((bf16[8,272,256]{2,1,0:T(8,128)(2,1)}), bf16[8,272,256]{2,1,0:T(8,128)(2,1)S(1)}, u32[]{:S(2)}, u32[]{:S(2)}) async-start(bf16[8,272,256]{2,1,0:T(8,128)(2,1)} %shard_map.102), calls=%async_computation | async-start | bytes 2228224 | tf_op jit(solution)/shard_map/all_to_all | solution.py:444
  33.2 0.1 collective-permute-start.2
  33.3 0.7 slice_bitcast_fusion.1
  34.0 0.9 collective-permute-start.4
  35.7 0.1 fusion.15
  35.8 0.1 multiply_sine_fusion.2
  35.9 1.0 multiply_sine_fusion
  36.9 25.5 %collective-permute-done.2.kv = bf16[16,16384]{1,0:T(8,128)(2,1)S(1)} collective-permute-done((bf16[16,16384]{1,0:T(8,128)(2,1)}, bf16[16,16384]{1,0:T(8,128)(2,1)S(1)}, u32[]{:S(2)}, u32[]{:S(2)}) %collective-permute-start.2) | collective-permute-done | bytes 524320 | tf_op jit(solution)/shard_map/ppermute | solution.py:430
  62.4 1.7 %collective-permute-start.3 = (bf16[16,16384]{1,0:T(8,128)(2,1)S(1)}, bf16[16,16384]{1,0:T(8,128)(2,1)S(1)}, u32[]{:S(2)}, u32[]{:S(2)}) collective-permute-start(bf16[16,16384]{1,0:T(8,128)(2,1)S(1)} %collective-permute-done.2.kv), channel_id=1, source_target_pairs={{0,1},{1,0},{2,3},{3,2},{4,5},{5,4},{6,7},{7,6},{8,9},{9,8},{10,11... | collective-permute-start | bytes 1572872 | tf_op jit(solution)/shard_map/ppermute | solution.py:410
  64.1 0.1 collective-permute-start.5
  64.3 1.3 collective-permute-done.5
  65.6 0.1 fusion.16
  65.7 0.1 reshape.121
  65.8 0.1 reshape.120
  65.9 0.1 pad_maximum_fusion
  66.0 0.8 copy-done.10
  66.8 11.0 %shard_map.103 = (bf16[64,256,256]{2,1,0:T(8,128)(2,1)}, bf16[64,32,256]{2,1,0:T(8,128)(2,1)}) custom-call(s32[1]{0:T(128)} %bitcast.core.refs_4_.r_0_, bf16[64,256,128]{2,1,0:T(8,128)(2,1)} %bitcast.33, bf16[64,256,128]{2,1,0:T(8,128)(2,1)} %bitcast.3.wo, bf16[16,16384]{1,0:T(8,128)(2,1)} %copy-done.9, bf16[16,16384]{1,0:T(8,128)(2,1)} %copy-done.10), custom_call_target="tpu_custom_call" | custom-call | flops 1000000000 | bytes 20000000 | tf_op jit(solution)/shard_map/pallas_call | solution.py:116
  77.9 0.1 collective-permute-start.6
  78.0 2.6 %collective-permute-start.7 = (bf16[1024,256]{1,0:T(8,128)(2,1)S(1)}, bf16[1024,256]{1,0:T(8,128)(2,1)S(1)}, u32[]{:S(2)}, u32[]{:S(2)}) collective-permute-start(bf16[1024,256]{1,0:T(8,128)(2,1)S(1)} %bitcast.29), channel_id=1, source_target_pairs={{0,112},{1,15},{2,114},{3,1},{4,116},{5,3},{6,118},{7,5},{8,120},{... | collective-permute-start | bytes 1572872 | tf_op jit(solution)/shard_map/ppermute | solution.py:407
  80.7 0.1 collective-permute-start.10
  80.9 2.6 %collective-permute-start.11 = (bf16[1040,256]{1,0:T(8,128)(2,1)S(1)}, bf16[1040,256]{1,0:T(8,128)(2,1)S(1)}, u32[]{:S(2)}, u32[]{:S(2)}) collective-permute-start(bf16[1040,256]{1,0:T(8,128)(2,1)S(1)} %shard_map.104.refs_2_), channel_id=1, source_target_pairs={{0,112},{1,15},{2,114},{3,1},{4,116},{5,3},{6,118},{7,5},{8,120},{... | collective-permute-start | bytes 1597448 | tf_op jit(solution)/shard_map/ppermute | solution.py:407
  83.5 0.1 pad_add_fusion.1
  83.6 3.4 %copy-done = bf16[64,256,256]{2,1,0:T(8,128)(2,1)S(1)} copy-done((bf16[64,256,256]{2,1,0:T(8,128)(2,1)S(1)}, bf16[64,256,256]{2,1,0:T(8,128)(2,1)}, u32[]{:S(2)}) %copy-start) | copy-done | bytes 8388632
  87.0 1.2 copy-done.3
  88.2 1.5 %shard_map.105 = (f32[256,256]{1,0:T(8,128)S(1)}, f32[32,256]{1,0:T(8,128)S(1)}, f32[8,256]{1,0:T(8,128)S(1)}) custom-call(s32[2]{0:T(128)S(1)} %get-tuple-element.201.refs_0_, bf16[1024,256]{1,0:T(8,128)(2,1)S(1)} %bitcast.30, bf16[1040,256]{1,0:T(8,128)(2,1)S(1)} %shard_map.104.refs_2_, ...), custom_call_target="tpu_custom_call", output_to_operand_aliasing={{0}: (5, {}), {1}: (6, {}), {2}: (7, {})} | custom-call | flops 301989888 | bytes 1000000 | tf_op jit(solution)/shard_map/pallas_call | solution.py:207
  89.8 0.1 pad_add_fusion.3.refs_0_
  89.9 0.1 collective-permute-start.8
  90.0 2.7 %collective-permute-start.9 = (bf16[1024,256]{1,0:T(8,128)(2,1)S(1)}, bf16[1024,256]{1,0:T(8,128)(2,1)S(1)}, u32[]{:S(2)}, u32[]{:S(2)}) collective-permute-start(bf16[1024,256]{1,0:T(8,128)(2,1)S(1)} %collective-permute-done.7.refs_2_), channel_id=1, source_target_pairs={{0,112},{1,15},{2,114},{3,1},{4,116},{5,3},{6,118},{7,5},{8,120},{... | collective-permute-start | bytes 1572872 | tf_op jit(solution)/shard_map/ppermute | solution.py:407
  92.6 1.5 %shard_map.106 = (f32[256,256]{1,0:T(8,128)S(1)}, f32[32,256]{1,0:T(8,128)S(1)}, f32[8,256]{1,0:T(8,128)S(1)}) custom-call(s32[2]{0:T(128)S(1)} %pad_add_fusion.3.refs_0_, bf16[1024,256]{1,0:T(8,128)(2,1)S(1)} %collective-permute-done.6.refs_1_, ...), custom_call_target="tpu_custom_call", output_to_operand_aliasing={{0}: (5, {}), {1}: (6, {}), {2}: (7, {})} | custom-call | flops 301989888 | bytes 1000000 | tf_op jit(solution)/shard_map/pallas_call | solution.py:207
  94.2 0.1 collective-permute-start.14
  94.3 2.6 %collective-permute-start.15 = (bf16[1040,256]{1,0:T(8,128)(2,1)S(1)}, bf16[1040,256]{1,0:T(8,128)(2,1)S(1)}, u32[]{:S(2)}, u32[]{:S(2)}) collective-permute-start(bf16[1040,256]{1,0:T(8,128)(2,1)S(1)} %collective-permute-done.11.refs_2_), channel_id=1, source_target_pairs={{0,112},{1,15},{2,114},{3,1},{4,116},{5,3},{6,118},{7,5},{8,120},{... | collective-permute-start | bytes 1597448 | tf_op jit(solution)/shard_map/ppermute | solution.py:407
  97.0 0.1 pad_add_fusion.5.refs_0_
  97.1 1.5 %shard_map.107 = (f32[256,256]{1,0:T(8,128)S(1)}, f32[32,256]{1,0:T(8,128)S(1)}, f32[8,256]{1,0:T(8,128)S(1)}) custom-call(s32[2]{0:T(128)S(1)} %get-tuple-element.202.refs_0_, bf16[1040,256]{1,0:T(8,128)(2,1)S(1)} %collective-permute-done.10.refs_1_, ...), custom_call_target="tpu_custom_call", output_to_operand_aliasing={{0}: (5, {}), {1}: (6, {}), {2}: (7, {})} | custom-call | flops 306708480 | bytes 1000000 | tf_op jit(solution)/shard_map/pallas_call | solution.py:207
  98.6 0.9 collective-permute-done.8.refs_1_
  99.5 2.7 %collective-permute-start.13 = (bf16[1024,256]{1,0:T(8,128)(2,1)S(1)}, bf16[1024,256]{1,0:T(8,128)(2,1)S(1)}, u32[]{:S(2)}, u32[]{:S(2)}) collective-permute-start(bf16[1024,256]{1,0:T(8,128)(2,1)S(1)} %collective-permute-done.9.refs_2_), channel_id=1, source_target_pairs={{0,112},{1,15},{2,114},{3,1},{4,116},{5,3},{6,118},{7,5},{8,120},{... | collective-permute-start | bytes 1572872 | tf_op jit(solution)/shard_map/ppermute | solution.py:407
  102.2 1.5 %shard_map.108 = (f32[256,256]{1,0:T(8,128)S(1)}, f32[32,256]{1,0:T(8,128)S(1)}, f32[8,256]{1,0:T(8,128)S(1)}) custom-call(s32[2]{0:T(128)S(1)} %pad_add_fusion.5.refs_0_, bf16[1024,256]{1,0:T(8,128)(2,1)S(1)} %collective-permute-done.8.refs_1_, ...), custom_call_target="tpu_custom_call", output_to_operand_aliasing={{0}: (5, {}), {1}: (6, {}), {2}: (7, {})} | custom-call | flops 301989888 | bytes 1000000 | tf_op jit(solution)/shard_map/pallas_call | solution.py:207
  103.7 1.5 collective-permute-done.14.refs_1_
  105.2 2.7 %collective-permute-start.18 = (bf16[1040,256]{1,0:T(8,128)(2,1)S(1)}, bf16[1040,256]{1,0:T(8,128)(2,1)S(1)}, u32[]{:S(2)}, u32[]{:S(2)}) collective-permute-start(bf16[1040,256]{1,0:T(8,128)(2,1)S(1)} %collective-permute-done.15.refs_2_), channel_id=1, source_target_pairs={{0,112},{1,15},{2,114},{3,1},{4,116},{5,3},{6,118},{7,5},{8,120},{... | collective-permute-start | bytes 1597448 | tf_op jit(solution)/shard_map/ppermute | solution.py:407
  107.9 0.1 pad_add_fusion.4.refs_0_
  107.9 0.1 pad_add_fusion.6.refs_0_
  108.0 1.5 %shard_map.109 = (f32[256,256]{1,0:T(8,128)S(1)}, f32[32,256]{1,0:T(8,128)S(1)}, f32[8,256]{1,0:T(8,128)S(1)}) custom-call(s32[2]{0:T(128)S(1)} %pad_add_fusion.4.refs_0_, bf16[1040,256]{1,0:T(8,128)(2,1)S(1)} %collective-permute-done.14.refs_1_, ...), custom_call_target="tpu_custom_call", output_to_operand_aliasing={{0}: (5, {}), {1}: (6, {}), {2}: (7, {})} | custom-call | flops 306708480 | bytes 1000000 | tf_op jit(solution)/shard_map/pallas_call | solution.py:207
  109.6 1.2 collective-permute-done.12.refs_1_
  110.8 1.5 %shard_map.110 = (f32[256,256]{1,0:T(8,128)S(1)}, f32[32,256]{1,0:T(8,128)S(1)}, f32[8,256]{1,0:T(8,128)S(1)}) custom-call(s32[2]{0:T(128)S(1)} %pad_add_fusion.6.refs_0_, bf16[1024,256]{1,0:T(8,128)(2,1)S(1)} %collective-permute-done.12.refs_1_, ...), custom_call_target="tpu_custom_call", output_to_operand_aliasing={{0}: (5, {}), {1}: (6, {}), {2}: (7, {})} | custom-call | flops 301989888 | bytes 1000000 | tf_op jit(solution)/shard_map/pallas_call | solution.py:207
  112.4 4.2 %collective-permute-done.17.refs_1_ = bf16[1040,256]{1,0:T(8,128)(2,1)S(1)} collective-permute-done((bf16[1040,256]{1,0:T(8,128)(2,1)S(1)}, bf16[1040,256]{1,0:T(8,128)(2,1)S(1)}, u32[]{:S(2)}, u32[]{:S(2)}) %collective-permute-start.17) | collective-permute-done | bytes 532512 | tf_op jit(solution)/shard_map/ppermute | solution.py:407
  116.5 2.4 %collective-permute-start.19 = (bf16[1040,256]{1,0:T(8,128)(2,1)S(1)}, bf16[1040,256]{1,0:T(8,128)(2,1)S(1)}, u32[]{:S(2)}, u32[]{:S(2)}) collective-permute-start(bf16[1040,256]{1,0:T(8,128)(2,1)S(1)} %collective-permute-done.18.refs_2_), channel_id=1, source_target_pairs={{0,112},{1,15},{2,114},{3,1},{4,116},{5,3},{6,118},{7,5},{8,120},{... | collective-permute-start | bytes 1597448 | tf_op jit(solution)/shard_map/ppermute | solution.py:407
  119.0 0.1 pad_add_fusion.7.refs_0_
  119.1 1.5 %shard_map.111 = (f32[256,256]{1,0:T(8,128)S(1)}, f32[32,256]{1,0:T(8,128)S(1)}, f32[8,256]{1,0:T(8,128)S(1)}) custom-call(s32[2]{0:T(128)S(1)} %pad_add_fusion.7.refs_0_, bf16[1040,256]{1,0:T(8,128)(2,1)S(1)} %collective-permute-done.17.refs_1_, ...), custom_call_target="tpu_custom_call", output_to_operand_aliasing={{0}: (5, {}), {1}: (6, {}), {2}: (7, {})} | custom-call | flops 306708480 | bytes 1000000 | tf_op jit(solution)/shard_map/pallas_call | solution.py:207
  120.6 7.8 %collective-permute-done.16.refs_1_ = bf16[1024,256]{1,0:T(8,128)(2,1)S(1)} collective-permute-done((bf16[1024,256]{1,0:T(8,128)(2,1)S(1)}, bf16[1024,256]{1,0:T(8,128)(2,1)S(1)}, u32[]{:S(2)}, u32[]{:S(2)}) %collective-permute-start.16) | collective-permute-done | bytes 524320 | tf_op jit(solution)/shard_map/ppermute | solution.py:407
  128.4 1.9 %shard_map.112 = (bf16[16,32,256]{2,1,0:T(8,128)(2,1)}, f32[8,256]{1,0:T(8,128)S(1)}) custom-call(s32[2]{0:T(128)S(1)} %pad_add_fusion.refs_0_, bf16[1024,256]{1,0:T(8,128)(2,1)S(1)} %collective-permute-done.16.refs_1_, bf16[1040,256]{1,0:T(8,128)(2,1)S(1)} %collective-permute-done.19.refs_2_, bf16[64,32,256]{2,1,0:T(8,128)(2,1)S(1)} %copy-done.4, ...), custom_call_target="tpu_custom_call" | custom-call | flops 1000000000 | bytes 1000000 | tf_op jit(solution)/shard_map/pallas_call | solution.py:207
  130.3 9.1 %all-to-all-start.1 = ((bf16[16,32,256]{2,1,0:T(8,128)(2,1)}), bf16[16,32,256]{2,1,0:T(8,128)(2,1)S(1)}, u32[]{:S(2)}, u32[]{:S(2)}) async-start(bf16[16,32,256]{2,1,0:T(8,128)(2,1)} %get-tuple-element.184), calls=%async_computation.1 | async-start | bytes 524288 | tf_op jit(solution)/shard_map/all_to_all | solution.py:541
  139.5 3.4 %copy-done.2 = bf16[64,256,256]{2,1,0:T(8,128)(2,1)S(1)} copy-done((bf16[64,256,256]{2,1,0:T(8,128)(2,1)S(1)}, bf16[64,256,256]{2,1,0:T(8,128)(2,1)}, u32[]{:S(2)}) %copy-start.2) | copy-done | bytes 8388632
  142.9 1.2 shard_map.113
  144.0 0.8 collective-permute-start.20
  144.8 1.0 collective-permute-done.20.r_2_
  145.8 1.0 shard_map.114
  146.8 4.7 %all-to-all-done.1.kvr = bf16[16,32,256]{2,1,0:T(8,128)(2,1)S(1)} async-done(((bf16[16,32,256]{2,1,0:T(8,128)(2,1)}), bf16[16,32,256]{2,1,0:T(8,128)(2,1)S(1)}, u32[]{:S(2)}, u32[]{:S(2)}) %all-to-all-start.1) | async-done | bytes 262176 | tf_op jit(solution)/shard_map/all_to_all | solution.py:541
  151.4 1.4 shard_map.115
  (47 shorter events, 0.4 us)
Async XLA Ops:
  0.6 65.3 %collective-permute-start.1 = (bf16[16384,128]{1,0:T(8,128)(2,1)}, bf16[16384,128]{1,0:T(8,128)(2,1)}, u32[]{:S(2)}, u32[]{:S(2)}) collective-permute-start(bf16[16384,128]{1,0:T(8,128)(2,1)} %param.9), channel_id=1, source_target_pairs={{0,1},{1,0},{2,3},{3,2},{4,5},{5,4},{6,7},{7,6},{8,9},{9,8},{10,11... | collective-permute-start | bytes 12582920 | tf_op jit(solution)/shard_map/ppermute | solution.py:410
  21.2 0.9 copy-start.5
  22.1 0.7 copy-start.7
  22.9 5.3 %collective-permute-start = (bf16[272,128]{1,0:T(8,128)(2,1)S(1)}, bf16[272,128]{1,0:T(8,128)(2,1)S(1)}, u32[]{:S(2)}, u32[]{:S(2)}) collective-permute-start(bf16[272,128]{1,0:T(8,128)(2,1)S(1)} %get-tuple-element.98), channel_id=1, source_target_pairs={{0,1},{1,0},{2,3},{3,2},{4,5},{5,4},{6,7},{7,6},{8,9},{9,8},{10,11... | collective-permute-start | bytes 208904 | tf_op jit(solution)/shard_map/ppermute | solution.py:410
  29.4 48.3 %all-to-all-start = ((bf16[8,272,256]{2,1,0:T(8,128)(2,1)}), bf16[8,272,256]{2,1,0:T(8,128)(2,1)S(1)}, u32[]{:S(2)}, u32[]{:S(2)}) async-start(bf16[8,272,256]{2,1,0:T(8,128)(2,1)} %shard_map.102), calls=%async_computation | async-start | bytes 2228224 | tf_op jit(solution)/shard_map/all_to_all | solution.py:444
  33.2 29.2 %collective-permute-start.2 = (bf16[16,16384]{1,0:T(8,128)(2,1)}, bf16[16,16384]{1,0:T(8,128)(2,1)S(1)}, u32[]{:S(2)}, u32[]{:S(2)}) collective-permute-start(bf16[16,16384]{1,0:T(8,128)(2,1)} %param.10), channel_id=1, source_target_pairs={{0,14},{1,30},{2,34},{3,50},{4,70},{5,86},{6,106},{7,122},{8,6},{9... | collective-permute-start | bytes 1572872 | tf_op jit(solution)/shard_map/ppermute | solution.py:430
  34.0 30.1 %collective-permute-start.4 = (f32[1,16]{1,0:T(1,128)S(1)}, f32[1,16]{1,0:T(1,128)S(1)}, u32[]{:S(2)}, u32[]{:S(2)}) collective-permute-start(f32[1,16]{1,0:T(1,128)S(1)} %slice_bitcast_fusion.1), channel_id=1, source_target_pairs={{0,14},{1,30},{2,34},{3,50},{4,70},{5,86},{6,106},{7,122},{8,6},{9... | collective-permute-start | bytes 200 | tf_op jit(solution)/shard_map/ppermute | solution.py:432
  62.4 3.5 %copy-start.9 = (bf16[16,16384]{1,0:T(8,128)(2,1)}, bf16[16,16384]{1,0:T(8,128)(2,1)S(1)}, u32[]{:S(2)}) copy-start(bf16[16,16384]{1,0:T(8,128)(2,1)S(1)} %collective-permute-done.2.kv) | copy-start | bytes 1572868
  62.4 3.5 %collective-permute-start.3 = (bf16[16,16384]{1,0:T(8,128)(2,1)S(1)}, bf16[16,16384]{1,0:T(8,128)(2,1)S(1)}, u32[]{:S(2)}, u32[]{:S(2)}) collective-permute-start(bf16[16,16384]{1,0:T(8,128)(2,1)S(1)} %collective-permute-done.2.kv), channel_id=1, source_target_pairs={{0,1},{1,0},{2,3},{3,2},{4,5},{5,4},{6,7},{7,6},{8,9},{9,8},{10,11... | collective-permute-start | bytes 1572872 | tf_op jit(solution)/shard_map/ppermute | solution.py:410
  64.1 1.5 collective-permute-start.5
  65.9 0.8 copy-start.10
  77.9 12.0 %collective-permute-start.6 = (bf16[1024,256]{1,0:T(8,128)(2,1)S(1)}, bf16[1024,256]{1,0:T(8,128)(2,1)S(1)}, u32[]{:S(2)}, u32[]{:S(2)}) collective-permute-start(bf16[1024,256]{1,0:T(8,128)(2,1)S(1)} %bitcast.28), channel_id=1, source_target_pairs={{0,16},{1,3},{2,18},{3,5},{4,20},{5,7},{6,22},{7,9},{8,24},{9,11},... | collective-permute-start | bytes 1572872 | tf_op jit(solution)/shard_map/ppermute | solution.py:407
  78.0 11.9 %collective-permute-start.7 = (bf16[1024,256]{1,0:T(8,128)(2,1)S(1)}, bf16[1024,256]{1,0:T(8,128)(2,1)S(1)}, u32[]{:S(2)}, u32[]{:S(2)}) collective-permute-start(bf16[1024,256]{1,0:T(8,128)(2,1)S(1)} %bitcast.29), channel_id=1, source_target_pairs={{0,112},{1,15},{2,114},{3,1},{4,116},{5,3},{6,118},{7,5},{8,120},{... | collective-permute-start | bytes 1572872 | tf_op jit(solution)/shard_map/ppermute | solution.py:407
  80.7 13.5 %collective-permute-start.10 = (bf16[1040,256]{1,0:T(8,128)(2,1)S(1)}, bf16[1040,256]{1,0:T(8,128)(2,1)S(1)}, u32[]{:S(2)}, u32[]{:S(2)}) collective-permute-start(bf16[1040,256]{1,0:T(8,128)(2,1)S(1)} %shard_map.104.refs_2_), channel_id=1, source_target_pairs={{0,16},{1,3},{2,18},{3,5},{4,20},{5,7},{6,22},{7,9},{8,24},{9,11},... | collective-permute-start | bytes 1597448 | tf_op jit(solution)/shard_map/ppermute | solution.py:407
  80.9 13.3 %collective-permute-start.11 = (bf16[1040,256]{1,0:T(8,128)(2,1)S(1)}, bf16[1040,256]{1,0:T(8,128)(2,1)S(1)}, u32[]{:S(2)}, u32[]{:S(2)}) collective-permute-start(bf16[1040,256]{1,0:T(8,128)(2,1)S(1)} %shard_map.104.refs_2_), channel_id=1, source_target_pairs={{0,112},{1,15},{2,114},{3,1},{4,116},{5,3},{6,118},{7,5},{8,120},{... | collective-permute-start | bytes 1597448 | tf_op jit(solution)/shard_map/ppermute | solution.py:407
  83.6 3.4 %copy-start = (bf16[64,256,256]{2,1,0:T(8,128)(2,1)S(1)}, bf16[64,256,256]{2,1,0:T(8,128)(2,1)}, u32[]{:S(2)}) copy-start(bf16[64,256,256]{2,1,0:T(8,128)(2,1)} %get-tuple-element.106.refs_3_) | copy-start | bytes 25165828
  87.0 1.2 copy-start.3
  88.2 4.4 %copy-start.1 = (bf16[64,256,256]{2,1,0:T(8,128)(2,1)S(1)}, bf16[64,256,256]{2,1,0:T(8,128)(2,1)}, u32[]{:S(2)}) copy-start(bf16[64,256,256]{2,1,0:T(8,128)(2,1)} %get-tuple-element.106.refs_3_) | copy-start | bytes 25165828
  88.2 4.4 %copy-start.4 = (bf16[64,32,256]{2,1,0:T(8,128)(2,1)S(1)}, bf16[64,32,256]{2,1,0:T(8,128)(2,1)}, u32[]{:S(2)}) copy-start(bf16[64,32,256]{2,1,0:T(8,128)(2,1)} %get-tuple-element.107.refs_4_.refs_3_) | copy-start | bytes 3145732
  89.9 9.6 %collective-permute-start.8 = (bf16[1024,256]{1,0:T(8,128)(2,1)S(1)}, bf16[1024,256]{1,0:T(8,128)(2,1)S(1)}, u32[]{:S(2)}, u32[]{:S(2)}) collective-permute-start(bf16[1024,256]{1,0:T(8,128)(2,1)S(1)} %collective-permute-done.6.refs_1_), channel_id=1, source_target_pairs={{0,16},{1,3},{2,18},{3,5},{4,20},{5,7},{6,22},{7,9},{8,24},{9,11},... | collective-permute-start | bytes 1572872 | tf_op jit(solution)/shard_map/ppermute | solution.py:407
  90.0 9.5 %collective-permute-start.9 = (bf16[1024,256]{1,0:T(8,128)(2,1)S(1)}, bf16[1024,256]{1,0:T(8,128)(2,1)S(1)}, u32[]{:S(2)}, u32[]{:S(2)}) collective-permute-start(bf16[1024,256]{1,0:T(8,128)(2,1)S(1)} %collective-permute-done.7.refs_2_), channel_id=1, source_target_pairs={{0,112},{1,15},{2,114},{3,1},{4,116},{5,3},{6,118},{7,5},{8,120},{... | collective-permute-start | bytes 1572872 | tf_op jit(solution)/shard_map/ppermute | solution.py:407
  94.2 11.0 %collective-permute-start.14 = (bf16[1040,256]{1,0:T(8,128)(2,1)S(1)}, bf16[1040,256]{1,0:T(8,128)(2,1)S(1)}, u32[]{:S(2)}, u32[]{:S(2)}) collective-permute-start(bf16[1040,256]{1,0:T(8,128)(2,1)S(1)} %collective-permute-done.10.refs_1_), channel_id=1, source_target_pairs={{0,16},{1,3},{2,18},{3,5},{4,20},{5,7},{6,22},{7,9},{8,24},{9,11},... | collective-permute-start | bytes 1597448 | tf_op jit(solution)/shard_map/ppermute | solution.py:407
  94.3 10.9 %collective-permute-start.15 = (bf16[1040,256]{1,0:T(8,128)(2,1)S(1)}, bf16[1040,256]{1,0:T(8,128)(2,1)S(1)}, u32[]{:S(2)}, u32[]{:S(2)}) collective-permute-start(bf16[1040,256]{1,0:T(8,128)(2,1)S(1)} %collective-permute-done.11.refs_2_), channel_id=1, source_target_pairs={{0,112},{1,15},{2,114},{3,1},{4,116},{5,3},{6,118},{7,5},{8,120},{... | collective-permute-start | bytes 1597448 | tf_op jit(solution)/shard_map/ppermute | solution.py:407
  99.5 11.3 %collective-permute-start.12 = (bf16[1024,256]{1,0:T(8,128)(2,1)S(1)}, bf16[1024,256]{1,0:T(8,128)(2,1)S(1)}, u32[]{:S(2)}, u32[]{:S(2)}) collective-permute-start(bf16[1024,256]{1,0:T(8,128)(2,1)S(1)} %collective-permute-done.8.refs_1_), channel_id=1, source_target_pairs={{0,16},{1,3},{2,18},{3,5},{4,20},{5,7},{6,22},{7,9},{8,24},{9,11},... | collective-permute-start | bytes 1572872 | tf_op jit(solution)/shard_map/ppermute | solution.py:407
  99.5 11.3 %collective-permute-start.13 = (bf16[1024,256]{1,0:T(8,128)(2,1)S(1)}, bf16[1024,256]{1,0:T(8,128)(2,1)S(1)}, u32[]{:S(2)}, u32[]{:S(2)}) collective-permute-start(bf16[1024,256]{1,0:T(8,128)(2,1)S(1)} %collective-permute-done.9.refs_2_), channel_id=1, source_target_pairs={{0,112},{1,15},{2,114},{3,1},{4,116},{5,3},{6,118},{7,5},{8,120},{... | collective-permute-start | bytes 1572872 | tf_op jit(solution)/shard_map/ppermute | solution.py:407
  105.2 11.3 %collective-permute-start.17 = (bf16[1040,256]{1,0:T(8,128)(2,1)S(1)}, bf16[1040,256]{1,0:T(8,128)(2,1)S(1)}, u32[]{:S(2)}, u32[]{:S(2)}) collective-permute-start(bf16[1040,256]{1,0:T(8,128)(2,1)S(1)} %collective-permute-done.14.refs_1_), channel_id=1, source_target_pairs={{0,16},{1,3},{2,18},{3,5},{4,20},{5,7},{6,22},{7,9},{8,24},{9,11},... | collective-permute-start | bytes 1597448 | tf_op jit(solution)/shard_map/ppermute | solution.py:407
  105.2 11.3 %collective-permute-start.18 = (bf16[1040,256]{1,0:T(8,128)(2,1)S(1)}, bf16[1040,256]{1,0:T(8,128)(2,1)S(1)}, u32[]{:S(2)}, u32[]{:S(2)}) collective-permute-start(bf16[1040,256]{1,0:T(8,128)(2,1)S(1)} %collective-permute-done.15.refs_2_), channel_id=1, source_target_pairs={{0,112},{1,15},{2,114},{3,1},{4,116},{5,3},{6,118},{7,5},{8,120},{... | collective-permute-start | bytes 1597448 | tf_op jit(solution)/shard_map/ppermute | solution.py:407
  116.5 11.9 %collective-permute-start.19 = (bf16[1040,256]{1,0:T(8,128)(2,1)S(1)}, bf16[1040,256]{1,0:T(8,128)(2,1)S(1)}, u32[]{:S(2)}, u32[]{:S(2)}) collective-permute-start(bf16[1040,256]{1,0:T(8,128)(2,1)S(1)} %collective-permute-done.18.refs_2_), channel_id=1, source_target_pairs={{0,112},{1,15},{2,114},{3,1},{4,116},{5,3},{6,118},{7,5},{8,120},{... | collective-permute-start | bytes 1597448 | tf_op jit(solution)/shard_map/ppermute | solution.py:407
  118.9 9.5 %collective-permute-start.16 = (bf16[1024,256]{1,0:T(8,128)(2,1)S(1)}, bf16[1024,256]{1,0:T(8,128)(2,1)S(1)}, u32[]{:S(2)}, u32[]{:S(2)}) collective-permute-start(bf16[1024,256]{1,0:T(8,128)(2,1)S(1)} %collective-permute-done.12.refs_1_), channel_id=1, source_target_pairs={{0,16},{1,3},{2,18},{3,5},{4,20},{5,7},{6,22},{7,9},{8,24},{9,11},... | collective-permute-start | bytes 1572872 | tf_op jit(solution)/shard_map/ppermute | solution.py:407
  120.6 18.9 %copy-start.11 = (f32[144]{0:T(256)S(1)}, f32[144]{0:T(256)}, u32[]{:S(2)}) copy-start(f32[144]{0:T(256)} %param.11) | copy-start | bytes 1732
  130.3 21.1 %all-to-all-start.1 = ((bf16[16,32,256]{2,1,0:T(8,128)(2,1)}), bf16[16,32,256]{2,1,0:T(8,128)(2,1)S(1)}, u32[]{:S(2)}, u32[]{:S(2)}) async-start(bf16[16,32,256]{2,1,0:T(8,128)(2,1)} %get-tuple-element.184), calls=%async_computation.1 | async-start | bytes 524288 | tf_op jit(solution)/shard_map/all_to_all | solution.py:541
  139.5 3.4 %copy-start.2 = (bf16[64,256,256]{2,1,0:T(8,128)(2,1)S(1)}, bf16[64,256,256]{2,1,0:T(8,128)(2,1)}, u32[]{:S(2)}) copy-start(bf16[64,256,256]{2,1,0:T(8,128)(2,1)} %get-tuple-element.106.refs_3_) | copy-start | bytes 25165828
  142.9 2.9 %copy-start.6 = (bf16[512,128]{1,0:T(8,128)(2,1)S(1)}, bf16[512,128]{1,0:T(8,128)(2,1)}, u32[]{:S(2)}) copy-start(bf16[512,128]{1,0:T(8,128)(2,1)} %r_4_.1) | copy-start | bytes 393220
  142.9 2.9 %copy-start.8 = (f32[128]{0:T(128)S(1)}, f32[128]{0:T(128)}, u32[]{:S(2)}) copy-start(f32[128]{0:T(128)} %param.7) | copy-start | bytes 1540
  144.0 1.8 %collective-permute-start.20 = (f32[264,128]{1,0:T(8,128)S(1)}, f32[264,128]{1,0:T(8,128)S(1)}, u32[]{:S(2)}, u32[]{:S(2)}) collective-permute-start(f32[264,128]{1,0:T(8,128)S(1)} %get-tuple-element.179), channel_id=1, source_target_pairs={{0,1},{1,0},{2,3},{3,2},{4,5},{5,4},{6,7},{7,6},{8,9},{9,8},{10,11... | collective-permute-start | bytes 405512 | tf_op jit(solution)/shard_map/ppermute | solution.py:410

commit v2 on v1

--- a/solution.py
+++ b/solution.py
@@ -15,6 +15,7 @@
 rope_base = 500000.0
 
 VMEM = 24 * 2**20
+RING_VMEM = 48 * 2**20
 
 F32 = jnp.float32
 BF16 = jnp.bfloat16
@@ -65,28 +66,23 @@
         out[s, half:, :] = stats
 
 
-def weights_kernel(core, wq, wo, kv, ko, w_all, kv_all, w_buf, kv_buf, sems):
+def block_at(core, i, side):
+    return jnp.where(core == 0, i, (i % side) * side + i // side)
+
+
+def weights_kernel(core, wq, wo, w_all, w_buf, sems):
     n = w_buf.shape[0]
-    kb = w_buf.shape[1]
-    hw = wq.shape[2]
-    rows = kv.shape[0]
     side = math.isqrt(n)
 
     def fetches(i):
-        b = jnp.where(core[0] == 0, i, (i % side) * side + i // side)
-        at = pl.ds(pl.multiple_of(b * kb, kb), kb)
+        b = block_at(core[0], i, side)
         return (
-            pltpu.make_async_copy(wq.at[b], w_buf.at[i, :, pl.ds(0, hw)], sems.at[0, i]),
-            pltpu.make_async_copy(wo.at[b], w_buf.at[i, :, pl.ds(hw, hw)], sems.at[1, i]),
-            pltpu.make_async_copy(kv.at[:, at], kv_buf.at[i, pl.ds(0, rows), :], sems.at[2, i]),
-            pltpu.make_async_copy(ko.at[:, at], kv_buf.at[i, pl.ds(rows, rows), :], sems.at[3, i]),
-        )
-
-    def stores(i):
-        return (
-            pltpu.make_async_copy(w_buf.at[i], w_all.at[i], sems.at[4, i]),
-            pltpu.make_async_copy(kv_buf.at[i], kv_all.at[i], sems.at[5, i]),
-        )
+            pltpu.make_async_copy(wq.at[b], w_buf.at[i, 0], sems.at[0, i]),
+            pltpu.make_async_copy(wo.at[b], w_buf.at[i, 1], sems.at[1, i]),
+        )
+
+    def store(i):
+        return pltpu.make_async_copy(w_buf.at[i], w_all.at[i], sems.at[2, i])
 
     @pl.loop(0, n)
     def _(i):
@@ -97,32 +93,50 @@
     def _(i):
         for c in fetches(i):
             c.wait()
-        for c in stores(i):
-            c.start()
+        store(i).start()
 
     @pl.loop(0, n)
     def _(i):
-        for c in stores(i):
-            c.wait()
-
-
-def arrange_weights(core, wq, wo, kv, ko):
+        store(i).wait()
+
+
+def arrange_weights(core, wq, wo):
     n, kb, hw = wq.shape
     hbm = pl.BlockSpec(memory_space=pltpu.HBM)
-    out_shape = (
-        jax.ShapeDtypeStruct((n, kb, 2 * hw), BF16),
-        jax.ShapeDtypeStruct((n, 2 * kv.shape[0], kb), BF16),
-    )
+    out = jax.ShapeDtypeStruct((n, 2, kb, hw), BF16)
     return pl.pallas_call(
         weights_kernel,
-        out_shape=out_shape,
-        in_specs=[pl.BlockSpec(memory_space=pltpu.SMEM), hbm, hbm, hbm, hbm],
-        out_specs=(hbm, hbm),
-        scratch_shapes=[pltpu.VMEM(o.shape, o.dtype) for o in out_shape]
-        + [pltpu.SemaphoreType.DMA((6, n))],
+        out_shape=out,
+        in_specs=[pl.BlockSpec(memory_space=pltpu.SMEM), hbm, hbm],
+        out_specs=hbm,
+        scratch_shapes=[pltpu.VMEM(out.shape, out.dtype), pltpu.SemaphoreType.DMA((3, n))],
         compiler_params=pltpu.CompilerParams(vmem_limit_bytes=60 * 2**20),
         cost_estimate=pl.CostEstimate(flops=10**9, bytes_accessed=2 * 10**7, transcendentals=0),
-    )(core, wq, wo, kv, ko)
+    )(core, wq, wo)
+
+
+def kv_weights_kernel(core, kv, ko, kv_all, kvscale):
+    n, rows2, kb = kv_all.shape
+    rows = rows2 // 2
+    side = math.isqrt(n)
+    for i in range(n):
+        at = pl.ds(pl.multiple_of(block_at(core[0], i, side) * kb, kb), kb)
+        kv_all[i, :rows, :] = kv[:, at]
+        kv_all[i, rows:, :] = ko[:, at]
+    width = kvscale.shape[1]
+
+    def scales(ref):
+        s = ref[:, n * kb : n * kb + 128].astype(F32)
+        s = (s[:, 0:1] + s[:, 1:2]) + s[:, 2:3]
+        return jnp.broadcast_to(s, (rows, width))
+
+    m, o = scales(kv), scales(ko)
+    first = core[0] == 0
+    k = rows // 2
+    for j, (lo, hi) in enumerate(((0, k), (k, 2 * k))):
+        a, b = m[lo:hi], o[lo:hi]
+        kvscale[2 * j * k : (2 * j + 1) * k, :] = jnp.where(first, a, b)
+        kvscale[(2 * j + 1) * k : (2 * j + 2) * k, :] = jnp.where(first, b, a)
 
 
 def high_kernel(gathered, high):
@@ -166,7 +180,9 @@
     for x, w in zip(xs, ws):
         for i in range(w.shape[0]):
             total = total + jnp.dot(
-                x[i * half : (i + 1) * half, :], w[i], preferred_element_type=F32
+                x[i * half : (i + 1) * half, :],
+                jnp.concatenate([w[i, 0], w[i, 1]], axis=1),
+                preferred_element_type=F32,
             )
     return total
 
@@ -212,7 +228,7 @@
         scratch_shapes=[pltpu.VMEM((m, n) + w.shape[1:], w.dtype) for w in weights]
         + [pltpu.SemaphoreType.DMA((len(weights), m))],
         input_output_aliases=aliases or {},
-        compiler_params=pltpu.CompilerParams(vmem_limit_bytes=VMEM),
+        compiler_params=pltpu.CompilerParams(vmem_limit_bytes=RING_VMEM),
         cost_estimate=pl.CostEstimate(flops=flops, bytes_accessed=10**6, transcendentals=0),
     )(table, *xs, *weights, *rest)
 
@@ -427,13 +443,16 @@
             o = (xs - source + 1) % side
             return 2 * ((o - source) % columns + columns * slot) + h
 
-        kv_mine = lax.ppermute(w_kv, "tp", to_row)
-        wq_other = swap(w_query)
-        kvs_mine = lax.ppermute(w_scale[None, HD:], "tp", to_row)
-
         blk = jax.ShapeDtypeStruct((half + STAT, width), BF16)
         keep, send = call(prep_kernel, (blk, blk), core1, hidden, gain)
         recv = swap(send)
+        kvs = w_scale[HD:]
+        hi = kvs.astype(BF16)
+        mid = kvs - hi.astype(F32)
+        mid, lo = mid.astype(BF16), (mid - mid.astype(BF16).astype(F32)).astype(BF16)
+        scales = jnp.pad(jnp.stack([hi, mid, lo], axis=1), ((0, 0), (0, 125)))
+        kv_mine = lax.ppermute(jnp.concatenate([w_kv, scales], axis=1), "tp", to_row)
+        wq_other = swap(w_query)
         slots = call(
             combine_kernel,
             jax.ShapeDtypeStruct((side, half + STAT, 2 * width), BF16),
@@ -444,10 +463,8 @@
         gathered = lax.all_to_all(
             slots, "tp", split_axis=0, concat_axis=0, tiled=False, axis_index_groups=first_groups
         )
-        kv_other = swap(kv_mine)
-        kvs_other = swap(kvs_mine)
-        w_all, kv_all = arrange_weights(
-            core1, w_query.reshape(-1, 2 * width, HD), wq_other.reshape(-1, 2 * width, HD), kv_mine, kv_other
+        w_all = arrange_weights(
+            core1, w_query.reshape(-1, 2 * width, HD), wq_other.reshape(-1, 2 * width, HD)
         )
 
         positions = (prefix[0] + jnp.arange(count, dtype=jnp.int32)).astype(F32)
@@ -466,17 +483,6 @@
         seats = jnp.arange(row, dtype=jnp.int32)
         order = piece_at(seats // 2, seats % 2).astype(jnp.int32)
         ang_k = fk[:, None] * pos_own[None, :]
-        ordered = jnp.where(
-            core == 0,
-            jnp.concatenate([kvs_mine, kvs_other], 0),
-            jnp.concatenate([kvs_other, kvs_mine], 0),
-        )
-        kvscale = jnp.broadcast_to(
-            jnp.concatenate(
-                [ordered[:, :KV_COLS_DEV].reshape(-1), ordered[:, KV_COLS_DEV:].reshape(-1)]
-            )[:, None],
-            (4 * KV_COLS_DEV, half),
-        )
         qscale = w_scale[None, :HD]
         tables = (
             jnp.cos(ang_own),
@@ -485,7 +491,6 @@
             jnp.sin(ang_far),
             jnp.cos(ang_k),
             jnp.sin(ang_k),
-            kvscale,
         )
         zeros = (
             jnp.zeros((half, 2 * HD), F32),
@@ -499,10 +504,10 @@
 
         shifts = [(s, k) for s in range(side) for k in range(2)]
         places = {sk: table_of([(*sk, None)]) for sk in shifts}
-        gathered, w_all, kv_all, tables, zeros, places, order = lax.optimization_barrier(
-            (gathered, w_all, kv_all, tables, zeros, places, order)
-        )
-        cos_own, sin_own, cos_far, sin_far, cos_k, sin_k, kvscale = tables
+        gathered, w_all, tables, zeros, places, order = lax.optimization_barrier(
+            (gathered, w_all, tables, zeros, places, order)
+        )
+        cos_own, sin_own, cos_far, sin_far, cos_k, sin_k = tables
 
         n = side // 2
         low = gathered[:n, :half].reshape(n * half, -1)
@@ -519,6 +524,17 @@
 
         up = [second(low, 1), second(high, 1)]
         down = [second(low, -1), second(high, -1)]
+        kv_other = swap(kv_mine)
+        kv_all, kvscale = call(
+            kv_weights_kernel,
+            (
+                jax.ShapeDtypeStruct((d // (2 * width), 4 * KV_COLS_DEV, 2 * width), BF16),
+                jax.ShapeDtypeStruct((4 * KV_COLS_DEV, half), F32),
+            ),
+            core1,
+            kv_mine,
+            kv_other,
+        )
         acc = mm(zeros, [(0, 0, low), (0, 1, high)])
         last_round = side // 2
         for r in range(1, last_round):

time: 153 us -> 149 us (0.974)
  local copies, waits for them, and re-layouts: 11.5 us -> 2.5 us
  Pallas kernels: 28.6 us -> 34 us
  waiting for transfers between devices: 53.3 us -> 51.1 us
    unnamed x24 -> x12, local copies, waits for them, and re-layouts: 10.4 us -> 1.58 us
    pallas_call x9, Pallas kernels: 13.8 us -> 21.8 us  [arrivals_call(): pl.pallas_call(kernel, out_shape=out_shape, in_specs=specs, out_specs=tup...]
    ppermute x14, waiting for transfers between devices: 15.6 us -> 12.5 us  [second(): return lax.ppermute(v, 'tp', pairs)]
    ppermute x5 -> x4, waiting for transfers between devices: 7.51 us -> 4.69 us  [swap(): return lax.ppermute(v, 'tp', to_partner)]
    pallas_call x1, Pallas kernels: 11 us -> 8.29 us  [arrange_weights(): pl.pallas_call(weights_kernel, out_shape=out, in_specs=[pl.BlockSpec(memo...]
    all_to_all x1, waiting for transfers between devices: 4.68 us -> 6.9 us  [body(): lax.all_to_all(kvt, 'tp', split_axis=0, concat_axis=0, tiled=False, axis_...]
    ppermute x2 -> x1, waiting for transfers between devices: 25.5 us -> 26.9 us  [body(): lax.ppermute(jnp.concatenate([w_kv, scales], axis=1), 'tp', to_row)]
    pallas_call x4 -> x5, Pallas kernels: 3.71 us -> 3.9 us  [call(): pl.pallas_call(kernel, out_shape=out_shape, in_specs=[pl.BlockSpec(memory...]
  transfers between devices with their start and end apart: 23 -> 21, of which waited for: 10 -> 11; matrix products, arithmetic and copies ran while one was open for 2% -> 2% of each run, Pallas kernels for 17% -> 21%
where the time goes in v2:
time: 149 us; the launch traced here: 148 us
  starting transfers between devices  56.2 us (38%)
  waiting for transfers between devices  51.1 us (34%)
  Pallas kernels  34 us (23%)
  local copies, waits for them, and re-layouts  2.5 us (2%)
  other arithmetic  2.48 us (2%)
  between operations  1.82 us (1%)
    ppermute x1, waiting for transfers between devices, body(): lax.ppermute(jnp.concatenate([w_kv, scales], axis=1), 'tp', to_row)  26.9 us
    ppermute x4, starting transfers between devices, swap(): return lax.ppermute(v, 'tp', to_partner)  23.2 us
    pallas_call x9, Pallas kernels, arrivals_call(): pl.pallas_call(kernel, out_shape=out_shape, in_specs=specs, out_specs=tup...  21.8 us
    ppermute x14, starting transfers between devices, second(): return lax.ppermute(v, 'tp', pairs)  18.7 us
    ppermute x14, waiting for transfers between devices, second(): return lax.ppermute(v, 'tp', pairs)  12.5 us
    all_to_all x1, starting transfers between devices, body(): lax.all_to_all(kvt, 'tp', split_axis=0, concat_axis=0, tiled=False, axis_...  10.4 us
    pallas_call x1, Pallas kernels, arrange_weights(): pl.pallas_call(weights_kernel, out_shape=out, in_specs=[pl.BlockSpec(memo...  8.29 us
    all_to_all x1, waiting for transfers between devices, body(): lax.all_to_all(kvt, 'tp', split_axis=0, concat_axis=0, tiled=False, axis_...  6.9 us
  transfers between devices with their start and end apart: 21, of which 11 were waited for; matrix products, arithmetic and copies ran while one was open for 2% of the time, Pallas kernels for 21%

profile of v2, /device:TPU:513, one launch (start us, length us, event | category | flops | bytes accessed | tf_op | source)
XLA Modules:
  0.0 148.1 jit_solution(9487006341689635320)
XLA Ops:
  0.6 20.5 %collective-permute-start.1 = (bf16[16384,128]{1,0:T(8,128)(2,1)}, bf16[16384,128]{1,0:T(8,128)(2,1)}, u32[]{:S(2)}, u32[]{:S(2)}) collective-permute-start(bf16[16384,128]{1,0:T(8,128)(2,1)} %param.9), channel_id=1, source_target_pairs={{0,1},{1,0},{2,3},{3,2},{4,5},{5,4},{6,7},{7,6},{8,9},{9,8},{10,11... | collective-permute-start | bytes 12582920 | tf_op jit(solution)/shard_map/ppermute | solution.py:426
  21.2 0.9 copy-done
  22.1 0.7 copy-done.2
  22.7 0.2 shard_map.101
  22.9 0.2 collective-permute-start
  23.1 0.7 convert_bitcast_fusion.2
  23.8 0.7 convert_bitcast_fusion.1
  24.5 0.1 copy.35
  24.6 3.7 %collective-permute-done.recv = bf16[272,128]{1,0:T(8,128)(2,1)S(1)} collective-permute-done((bf16[272,128]{1,0:T(8,128)(2,1)S(1)}, bf16[272,128]{1,0:T(8,128)(2,1)S(1)}, u32[]{:S(2)}, u32[]{:S(2)}) %collective-permute-start) | collective-permute-done | bytes 69664 | tf_op jit(solution)/shard_map/ppermute | solution.py:426
  28.3 1.1 shard_map.102
  29.4 3.9 %all-to-all-start = ((bf16[8,272,256]{2,1,0:T(8,128)(2,1)}), bf16[8,272,256]{2,1,0:T(8,128)(2,1)S(1)}, u32[]{:S(2)}, u32[]{:S(2)}) async-start(bf16[8,272,256]{2,1,0:T(8,128)(2,1)} %shard_map.102), calls=%async_computation | async-start | bytes 2228224 | tf_op jit(solution)/shard_map/all_to_all | solution.py:463
  33.4 0.1 collective-permute-start.4
  34.6 0.1 fusion.17
  34.7 1.0 multiply_sine_fusion
  35.6 26.9 %collective-permute-done.4.kv = bf16[16,16512]{1,0:T(8,128)(2,1)S(1)} collective-permute-done((bf16[16,16512]{1,0:T(8,128)(2,1)S(1)}, bf16[16,16512]{1,0:T(8,128)(2,1)S(1)}, u32[]{:S(2)}, u32[]{:S(2)}) %collective-permute-start.4) | collective-permute-done | bytes 528416 | tf_op jit(solution)/shard_map/ppermute | solution.py:454
  62.6 1.7 %collective-permute-start.5 = (bf16[16,16512]{1,0:T(8,128)(2,1)S(1)}, bf16[16,16512]{1,0:T(8,128)(2,1)S(1)}, u32[]{:S(2)}, u32[]{:S(2)}) collective-permute-start(bf16[16,16512]{1,0:T(8,128)(2,1)S(1)} %collective-permute-done.4.kv), channel_id=1, source_target_pairs={{0,1},{1,0},{2,3},{3,2},{4,5},{5,4},{6,7},{7,6},{8,9},{9,8},{10,11... | collective-permute-start | bytes 1585160 | tf_op jit(solution)/shard_map/ppermute | solution.py:426
  64.3 0.1 multiply_sine_fusion.2
  64.5 0.0 collective-permute-done.1
  64.5 8.3 %shard_map.103.refs_3_ = bf16[64,2,256,128]{3,2,1,0:T(8,128)(2,1)} custom-call(s32[1]{0:T(128)} %bitcast.core.refs_4_.r_0_, bf16[64,256,128]{2,1,0:T(8,128)(2,1)} %bitcast.37, bf16[64,256,128]{2,1,0:T(8,128)(2,1)} %bitcast.3.wo), custom_call_target="tpu_custom_call" | custom-call | flops 1000000000 | bytes 20000000 | tf_op jit(solution)/shard_map/pallas_call | solution.py:107
  72.8 0.1 collective-permute-start.2
  73.0 2.6 %collective-permute-start.3 = (bf16[1024,256]{1,0:T(8,128)(2,1)S(1)}, bf16[1024,256]{1,0:T(8,128)(2,1)S(1)}, u32[]{:S(2)}, u32[]{:S(2)}) collective-permute-start(bf16[1024,256]{1,0:T(8,128)(2,1)S(1)} %bitcast.33), channel_id=1, source_target_pairs={{0,112},{1,15},{2,114},{3,1},{4,116},{5,3},{6,118},{7,5},{8,120},{... | collective-permute-start | bytes 1572872 | tf_op jit(solution)/shard_map/ppermute | solution.py:423
  75.6 0.1 shard_map.104.refs_2_
  75.7 0.1 collective-permute-start.8
  75.8 2.6 %collective-permute-start.9 = (bf16[1040,256]{1,0:T(8,128)(2,1)S(1)}, bf16[1040,256]{1,0:T(8,128)(2,1)S(1)}, u32[]{:S(2)}, u32[]{:S(2)}) collective-permute-start(bf16[1040,256]{1,0:T(8,128)(2,1)S(1)} %shard_map.104.refs_2_), channel_id=1, source_target_pairs={{0,112},{1,15},{2,114},{3,1},{4,116},{5,3},{6,118},{7,5},{8,120},{... | collective-permute-start | bytes 1597448 | tf_op jit(solution)/shard_map/ppermute | solution.py:423
  78.5 0.2 shard_map.105
  78.6 0.1 pad_add_fusion.1
  78.8 2.5 %shard_map.106 = (f32[256,256]{1,0:T(8,128)S(1)}, f32[32,256]{1,0:T(8,128)S(1)}, f32[8,256]{1,0:T(8,128)S(1)}) custom-call(s32[2]{0:T(128)S(1)} %get-tuple-element.197.refs_0_, bf16[1024,256]{1,0:T(8,128)(2,1)S(1)} %bitcast.34, bf16[1040,256]{1,0:T(8,128)(2,1)S(1)} %shard_map.104.refs_2_, ...), custom_call_target="tpu_custom_call", output_to_operand_aliasing={{0}: (5, {}), {1}: (6, {}), {2}: (7, {})} | custom-call | flops 301989888 | bytes 1000000 | tf_op jit(solution)/shard_map/pallas_call | solution.py:223
  81.3 0.1 pad_add_fusion.3.refs_0_
  81.3 1.1 collective-permute-done.2.refs_1_
  82.5 0.0 collective-permute-done.3.refs_2_
  82.5 0.0 collective-permute-start.6
  82.5 2.7 %collective-permute-start.7 = (bf16[1024,256]{1,0:T(8,128)(2,1)S(1)}, bf16[1024,256]{1,0:T(8,128)(2,1)S(1)}, u32[]{:S(2)}, u32[]{:S(2)}) collective-permute-start(bf16[1024,256]{1,0:T(8,128)(2,1)S(1)} %collective-permute-done.3.refs_2_), channel_id=1, source_target_pairs={{0,112},{1,15},{2,114},{3,1},{4,116},{5,3},{6,118},{7,5},{8,120},{... | collective-permute-start | bytes 1572872 | tf_op jit(solution)/shard_map/ppermute | solution.py:423
  85.2 2.5 %shard_map.107 = (f32[256,256]{1,0:T(8,128)S(1)}, f32[32,256]{1,0:T(8,128)S(1)}, f32[8,256]{1,0:T(8,128)S(1)}) custom-call(s32[2]{0:T(128)S(1)} %pad_add_fusion.3.refs_0_, bf16[1024,256]{1,0:T(8,128)(2,1)S(1)} %collective-permute-done.2.refs_1_, ...), custom_call_target="tpu_custom_call", output_to_operand_aliasing={{0}: (5, {}), {1}: (6, {}), {2}: (7, {})} | custom-call | flops 301989888 | bytes 1000000 | tf_op jit(solution)/shard_map/pallas_call | solution.py:223
  87.7 0.5 collective-permute-done.8.refs_1_
  88.2 0.0 collective-permute-start.12
  88.2 2.7 %collective-permute-start.13 = (bf16[1040,256]{1,0:T(8,128)(2,1)S(1)}, bf16[1040,256]{1,0:T(8,128)(2,1)S(1)}, u32[]{:S(2)}, u32[]{:S(2)}) collective-permute-start(bf16[1040,256]{1,0:T(8,128)(2,1)S(1)} %collective-permute-done.9.refs_2_), channel_id=1, source_target_pairs={{0,112},{1,15},{2,114},{3,1},{4,116},{5,3},{6,118},{7,5},{8,120},{... | collective-permute-start | bytes 1597448 | tf_op jit(solution)/shard_map/ppermute | solution.py:423
  90.9 0.1 pad_add_fusion.5.refs_0_
  90.9 2.5 %shard_map.108 = (f32[256,256]{1,0:T(8,128)S(1)}, f32[32,256]{1,0:T(8,128)S(1)}, f32[8,256]{1,0:T(8,128)S(1)}) custom-call(s32[2]{0:T(128)S(1)} %get-tuple-element.198.refs_0_, bf16[1040,256]{1,0:T(8,128)(2,1)S(1)} %collective-permute-done.8.refs_1_, ...), custom_call_target="tpu_custom_call", output_to_operand_aliasing={{0}: (5, {}), {1}: (6, {}), {2}: (7, {})} | custom-call | flops 306708480 | bytes 1000000 | tf_op jit(solution)/shard_map/pallas_call | solution.py:223
  93.4 0.3 collective-permute-done.6.refs_1_
  93.8 2.7 %collective-permute-start.11 = (bf16[1024,256]{1,0:T(8,128)(2,1)S(1)}, bf16[1024,256]{1,0:T(8,128)(2,1)S(1)}, u32[]{:S(2)}, u32[]{:S(2)}) collective-permute-start(bf16[1024,256]{1,0:T(8,128)(2,1)S(1)} %collective-permute-done.7.refs_2_), channel_id=1, source_target_pairs={{0,112},{1,15},{2,114},{3,1},{4,116},{5,3},{6,118},{7,5},{8,120},{... | collective-permute-start | bytes 1572872 | tf_op jit(solution)/shard_map/ppermute | solution.py:423
  96.5 2.5 %shard_map.109 = (f32[256,256]{1,0:T(8,128)S(1)}, f32[32,256]{1,0:T(8,128)S(1)}, f32[8,256]{1,0:T(8,128)S(1)}) custom-call(s32[2]{0:T(128)S(1)} %pad_add_fusion.5.refs_0_, bf16[1024,256]{1,0:T(8,128)(2,1)S(1)} %collective-permute-done.6.refs_1_, ...), custom_call_target="tpu_custom_call", output_to_operand_aliasing={{0}: (5, {}), {1}: (6, {}), {2}: (7, {})} | custom-call | flops 301989888 | bytes 1000000 | tf_op jit(solution)/shard_map/pallas_call | solution.py:223
  99.0 0.5 collective-permute-done.12.refs_1_
  99.5 2.7 %collective-permute-start.16 = (bf16[1040,256]{1,0:T(8,128)(2,1)S(1)}, bf16[1040,256]{1,0:T(8,128)(2,1)S(1)}, u32[]{:S(2)}, u32[]{:S(2)}) collective-permute-start(bf16[1040,256]{1,0:T(8,128)(2,1)S(1)} %collective-permute-done.13.refs_2_), channel_id=1, source_target_pairs={{0,112},{1,15},{2,114},{3,1},{4,116},{5,3},{6,118},{7,5},{8,120},{... | collective-permute-start | bytes 1597448 | tf_op jit(solution)/shard_map/ppermute | solution.py:423
  102.2 0.1 pad_add_fusion.4.refs_0_
  102.3 0.1 pad_add_fusion.6.refs_0_
  102.3 2.5 %shard_map.110 = (f32[256,256]{1,0:T(8,128)S(1)}, f32[32,256]{1,0:T(8,128)S(1)}, f32[8,256]{1,0:T(8,128)S(1)}) custom-call(s32[2]{0:T(128)S(1)} %pad_add_fusion.4.refs_0_, bf16[1040,256]{1,0:T(8,128)(2,1)S(1)} %collective-permute-done.12.refs_1_, ...), custom_call_target="tpu_custom_call", output_to_operand_aliasing={{0}: (5, {}), {1}: (6, {}), {2}: (7, {})} | custom-call | flops 306708480 | bytes 1000000 | tf_op jit(solution)/shard_map/pallas_call | solution.py:223
  104.8 0.3 collective-permute-done.10.refs_1_
  105.1 2.5 %shard_map.111 = (f32[256,256]{1,0:T(8,128)S(1)}, f32[32,256]{1,0:T(8,128)S(1)}, f32[8,256]{1,0:T(8,128)S(1)}) custom-call(s32[2]{0:T(128)S(1)} %pad_add_fusion.6.refs_0_, bf16[1024,256]{1,0:T(8,128)(2,1)S(1)} %collective-permute-done.10.refs_1_, ...), custom_call_target="tpu_custom_call", output_to_operand_aliasing={{0}: (5, {}), {1}: (6, {}), {2}: (7, {})} | custom-call | flops 301989888 | bytes 1000000 | tf_op jit(solution)/shard_map/pallas_call | solution.py:223
  107.6 3.2 %collective-permute-done.15.refs_1_ = bf16[1040,256]{1,0:T(8,128)(2,1)S(1)} collective-permute-done((bf16[1040,256]{1,0:T(8,128)(2,1)S(1)}, bf16[1040,256]{1,0:T(8,128)(2,1)S(1)}, u32[]{:S(2)}, u32[]{:S(2)}) %collective-permute-start.15) | collective-permute-done | bytes 532512 | tf_op jit(solution)/shard_map/ppermute | solution.py:423
  110.8 2.4 %collective-permute-start.17 = (bf16[1040,256]{1,0:T(8,128)(2,1)S(1)}, bf16[1040,256]{1,0:T(8,128)(2,1)S(1)}, u32[]{:S(2)}, u32[]{:S(2)}) collective-permute-start(bf16[1040,256]{1,0:T(8,128)(2,1)S(1)} %collective-permute-done.16.refs_2_), channel_id=1, source_target_pairs={{0,112},{1,15},{2,114},{3,1},{4,116},{5,3},{6,118},{7,5},{8,120},{... | collective-permute-start | bytes 1597448 | tf_op jit(solution)/shard_map/ppermute | solution.py:423
  113.2 0.1 pad_add_fusion.refs_0_
  113.3 0.1 pad_add_fusion.7.refs_0_
  113.4 2.5 %shard_map.112 = (f32[256,256]{1,0:T(8,128)S(1)}, f32[32,256]{1,0:T(8,128)S(1)}, f32[8,256]{1,0:T(8,128)S(1)}) custom-call(s32[2]{0:T(128)S(1)} %pad_add_fusion.7.refs_0_, bf16[1040,256]{1,0:T(8,128)(2,1)S(1)} %collective-permute-done.15.refs_1_, ...), custom_call_target="tpu_custom_call", output_to_operand_aliasing={{0}: (5, {}), {1}: (6, {}), {2}: (7, {})} | custom-call | flops 306708480 | bytes 1000000 | tf_op jit(solution)/shard_map/pallas_call | solution.py:223
  115.9 6.6 %collective-permute-done.14.refs_1_ = bf16[1024,256]{1,0:T(8,128)(2,1)S(1)} collective-permute-done((bf16[1024,256]{1,0:T(8,128)(2,1)S(1)}, bf16[1024,256]{1,0:T(8,128)(2,1)S(1)}, u32[]{:S(2)}, u32[]{:S(2)}) %collective-permute-start.14) | collective-permute-done | bytes 524320 | tf_op jit(solution)/shard_map/ppermute | solution.py:423
  122.5 1.9 %shard_map.113 = (bf16[16,32,256]{2,1,0:T(8,128)(2,1)}, f32[8,256]{1,0:T(8,128)S(1)}) custom-call(s32[2]{0:T(128)S(1)} %pad_add_fusion.refs_0_, bf16[1024,256]{1,0:T(8,128)(2,1)S(1)} %collective-permute-done.14.refs_1_, bf16[1040,256]{1,0:T(8,128)(2,1)S(1)} %collective-permute-done.17.refs_2_, bf16[64,32,256]{2,1,0:T(8,128)(2,1)S(1)} %get-tuple-element.103.refs_4_.refs_3_, ...), custom_call_target="tpu_custom_call" | custom-call | flops 1000000000 | bytes 1000000 | tf_op jit(solution)/shard_map/pallas_call | solution.py:223
  124.4 10.4 %all-to-all-start.1 = ((bf16[16,32,256]{2,1,0:T(8,128)(2,1)}), bf16[16,32,256]{2,1,0:T(8,128)(2,1)S(1)}, u32[]{:S(2)}, u32[]{:S(2)}) async-start(bf16[16,32,256]{2,1,0:T(8,128)(2,1)} %get-tuple-element.180), calls=%async_computation.1 | async-start | bytes 524288 | tf_op jit(solution)/shard_map/all_to_all | solution.py:557
  134.8 0.0 copy-start.1
  134.8 0.0 copy-start.3
  134.8 2.3 %shard_map.114 = (bf16[256,128]{1,0:T(8,128)(2,1)S(1)}, f32[264,128]{1,0:T(8,128)S(1)}) custom-call(s32[2]{0:T(128)S(1)} %pad_add_fusion.refs_0_, bf16[1024,256]{1,0:T(8,128)(2,1)S(1)} %collective-permute-done.14.refs_1_, bf16[1040,256]{1,0:T(8,128)(2,1)S(1)} %collective-permute-done.17.refs_2_, bf16[64,2,256,128]{3,2,1,0:T(8,128)(2,1)} %shard_map.103.refs_3_, ...), custom_call_target="tpu_custom_call" | custom-call | flops 1000000000 | bytes 1000000 | tf_op jit(solution)/shard_map/pallas_call | solution.py:223
  137.1 0.8 collective-permute-start.18
  137.9 1.0 collective-permute-done.18.r_2_
  138.9 1.0 shard_map.115
  139.8 6.9 %all-to-all-done.1.kvr = bf16[16,32,256]{2,1,0:T(8,128)(2,1)S(1)} async-done(((bf16[16,32,256]{2,1,0:T(8,128)(2,1)}), bf16[16,32,256]{2,1,0:T(8,128)(2,1)S(1)}, u32[]{:S(2)}, u32[]{:S(2)}) %all-to-all-start.1) | async-done | bytes 262176 | tf_op jit(solution)/shard_map/all_to_all | solution.py:557
  146.7 1.4 shard_map.116
  (30 shorter events, 0.2 us)
Async XLA Ops:
  0.6 63.8 %collective-permute-start.1 = (bf16[16384,128]{1,0:T(8,128)(2,1)}, bf16[16384,128]{1,0:T(8,128)(2,1)}, u32[]{:S(2)}, u32[]{:S(2)}) collective-permute-start(bf16[16384,128]{1,0:T(8,128)(2,1)} %param.9), channel_id=1, source_target_pairs={{0,1},{1,0},{2,3},{3,2},{4,5},{5,4},{6,7},{7,6},{8,9},{9,8},{10,11... | collective-permute-start | bytes 12582920 | tf_op jit(solution)/shard_map/ppermute | solution.py:426
  21.2 0.9 copy-start
  22.1 0.7 copy-start.2
  22.9 5.3 %collective-permute-start = (bf16[272,128]{1,0:T(8,128)(2,1)S(1)}, bf16[272,128]{1,0:T(8,128)(2,1)S(1)}, u32[]{:S(2)}, u32[]{:S(2)}) collective-permute-start(bf16[272,128]{1,0:T(8,128)(2,1)S(1)} %get-tuple-element.96), channel_id=1, source_target_pairs={{0,1},{1,0},{2,3},{3,2},{4,5},{5,4},{6,7},{7,6},{8,9},{9,8},{10,11... | collective-permute-start | bytes 208904 | tf_op jit(solution)/shard_map/ppermute | solution.py:426
  29.4 3.9 %copy-start.4 = (bf16[16,16384]{1,0:T(8,128)(2,1)S(1)}, bf16[16,16384]{1,0:T(8,128)(2,1)}, u32[]{:S(2)}) copy-start(bf16[16,16384]{1,0:T(8,128)(2,1)} %param.10) | copy-start | bytes 1572868
  29.4 43.3 %all-to-all-start = ((bf16[8,272,256]{2,1,0:T(8,128)(2,1)}), bf16[8,272,256]{2,1,0:T(8,128)(2,1)S(1)}, u32[]{:S(2)}, u32[]{:S(2)}) async-start(bf16[8,272,256]{2,1,0:T(8,128)(2,1)} %shard_map.102), calls=%async_computation | async-start | bytes 2228224 | tf_op jit(solution)/shard_map/all_to_all | solution.py:463
  33.4 29.2 %collective-permute-start.4 = (bf16[16,16512]{1,0:T(8,128)(2,1)S(1)}, bf16[16,16512]{1,0:T(8,128)(2,1)S(1)}, u32[]{:S(2)}, u32[]{:S(2)}) collective-permute-start(bf16[16,16512]{1,0:T(8,128)(2,1)S(1)} %fusion.1), channel_id=1, source_target_pairs={{0,14},{1,30},{2,34},{3,50},{4,70},{5,86},{6,106},{7,122},{8,6},{9... | collective-permute-start | bytes 1585160 | tf_op jit(solution)/shard_map/ppermute | solution.py:454
  62.6 15.9 %collective-permute-start.5 = (bf16[16,16512]{1,0:T(8,128)(2,1)S(1)}, bf16[16,16512]{1,0:T(8,128)(2,1)S(1)}, u32[]{:S(2)}, u32[]{:S(2)}) collective-permute-start(bf16[16,16512]{1,0:T(8,128)(2,1)S(1)} %collective-permute-done.4.kv), channel_id=1, source_target_pairs={{0,1},{1,0},{2,3},{3,2},{4,5},{5,4},{6,7},{7,6},{8,9},{9,8},{10,11... | collective-permute-start | bytes 1585160 | tf_op jit(solution)/shard_map/ppermute | solution.py:426
  72.8 9.7 %collective-permute-start.2 = (bf16[1024,256]{1,0:T(8,128)(2,1)S(1)}, bf16[1024,256]{1,0:T(8,128)(2,1)S(1)}, u32[]{:S(2)}, u32[]{:S(2)}) collective-permute-start(bf16[1024,256]{1,0:T(8,128)(2,1)S(1)} %bitcast.32), channel_id=1, source_target_pairs={{0,16},{1,3},{2,18},{3,5},{4,20},{5,7},{6,22},{7,9},{8,24},{9,11},... | collective-permute-start | bytes 1572872 | tf_op jit(solution)/shard_map/ppermute | solution.py:423
  73.0 9.5 %collective-permute-start.3 = (bf16[1024,256]{1,0:T(8,128)(2,1)S(1)}, bf16[1024,256]{1,0:T(8,128)(2,1)S(1)}, u32[]{:S(2)}, u32[]{:S(2)}) collective-permute-start(bf16[1024,256]{1,0:T(8,128)(2,1)S(1)} %bitcast.33), channel_id=1, source_target_pairs={{0,112},{1,15},{2,114},{3,1},{4,116},{5,3},{6,118},{7,5},{8,120},{... | collective-permute-start | bytes 1572872 | tf_op jit(solution)/shard_map/ppermute | solution.py:423
  75.7 12.5 %collective-permute-start.8 = (bf16[1040,256]{1,0:T(8,128)(2,1)S(1)}, bf16[1040,256]{1,0:T(8,128)(2,1)S(1)}, u32[]{:S(2)}, u32[]{:S(2)}) collective-permute-start(bf16[1040,256]{1,0:T(8,128)(2,1)S(1)} %shard_map.104.refs_2_), channel_id=1, source_target_pairs={{0,16},{1,3},{2,18},{3,5},{4,20},{5,7},{6,22},{7,9},{8,24},{9,11},... | collective-permute-start | bytes 1597448 | tf_op jit(solution)/shard_map/ppermute | solution.py:423
  75.8 12.4 %collective-permute-start.9 = (bf16[1040,256]{1,0:T(8,128)(2,1)S(1)}, bf16[1040,256]{1,0:T(8,128)(2,1)S(1)}, u32[]{:S(2)}, u32[]{:S(2)}) collective-permute-start(bf16[1040,256]{1,0:T(8,128)(2,1)S(1)} %shard_map.104.refs_2_), channel_id=1, source_target_pairs={{0,112},{1,15},{2,114},{3,1},{4,116},{5,3},{6,118},{7,5},{8,120},{... | collective-permute-start | bytes 1597448 | tf_op jit(solution)/shard_map/ppermute | solution.py:423
  82.5 11.3 %collective-permute-start.6 = (bf16[1024,256]{1,0:T(8,128)(2,1)S(1)}, bf16[1024,256]{1,0:T(8,128)(2,1)S(1)}, u32[]{:S(2)}, u32[]{:S(2)}) collective-permute-start(bf16[1024,256]{1,0:T(8,128)(2,1)S(1)} %collective-permute-done.2.refs_1_), channel_id=1, source_target_pairs={{0,16},{1,3},{2,18},{3,5},{4,20},{5,7},{6,22},{7,9},{8,24},{9,11},... | collective-permute-start | bytes 1572872 | tf_op jit(solution)/shard_map/ppermute | solution.py:423
  82.5 11.3 %collective-permute-start.7 = (bf16[1024,256]{1,0:T(8,128)(2,1)S(1)}, bf16[1024,256]{1,0:T(8,128)(2,1)S(1)}, u32[]{:S(2)}, u32[]{:S(2)}) collective-permute-start(bf16[1024,256]{1,0:T(8,128)(2,1)S(1)} %collective-permute-done.3.refs_2_), channel_id=1, source_target_pairs={{0,112},{1,15},{2,114},{3,1},{4,116},{5,3},{6,118},{7,5},{8,120},{... | collective-permute-start | bytes 1572872 | tf_op jit(solution)/shard_map/ppermute | solution.py:423
  88.2 11.3 %collective-permute-start.12 = (bf16[1040,256]{1,0:T(8,128)(2,1)S(1)}, bf16[1040,256]{1,0:T(8,128)(2,1)S(1)}, u32[]{:S(2)}, u32[]{:S(2)}) collective-permute-start(bf16[1040,256]{1,0:T(8,128)(2,1)S(1)} %collective-permute-done.8.refs_1_), channel_id=1, source_target_pairs={{0,16},{1,3},{2,18},{3,5},{4,20},{5,7},{6,22},{7,9},{8,24},{9,11},... | collective-permute-start | bytes 1597448 | tf_op jit(solution)/shard_map/ppermute | solution.py:423
  88.2 11.3 %collective-permute-start.13 = (bf16[1040,256]{1,0:T(8,128)(2,1)S(1)}, bf16[1040,256]{1,0:T(8,128)(2,1)S(1)}, u32[]{:S(2)}, u32[]{:S(2)}) collective-permute-start(bf16[1040,256]{1,0:T(8,128)(2,1)S(1)} %collective-permute-done.9.refs_2_), channel_id=1, source_target_pairs={{0,112},{1,15},{2,114},{3,1},{4,116},{5,3},{6,118},{7,5},{8,120},{... | collective-permute-start | bytes 1597448 | tf_op jit(solution)/shard_map/ppermute | solution.py:423
  93.8 11.3 %collective-permute-start.10 = (bf16[1024,256]{1,0:T(8,128)(2,1)S(1)}, bf16[1024,256]{1,0:T(8,128)(2,1)S(1)}, u32[]{:S(2)}, u32[]{:S(2)}) collective-permute-start(bf16[1024,256]{1,0:T(8,128)(2,1)S(1)} %collective-permute-done.6.refs_1_), channel_id=1, source_target_pairs={{0,16},{1,3},{2,18},{3,5},{4,20},{5,7},{6,22},{7,9},{8,24},{9,11},... | collective-permute-start | bytes 1572872 | tf_op jit(solution)/shard_map/ppermute | solution.py:423
  93.8 11.3 %collective-permute-start.11 = (bf16[1024,256]{1,0:T(8,128)(2,1)S(1)}, bf16[1024,256]{1,0:T(8,128)(2,1)S(1)}, u32[]{:S(2)}, u32[]{:S(2)}) collective-permute-start(bf16[1024,256]{1,0:T(8,128)(2,1)S(1)} %collective-permute-done.7.refs_2_), channel_id=1, source_target_pairs={{0,112},{1,15},{2,114},{3,1},{4,116},{5,3},{6,118},{7,5},{8,120},{... | collective-permute-start | bytes 1572872 | tf_op jit(solution)/shard_map/ppermute | solution.py:423
  99.5 11.3 %collective-permute-start.15 = (bf16[1040,256]{1,0:T(8,128)(2,1)S(1)}, bf16[1040,256]{1,0:T(8,128)(2,1)S(1)}, u32[]{:S(2)}, u32[]{:S(2)}) collective-permute-start(bf16[1040,256]{1,0:T(8,128)(2,1)S(1)} %collective-permute-done.12.refs_1_), channel_id=1, source_target_pairs={{0,16},{1,3},{2,18},{3,5},{4,20},{5,7},{6,22},{7,9},{8,24},{9,11},... | collective-permute-start | bytes 1597448 | tf_op jit(solution)/shard_map/ppermute | solution.py:423
  99.5 11.3 %collective-permute-start.16 = (bf16[1040,256]{1,0:T(8,128)(2,1)S(1)}, bf16[1040,256]{1,0:T(8,128)(2,1)S(1)}, u32[]{:S(2)}, u32[]{:S(2)}) collective-permute-start(bf16[1040,256]{1,0:T(8,128)(2,1)S(1)} %collective-permute-done.13.refs_2_), channel_id=1, source_target_pairs={{0,112},{1,15},{2,114},{3,1},{4,116},{5,3},{6,118},{7,5},{8,120},{... | collective-permute-start | bytes 1597448 | tf_op jit(solution)/shard_map/ppermute | solution.py:423
  110.8 11.6 %collective-permute-start.17 = (bf16[1040,256]{1,0:T(8,128)(2,1)S(1)}, bf16[1040,256]{1,0:T(8,128)(2,1)S(1)}, u32[]{:S(2)}, u32[]{:S(2)}) collective-permute-start(bf16[1040,256]{1,0:T(8,128)(2,1)S(1)} %collective-permute-done.16.refs_2_), channel_id=1, source_target_pairs={{0,112},{1,15},{2,114},{3,1},{4,116},{5,3},{6,118},{7,5},{8,120},{... | collective-permute-start | bytes 1597448 | tf_op jit(solution)/shard_map/ppermute | solution.py:423
  113.2 9.2 %collective-permute-start.14 = (bf16[1024,256]{1,0:T(8,128)(2,1)S(1)}, bf16[1024,256]{1,0:T(8,128)(2,1)S(1)}, u32[]{:S(2)}, u32[]{:S(2)}) collective-permute-start(bf16[1024,256]{1,0:T(8,128)(2,1)S(1)} %collective-permute-done.10.refs_1_), channel_id=1, source_target_pairs={{0,16},{1,3},{2,18},{3,5},{4,20},{5,7},{6,22},{7,9},{8,24},{9,11},... | collective-permute-start | bytes 1572872 | tf_op jit(solution)/shard_map/ppermute | solution.py:423
  122.4 12.3 %copy-start.5 = (f32[144]{0:T(256)S(1)}, f32[144]{0:T(256)}, u32[]{:S(2)}) copy-start(f32[144]{0:T(256)} %param.11) | copy-start | bytes 1732
  124.4 22.3 %all-to-all-start.1 = ((bf16[16,32,256]{2,1,0:T(8,128)(2,1)}), bf16[16,32,256]{2,1,0:T(8,128)(2,1)S(1)}, u32[]{:S(2)}, u32[]{:S(2)}) async-start(bf16[16,32,256]{2,1,0:T(8,128)(2,1)} %get-tuple-element.180), calls=%async_computation.1 | async-start | bytes 524288 | tf_op jit(solution)/shard_map/all_to_all | solution.py:557
  134.8 4.1 %copy-start.1 = (bf16[512,128]{1,0:T(8,128)(2,1)S(1)}, bf16[512,128]{1,0:T(8,128)(2,1)}, u32[]{:S(2)}) copy-start(bf16[512,128]{1,0:T(8,128)(2,1)} %r_4_.1) | copy-start | bytes 393220
  134.8 4.1 %copy-start.3 = (f32[128]{0:T(128)S(1)}, f32[128]{0:T(128)}, u32[]{:S(2)}) copy-start(f32[128]{0:T(128)} %param.7) | copy-start | bytes 1540
  137.1 1.8 %collective-permute-start.18 = (f32[264,128]{1,0:T(8,128)S(1)}, f32[264,128]{1,0:T(8,128)S(1)}, u32[]{:S(2)}, u32[]{:S(2)}) collective-permute-start(f32[264,128]{1,0:T(8,128)S(1)} %get-tuple-element.175), channel_id=1, source_target_pairs={{0,1},{1,0},{2,3},{3,2},{4,5},{5,4},{6,7},{7,6},{8,9},{9,8},{10,11... | collective-permute-start | bytes 405512 | tf_op jit(solution)/shard_map/ppermute | solution.py:426

commit v3 on v2

--- a/solution.py
+++ b/solution.py
@@ -187,8 +187,11 @@
     return total
 
 
-def fetch(table, m, pairs, sems):
-    copies = []
+def fetch(table, m, pairs, sems, xs, x_buf):
+    copies = [
+        pltpu.make_async_copy(x, x_buf.at[i, pl.ds(0, x.shape[0])], sems.at[len(pairs), i])
+        for i, x in enumerate(xs)
+    ]
     for i in range(m):
         for j, (whole, buf) in enumerate(pairs):
             n = buf.shape[1]
@@ -198,12 +201,13 @@
         c.start()
     for c in copies:
         c.wait()
+    return [x_buf.at[i, pl.ds(0, x.shape[0])] for i, x in enumerate(xs)]
 
 
 def matmul_kernel(m, table, *refs):
     xs, w_all, kv_all = refs[:m], refs[m], refs[m + 1]
-    q_in, kv_in, st_in, q_out, kv_out, st_out, w_buf, kv_buf, sems = refs[m + 2 :]
-    fetch(table, m, ((w_all, w_buf), (kv_all, kv_buf)), sems)
+    q_in, kv_in, st_in, q_out, kv_out, st_out, x_buf, w_buf, kv_buf, sems = refs[m + 2 :]
+    xs = fetch(table, m, ((w_all, w_buf), (kv_all, kv_buf)), sems, xs, x_buf)
     ws, kvs = [w_buf.at[i] for i in range(m)], [kv_buf.at[i] for i in range(m)]
     q_out[...] = q_sum(xs, ws, q_in)
     total, squares, largest = kv_rows(xs, kvs, kv_in, st_in)
@@ -218,15 +222,16 @@
     hbm = pl.BlockSpec(memory_space=pltpu.HBM)
     vmem = pl.BlockSpec(memory_space=pltpu.VMEM)
     smem = pl.BlockSpec(memory_space=pltpu.SMEM)
-    specs = [smem] + [vmem] * m + [hbm] * len(weights)
+    specs = [smem] + [hbm] * (m + len(weights))
     specs += [smem if a.dtype == jnp.int32 else vmem for a in rest]
     return pl.pallas_call(
         kernel,
         out_shape=out_shape,
         in_specs=specs,
         out_specs=tuple(vmem for _ in out_shape),
-        scratch_shapes=[pltpu.VMEM((m, n) + w.shape[1:], w.dtype) for w in weights]
-        + [pltpu.SemaphoreType.DMA((len(weights), m))],
+        scratch_shapes=[pltpu.VMEM((m, max(x.shape[0] for x in xs), xs[0].shape[1]), BF16)]
+        + [pltpu.VMEM((m, n) + w.shape[1:], w.dtype) for w in weights]
+        + [pltpu.SemaphoreType.DMA((len(weights) + 1, m))],
         input_output_aliases=aliases or {},
         compiler_params=pltpu.CompilerParams(vmem_limit_bytes=RING_VMEM),
         cost_estimate=pl.CostEstimate(flops=flops, bytes_accessed=10**6, transcendentals=0),
@@ -250,8 +255,8 @@
 
 def last_kv_kernel(d, m, table, *refs):
     xs, kv_all = refs[:m], refs[m]
-    core, kv_in, st_in, kvscale, kcos, ksin, kvt, st_out, kv_buf, sems = refs[m + 1 :]
-    fetch(table, m, ((kv_all, kv_buf),), sems)
+    core, kv_in, st_in, kvscale, kcos, ksin, kvt, st_out, x_buf, kv_buf, sems = refs[m + 1 :]
+    xs = fetch(table, m, ((kv_all, kv_buf),), sems, xs, x_buf)
     t, squares, largest = kv_rows(xs, [kv_buf.at[i] for i in range(m)], kv_in, st_in)
     st_out[0:1, :] = squares
     st_out[1:2, :] = largest
@@ -289,8 +294,8 @@
 
 def last_q_kernel(d, m, table, *refs):
     xs, w_all = refs[:m], refs[m]
-    q_in, st, wscale, cosine, sine, mine, msg, w_buf, sems = refs[m + 1 :]
-    fetch(table, m, ((w_all, w_buf),), sems)
+    q_in, st, wscale, cosine, sine, mine, msg, x_buf, w_buf, sems = refs[m + 1 :]
+    xs = fetch(table, m, ((w_all, w_buf),), sems, xs, x_buf)
     q = q_sum(xs, [w_buf.at[i] for i in range(m)], q_in)
     half = q.shape[0]
     squares, largest = st[0:1, :], st[1:2, :]

time: 149 us -> 149 us (level)
  no operation moved by 1% of the time
where the time goes in v3:
time: 149 us; the launch traced here: 148 us
  starting transfers between devices  56.5 us (38%)
  waiting for transfers between devices  50.3 us (34%)
  Pallas kernels  34.8 us (23%)
  local copies, waits for them, and re-layouts  2.5 us (2%)
  other arithmetic  2.48 us (2%)
  between operations  1.82 us (1%)
    ppermute x1, waiting for transfers between devices, body(): lax.ppermute(jnp.concatenate([w_kv, scales], axis=1), 'tp', to_row)  26.9 us
    ppermute x4, starting transfers between devices, swap(): return lax.ppermute(v, 'tp', to_partner)  23.2 us
    pallas_call x9, Pallas kernels, arrivals_call(): pl.pallas_call(kernel, out_shape=out_shape, in_specs=specs, out_specs=tup...  22.6 us
    ppermute x14, starting transfers between devices, second(): return lax.ppermute(v, 'tp', pairs)  18.7 us
    ppermute x14, waiting for transfers between devices, second(): return lax.ppermute(v, 'tp', pairs)  11.9 us
    all_to_all x1, starting transfers between devices, body(): lax.all_to_all(kvt, 'tp', split_axis=0, concat_axis=0, tiled=False, axis_...  10.6 us
    pallas_call x1, Pallas kernels, arrange_weights(): pl.pallas_call(weights_kernel, out_shape=out, in_specs=[pl.BlockSpec(memo...  8.29 us
    all_to_all x1, waiting for transfers between devices, body(): lax.all_to_all(kvt, 'tp', split_axis=0, concat_axis=0, tiled=False, axis_...  6.82 us
  transfers between devices with their start and end apart: 21, of which 11 were waited for; matrix products, arithmetic and copies ran while one was open for 2% of the time, Pallas kernels for 21%

profile of v3, /device:TPU:513, one launch (start us, length us, event | category | flops | bytes accessed | tf_op | source)
XLA Modules:
  0.0 148.5 jit_solution(6610770453145198815)
XLA Ops:
  0.6 20.5 %collective-permute-start.1 = (bf16[16384,128]{1,0:T(8,128)(2,1)}, bf16[16384,128]{1,0:T(8,128)(2,1)}, u32[]{:S(2)}, u32[]{:S(2)}) collective-permute-start(bf16[16384,128]{1,0:T(8,128)(2,1)} %param.9), channel_id=1, source_target_pairs={{0,1},{1,0},{2,3},{3,2},{4,5},{5,4},{6,7},{7,6},{8,9},{9,8},{10,11... | collective-permute-start | bytes 12582920 | tf_op jit(solution)/shard_map/ppermute | solution.py:431
  21.2 0.9 copy-done
  22.1 0.7 copy-done.2
  22.7 0.2 shard_map.101
  22.9 0.2 collective-permute-start
  23.1 0.7 convert_bitcast_fusion.2
  23.8 0.7 convert_bitcast_fusion.1
  24.5 0.1 copy.35
  24.6 3.7 %collective-permute-done.recv = bf16[272,128]{1,0:T(8,128)(2,1)S(1)} collective-permute-done((bf16[272,128]{1,0:T(8,128)(2,1)S(1)}, bf16[272,128]{1,0:T(8,128)(2,1)S(1)}, u32[]{:S(2)}, u32[]{:S(2)}) %collective-permute-start) | collective-permute-done | bytes 69664 | tf_op jit(solution)/shard_map/ppermute | solution.py:431
  28.3 1.1 shard_map.102
  29.4 3.9 %all-to-all-start = ((bf16[8,272,256]{2,1,0:T(8,128)(2,1)}), bf16[8,272,256]{2,1,0:T(8,128)(2,1)S(1)}, u32[]{:S(2)}, u32[]{:S(2)}) async-start(bf16[8,272,256]{2,1,0:T(8,128)(2,1)} %shard_map.102), calls=%async_computation | async-start | bytes 2228224 | tf_op jit(solution)/shard_map/all_to_all | solution.py:468
  33.4 0.1 collective-permute-start.4
  34.6 0.1 fusion.17
  34.7 1.0 multiply_sine_fusion
  35.6 26.9 %collective-permute-done.4.kv = bf16[16,16512]{1,0:T(8,128)(2,1)S(1)} collective-permute-done((bf16[16,16512]{1,0:T(8,128)(2,1)S(1)}, bf16[16,16512]{1,0:T(8,128)(2,1)S(1)}, u32[]{:S(2)}, u32[]{:S(2)}) %collective-permute-start.4) | collective-permute-done | bytes 528416 | tf_op jit(solution)/shard_map/ppermute | solution.py:459
  62.6 1.7 %collective-permute-start.5 = (bf16[16,16512]{1,0:T(8,128)(2,1)S(1)}, bf16[16,16512]{1,0:T(8,128)(2,1)S(1)}, u32[]{:S(2)}, u32[]{:S(2)}) collective-permute-start(bf16[16,16512]{1,0:T(8,128)(2,1)S(1)} %collective-permute-done.4.kv), channel_id=1, source_target_pairs={{0,1},{1,0},{2,3},{3,2},{4,5},{5,4},{6,7},{7,6},{8,9},{9,8},{10,11... | collective-permute-start | bytes 1585160 | tf_op jit(solution)/shard_map/ppermute | solution.py:431
  64.3 0.1 multiply_sine_fusion.2
  64.5 0.0 collective-permute-done.1
  64.5 8.3 %shard_map.103.refs_3_ = bf16[64,2,256,128]{3,2,1,0:T(8,128)(2,1)} custom-call(s32[1]{0:T(128)} %bitcast.core.refs_4_.r_0_, bf16[64,256,128]{2,1,0:T(8,128)(2,1)} %bitcast.37, bf16[64,256,128]{2,1,0:T(8,128)(2,1)} %bitcast.3.wo), custom_call_target="tpu_custom_call" | custom-call | flops 1000000000 | bytes 20000000 | tf_op jit(solution)/shard_map/pallas_call | solution.py:107
  72.8 0.1 collective-permute-start.2
  73.0 2.6 %collective-permute-start.3 = (bf16[1024,256]{1,0:T(8,128)(2,1)S(1)}, bf16[1024,256]{1,0:T(8,128)(2,1)S(1)}, u32[]{:S(2)}, u32[]{:S(2)}) collective-permute-start(bf16[1024,256]{1,0:T(8,128)(2,1)S(1)} %bitcast.33), channel_id=1, source_target_pairs={{0,112},{1,15},{2,114},{3,1},{4,116},{5,3},{6,118},{7,5},{8,120},{... | collective-permute-start | bytes 1572872 | tf_op jit(solution)/shard_map/ppermute | solution.py:428
  75.6 0.1 shard_map.104.refs_2_
  75.7 0.1 collective-permute-start.8
  75.8 2.6 %collective-permute-start.9 = (bf16[1040,256]{1,0:T(8,128)(2,1)S(1)}, bf16[1040,256]{1,0:T(8,128)(2,1)S(1)}, u32[]{:S(2)}, u32[]{:S(2)}) collective-permute-start(bf16[1040,256]{1,0:T(8,128)(2,1)S(1)} %shard_map.104.refs_2_), channel_id=1, source_target_pairs={{0,112},{1,15},{2,114},{3,1},{4,116},{5,3},{6,118},{7,5},{8,120},{... | collective-permute-start | bytes 1597448 | tf_op jit(solution)/shard_map/ppermute | solution.py:428
  78.5 0.2 shard_map.105
  78.6 0.1 pad_add_fusion.1
  78.8 2.6 %shard_map.106 = (f32[256,256]{1,0:T(8,128)S(1)}, f32[32,256]{1,0:T(8,128)S(1)}, f32[8,256]{1,0:T(8,128)S(1)}) custom-call(s32[2]{0:T(128)S(1)} %get-tuple-element.197.refs_0_, bf16[1024,256]{1,0:T(8,128)(2,1)S(1)} %bitcast.34, bf16[1040,256]{1,0:T(8,128)(2,1)S(1)} %shard_map.104.refs_2_, ...), custom_call_target="tpu_custom_call", output_to_operand_aliasing={{0}: (5, {}), {1}: (6, {}), {2}: (7, {})} | custom-call | flops 301989888 | bytes 1000000 | tf_op jit(solution)/shard_map/pallas_call | solution.py:227
  81.4 0.1 pad_add_fusion.3.refs_0_
  81.4 1.0 collective-permute-done.2.refs_1_
  82.5 0.0 collective-permute-done.3.refs_2_
  82.5 0.0 collective-permute-start.6
  82.5 2.7 %collective-permute-start.7 = (bf16[1024,256]{1,0:T(8,128)(2,1)S(1)}, bf16[1024,256]{1,0:T(8,128)(2,1)S(1)}, u32[]{:S(2)}, u32[]{:S(2)}) collective-permute-start(bf16[1024,256]{1,0:T(8,128)(2,1)S(1)} %collective-permute-done.3.refs_2_), channel_id=1, source_target_pairs={{0,112},{1,15},{2,114},{3,1},{4,116},{5,3},{6,118},{7,5},{8,120},{... | collective-permute-start | bytes 1572872 | tf_op jit(solution)/shard_map/ppermute | solution.py:428
  85.2 2.6 %shard_map.107 = (f32[256,256]{1,0:T(8,128)S(1)}, f32[32,256]{1,0:T(8,128)S(1)}, f32[8,256]{1,0:T(8,128)S(1)}) custom-call(s32[2]{0:T(128)S(1)} %pad_add_fusion.3.refs_0_, bf16[1024,256]{1,0:T(8,128)(2,1)S(1)} %collective-permute-done.2.refs_1_, ...), custom_call_target="tpu_custom_call", output_to_operand_aliasing={{0}: (5, {}), {1}: (6, {}), {2}: (7, {})} | custom-call | flops 301989888 | bytes 1000000 | tf_op jit(solution)/shard_map/pallas_call | solution.py:227
  87.7 0.4 collective-permute-done.8.refs_1_
  88.2 0.0 collective-permute-start.12
  88.2 2.7 %collective-permute-start.13 = (bf16[1040,256]{1,0:T(8,128)(2,1)S(1)}, bf16[1040,256]{1,0:T(8,128)(2,1)S(1)}, u32[]{:S(2)}, u32[]{:S(2)}) collective-permute-start(bf16[1040,256]{1,0:T(8,128)(2,1)S(1)} %collective-permute-done.9.refs_2_), channel_id=1, source_target_pairs={{0,112},{1,15},{2,114},{3,1},{4,116},{5,3},{6,118},{7,5},{8,120},{... | collective-permute-start | bytes 1597448 | tf_op jit(solution)/shard_map/ppermute | solution.py:428
  90.9 0.1 pad_add_fusion.5.refs_0_
  90.9 2.6 %shard_map.108 = (f32[256,256]{1,0:T(8,128)S(1)}, f32[32,256]{1,0:T(8,128)S(1)}, f32[8,256]{1,0:T(8,128)S(1)}) custom-call(s32[2]{0:T(128)S(1)} %get-tuple-element.198.refs_0_, bf16[1040,256]{1,0:T(8,128)(2,1)S(1)} %collective-permute-done.8.refs_1_, ...), custom_call_target="tpu_custom_call", output_to_operand_aliasing={{0}: (5, {}), {1}: (6, {}), {2}: (7, {})} | custom-call | flops 306708480 | bytes 1000000 | tf_op jit(solution)/shard_map/pallas_call | solution.py:227
  93.5 0.2 collective-permute-done.6.refs_1_
  93.8 2.7 %collective-permute-start.11 = (bf16[1024,256]{1,0:T(8,128)(2,1)S(1)}, bf16[1024,256]{1,0:T(8,128)(2,1)S(1)}, u32[]{:S(2)}, u32[]{:S(2)}) collective-permute-start(bf16[1024,256]{1,0:T(8,128)(2,1)S(1)} %collective-permute-done.7.refs_2_), channel_id=1, source_target_pairs={{0,112},{1,15},{2,114},{3,1},{4,116},{5,3},{6,118},{7,5},{8,120},{... | collective-permute-start | bytes 1572872 | tf_op jit(solution)/shard_map/ppermute | solution.py:428
  96.5 2.6 %shard_map.109 = (f32[256,256]{1,0:T(8,128)S(1)}, f32[32,256]{1,0:T(8,128)S(1)}, f32[8,256]{1,0:T(8,128)S(1)}) custom-call(s32[2]{0:T(128)S(1)} %pad_add_fusion.5.refs_0_, bf16[1024,256]{1,0:T(8,128)(2,1)S(1)} %collective-permute-done.6.refs_1_, ...), custom_call_target="tpu_custom_call", output_to_operand_aliasing={{0}: (5, {}), {1}: (6, {}), {2}: (7, {})} | custom-call | flops 301989888 | bytes 1000000 | tf_op jit(solution)/shard_map/pallas_call | solution.py:227
  99.1 0.4 collective-permute-done.12.refs_1_
  99.5 2.7 %collective-permute-start.16 = (bf16[1040,256]{1,0:T(8,128)(2,1)S(1)}, bf16[1040,256]{1,0:T(8,128)(2,1)S(1)}, u32[]{:S(2)}, u32[]{:S(2)}) collective-permute-start(bf16[1040,256]{1,0:T(8,128)(2,1)S(1)} %collective-permute-done.13.refs_2_), channel_id=1, source_target_pairs={{0,112},{1,15},{2,114},{3,1},{4,116},{5,3},{6,118},{7,5},{8,120},{... | collective-permute-start | bytes 1597448 | tf_op jit(solution)/shard_map/ppermute | solution.py:428
  102.2 0.1 pad_add_fusion.4.refs_0_
  102.3 0.1 pad_add_fusion.6.refs_0_
  102.3 2.6 %shard_map.110 = (f32[256,256]{1,0:T(8,128)S(1)}, f32[32,256]{1,0:T(8,128)S(1)}, f32[8,256]{1,0:T(8,128)S(1)}) custom-call(s32[2]{0:T(128)S(1)} %pad_add_fusion.4.refs_0_, bf16[1040,256]{1,0:T(8,128)(2,1)S(1)} %collective-permute-done.12.refs_1_, ...), custom_call_target="tpu_custom_call", output_to_operand_aliasing={{0}: (5, {}), {1}: (6, {}), {2}: (7, {})} | custom-call | flops 306708480 | bytes 1000000 | tf_op jit(solution)/shard_map/pallas_call | solution.py:227
  104.9 0.2 collective-permute-done.10.refs_1_
  105.1 2.6 %shard_map.111 = (f32[256,256]{1,0:T(8,128)S(1)}, f32[32,256]{1,0:T(8,128)S(1)}, f32[8,256]{1,0:T(8,128)S(1)}) custom-call(s32[2]{0:T(128)S(1)} %pad_add_fusion.6.refs_0_, bf16[1024,256]{1,0:T(8,128)(2,1)S(1)} %collective-permute-done.10.refs_1_, ...), custom_call_target="tpu_custom_call", output_to_operand_aliasing={{0}: (5, {}), {1}: (6, {}), {2}: (7, {})} | custom-call | flops 301989888 | bytes 1000000 | tf_op jit(solution)/shard_map/pallas_call | solution.py:227
  107.7 3.1 %collective-permute-done.15.refs_1_ = bf16[1040,256]{1,0:T(8,128)(2,1)S(1)} collective-permute-done((bf16[1040,256]{1,0:T(8,128)(2,1)S(1)}, bf16[1040,256]{1,0:T(8,128)(2,1)S(1)}, u32[]{:S(2)}, u32[]{:S(2)}) %collective-permute-start.15) | collective-permute-done | bytes 532512 | tf_op jit(solution)/shard_map/ppermute | solution.py:428
  110.8 2.4 %collective-permute-start.17 = (bf16[1040,256]{1,0:T(8,128)(2,1)S(1)}, bf16[1040,256]{1,0:T(8,128)(2,1)S(1)}, u32[]{:S(2)}, u32[]{:S(2)}) collective-permute-start(bf16[1040,256]{1,0:T(8,128)(2,1)S(1)} %collective-permute-done.16.refs_2_), channel_id=1, source_target_pairs={{0,112},{1,15},{2,114},{3,1},{4,116},{5,3},{6,118},{7,5},{8,120},{... | collective-permute-start | bytes 1597448 | tf_op jit(solution)/shard_map/ppermute | solution.py:428
  113.2 0.1 pad_add_fusion.refs_0_
  113.3 0.1 pad_add_fusion.7.refs_0_
  113.4 2.6 %shard_map.112 = (f32[256,256]{1,0:T(8,128)S(1)}, f32[32,256]{1,0:T(8,128)S(1)}, f32[8,256]{1,0:T(8,128)S(1)}) custom-call(s32[2]{0:T(128)S(1)} %pad_add_fusion.7.refs_0_, bf16[1040,256]{1,0:T(8,128)(2,1)S(1)} %collective-permute-done.15.refs_1_, ...), custom_call_target="tpu_custom_call", output_to_operand_aliasing={{0}: (5, {}), {1}: (6, {}), {2}: (7, {})} | custom-call | flops 306708480 | bytes 1000000 | tf_op jit(solution)/shard_map/pallas_call | solution.py:227
  116.0 6.5 %collective-permute-done.14.refs_1_ = bf16[1024,256]{1,0:T(8,128)(2,1)S(1)} collective-permute-done((bf16[1024,256]{1,0:T(8,128)(2,1)S(1)}, bf16[1024,256]{1,0:T(8,128)(2,1)S(1)}, u32[]{:S(2)}, u32[]{:S(2)}) %collective-permute-start.14) | collective-permute-done | bytes 524320 | tf_op jit(solution)/shard_map/ppermute | solution.py:428
  122.5 2.0 %shard_map.113 = (bf16[16,32,256]{2,1,0:T(8,128)(2,1)}, f32[8,256]{1,0:T(8,128)S(1)}) custom-call(s32[2]{0:T(128)S(1)} %pad_add_fusion.refs_0_, bf16[1024,256]{1,0:T(8,128)(2,1)S(1)} %collective-permute-done.14.refs_1_, bf16[1040,256]{1,0:T(8,128)(2,1)S(1)} %collective-permute-done.17.refs_2_, bf16[64,32,256]{2,1,0:T(8,128)(2,1)S(1)} %get-tuple-element.103.refs_4_.refs_3_, ...), custom_call_target="tpu_custom_call" | custom-call | flops 1000000000 | bytes 1000000 | tf_op jit(solution)/shard_map/pallas_call | solution.py:227
  124.5 10.6 %all-to-all-start.1 = ((bf16[16,32,256]{2,1,0:T(8,128)(2,1)}), bf16[16,32,256]{2,1,0:T(8,128)(2,1)S(1)}, u32[]{:S(2)}, u32[]{:S(2)}) async-start(bf16[16,32,256]{2,1,0:T(8,128)(2,1)} %get-tuple-element.180), calls=%async_computation.1 | async-start | bytes 524288 | tf_op jit(solution)/shard_map/all_to_all | solution.py:562
  135.1 0.0 copy-start.1
  135.1 0.0 copy-start.3
  135.2 2.4 %shard_map.114 = (bf16[256,128]{1,0:T(8,128)(2,1)S(1)}, f32[264,128]{1,0:T(8,128)S(1)}) custom-call(s32[2]{0:T(128)S(1)} %pad_add_fusion.refs_0_, bf16[1024,256]{1,0:T(8,128)(2,1)S(1)} %collective-permute-done.14.refs_1_, bf16[1040,256]{1,0:T(8,128)(2,1)S(1)} %collective-permute-done.17.refs_2_, bf16[64,2,256,128]{3,2,1,0:T(8,128)(2,1)} %shard_map.103.refs_3_, ...), custom_call_target="tpu_custom_call" | custom-call | flops 1000000000 | bytes 1000000 | tf_op jit(solution)/shard_map/pallas_call | solution.py:227
  137.5 0.8 collective-permute-start.18
  138.3 1.0 collective-permute-done.18.r_2_
  139.3 1.0 shard_map.115
  140.3 6.8 %all-to-all-done.1.kvr = bf16[16,32,256]{2,1,0:T(8,128)(2,1)S(1)} async-done(((bf16[16,32,256]{2,1,0:T(8,128)(2,1)}), bf16[16,32,256]{2,1,0:T(8,128)(2,1)S(1)}, u32[]{:S(2)}, u32[]{:S(2)}) %all-to-all-start.1) | async-done | bytes 262176 | tf_op jit(solution)/shard_map/all_to_all | solution.py:562
  147.1 1.4 shard_map.116
  (30 shorter events, 0.2 us)
Async XLA Ops:
  0.6 63.8 %collective-permute-start.1 = (bf16[16384,128]{1,0:T(8,128)(2,1)}, bf16[16384,128]{1,0:T(8,128)(2,1)}, u32[]{:S(2)}, u32[]{:S(2)}) collective-permute-start(bf16[16384,128]{1,0:T(8,128)(2,1)} %param.9), channel_id=1, source_target_pairs={{0,1},{1,0},{2,3},{3,2},{4,5},{5,4},{6,7},{7,6},{8,9},{9,8},{10,11... | collective-permute-start | bytes 12582920 | tf_op jit(solution)/shard_map/ppermute | solution.py:431
  21.2 0.9 copy-start
  22.1 0.7 copy-start.2
  22.9 5.3 %collective-permute-start = (bf16[272,128]{1,0:T(8,128)(2,1)S(1)}, bf16[272,128]{1,0:T(8,128)(2,1)S(1)}, u32[]{:S(2)}, u32[]{:S(2)}) collective-permute-start(bf16[272,128]{1,0:T(8,128)(2,1)S(1)} %get-tuple-element.96), channel_id=1, source_target_pairs={{0,1},{1,0},{2,3},{3,2},{4,5},{5,4},{6,7},{7,6},{8,9},{9,8},{10,11... | collective-permute-start | bytes 208904 | tf_op jit(solution)/shard_map/ppermute | solution.py:431
  29.4 3.9 %copy-start.4 = (bf16[16,16384]{1,0:T(8,128)(2,1)S(1)}, bf16[16,16384]{1,0:T(8,128)(2,1)}, u32[]{:S(2)}) copy-start(bf16[16,16384]{1,0:T(8,128)(2,1)} %param.10) | copy-start | bytes 1572868
  29.4 43.3 %all-to-all-start = ((bf16[8,272,256]{2,1,0:T(8,128)(2,1)}), bf16[8,272,256]{2,1,0:T(8,128)(2,1)S(1)}, u32[]{:S(2)}, u32[]{:S(2)}) async-start(bf16[8,272,256]{2,1,0:T(8,128)(2,1)} %shard_map.102), calls=%async_computation | async-start | bytes 2228224 | tf_op jit(solution)/shard_map/all_to_all | solution.py:468
  33.4 29.2 %collective-permute-start.4 = (bf16[16,16512]{1,0:T(8,128)(2,1)S(1)}, bf16[16,16512]{1,0:T(8,128)(2,1)S(1)}, u32[]{:S(2)}, u32[]{:S(2)}) collective-permute-start(bf16[16,16512]{1,0:T(8,128)(2,1)S(1)} %fusion.1), channel_id=1, source_target_pairs={{0,14},{1,30},{2,34},{3,50},{4,70},{5,86},{6,106},{7,122},{8,6},{9... | collective-permute-start | bytes 1585160 | tf_op jit(solution)/shard_map/ppermute | solution.py:459
  62.6 15.9 %collective-permute-start.5 = (bf16[16,16512]{1,0:T(8,128)(2,1)S(1)}, bf16[16,16512]{1,0:T(8,128)(2,1)S(1)}, u32[]{:S(2)}, u32[]{:S(2)}) collective-permute-start(bf16[16,16512]{1,0:T(8,128)(2,1)S(1)} %collective-permute-done.4.kv), channel_id=1, source_target_pairs={{0,1},{1,0},{2,3},{3,2},{4,5},{5,4},{6,7},{7,6},{8,9},{9,8},{10,11... | collective-permute-start | bytes 1585160 | tf_op jit(solution)/shard_map/ppermute | solution.py:431
  72.8 9.7 %collective-permute-start.2 = (bf16[1024,256]{1,0:T(8,128)(2,1)S(1)}, bf16[1024,256]{1,0:T(8,128)(2,1)S(1)}, u32[]{:S(2)}, u32[]{:S(2)}) collective-permute-start(bf16[1024,256]{1,0:T(8,128)(2,1)S(1)} %bitcast.32), channel_id=1, source_target_pairs={{0,16},{1,3},{2,18},{3,5},{4,20},{5,7},{6,22},{7,9},{8,24},{9,11},... | collective-permute-start | bytes 1572872 | tf_op jit(solution)/shard_map/ppermute | solution.py:428
  73.0 9.5 %collective-permute-start.3 = (bf16[1024,256]{1,0:T(8,128)(2,1)S(1)}, bf16[1024,256]{1,0:T(8,128)(2,1)S(1)}, u32[]{:S(2)}, u32[]{:S(2)}) collective-permute-start(bf16[1024,256]{1,0:T(8,128)(2,1)S(1)} %bitcast.33), channel_id=1, source_target_pairs={{0,112},{1,15},{2,114},{3,1},{4,116},{5,3},{6,118},{7,5},{8,120},{... | collective-permute-start | bytes 1572872 | tf_op jit(solution)/shard_map/ppermute | solution.py:428
  75.7 12.5 %collective-permute-start.8 = (bf16[1040,256]{1,0:T(8,128)(2,1)S(1)}, bf16[1040,256]{1,0:T(8,128)(2,1)S(1)}, u32[]{:S(2)}, u32[]{:S(2)}) collective-permute-start(bf16[1040,256]{1,0:T(8,128)(2,1)S(1)} %shard_map.104.refs_2_), channel_id=1, source_target_pairs={{0,16},{1,3},{2,18},{3,5},{4,20},{5,7},{6,22},{7,9},{8,24},{9,11},... | collective-permute-start | bytes 1597448 | tf_op jit(solution)/shard_map/ppermute | solution.py:428
  75.8 12.4 %collective-permute-start.9 = (bf16[1040,256]{1,0:T(8,128)(2,1)S(1)}, bf16[1040,256]{1,0:T(8,128)(2,1)S(1)}, u32[]{:S(2)}, u32[]{:S(2)}) collective-permute-start(bf16[1040,256]{1,0:T(8,128)(2,1)S(1)} %shard_map.104.refs_2_), channel_id=1, source_target_pairs={{0,112},{1,15},{2,114},{3,1},{4,116},{5,3},{6,118},{7,5},{8,120},{... | collective-permute-start | bytes 1597448 | tf_op jit(solution)/shard_map/ppermute | solution.py:428
  82.5 11.3 %collective-permute-start.6 = (bf16[1024,256]{1,0:T(8,128)(2,1)S(1)}, bf16[1024,256]{1,0:T(8,128)(2,1)S(1)}, u32[]{:S(2)}, u32[]{:S(2)}) collective-permute-start(bf16[1024,256]{1,0:T(8,128)(2,1)S(1)} %collective-permute-done.2.refs_1_), channel_id=1, source_target_pairs={{0,16},{1,3},{2,18},{3,5},{4,20},{5,7},{6,22},{7,9},{8,24},{9,11},... | collective-permute-start | bytes 1572872 | tf_op jit(solution)/shard_map/ppermute | solution.py:428
  82.5 11.3 %collective-permute-start.7 = (bf16[1024,256]{1,0:T(8,128)(2,1)S(1)}, bf16[1024,256]{1,0:T(8,128)(2,1)S(1)}, u32[]{:S(2)}, u32[]{:S(2)}) collective-permute-start(bf16[1024,256]{1,0:T(8,128)(2,1)S(1)} %collective-permute-done.3.refs_2_), channel_id=1, source_target_pairs={{0,112},{1,15},{2,114},{3,1},{4,116},{5,3},{6,118},{7,5},{8,120},{... | collective-permute-start | bytes 1572872 | tf_op jit(solution)/shard_map/ppermute | solution.py:428
  88.2 11.3 %collective-permute-start.12 = (bf16[1040,256]{1,0:T(8,128)(2,1)S(1)}, bf16[1040,256]{1,0:T(8,128)(2,1)S(1)}, u32[]{:S(2)}, u32[]{:S(2)}) collective-permute-start(bf16[1040,256]{1,0:T(8,128)(2,1)S(1)} %collective-permute-done.8.refs_1_), channel_id=1, source_target_pairs={{0,16},{1,3},{2,18},{3,5},{4,20},{5,7},{6,22},{7,9},{8,24},{9,11},... | collective-permute-start | bytes 1597448 | tf_op jit(solution)/shard_map/ppermute | solution.py:428
  88.2 11.3 %collective-permute-start.13 = (bf16[1040,256]{1,0:T(8,128)(2,1)S(1)}, bf16[1040,256]{1,0:T(8,128)(2,1)S(1)}, u32[]{:S(2)}, u32[]{:S(2)}) collective-permute-start(bf16[1040,256]{1,0:T(8,128)(2,1)S(1)} %collective-permute-done.9.refs_2_), channel_id=1, source_target_pairs={{0,112},{1,15},{2,114},{3,1},{4,116},{5,3},{6,118},{7,5},{8,120},{... | collective-permute-start | bytes 1597448 | tf_op jit(solution)/shard_map/ppermute | solution.py:428
  93.8 11.3 %collective-permute-start.10 = (bf16[1024,256]{1,0:T(8,128)(2,1)S(1)}, bf16[1024,256]{1,0:T(8,128)(2,1)S(1)}, u32[]{:S(2)}, u32[]{:S(2)}) collective-permute-start(bf16[1024,256]{1,0:T(8,128)(2,1)S(1)} %collective-permute-done.6.refs_1_), channel_id=1, source_target_pairs={{0,16},{1,3},{2,18},{3,5},{4,20},{5,7},{6,22},{7,9},{8,24},{9,11},... | collective-permute-start | bytes 1572872 | tf_op jit(solution)/shard_map/ppermute | solution.py:428
  93.8 11.3 %collective-permute-start.11 = (bf16[1024,256]{1,0:T(8,128)(2,1)S(1)}, bf16[1024,256]{1,0:T(8,128)(2,1)S(1)}, u32[]{:S(2)}, u32[]{:S(2)}) collective-permute-start(bf16[1024,256]{1,0:T(8,128)(2,1)S(1)} %collective-permute-done.7.refs_2_), channel_id=1, source_target_pairs={{0,112},{1,15},{2,114},{3,1},{4,116},{5,3},{6,118},{7,5},{8,120},{... | collective-permute-start | bytes 1572872 | tf_op jit(solution)/shard_map/ppermute | solution.py:428
  99.5 11.3 %collective-permute-start.15 = (bf16[1040,256]{1,0:T(8,128)(2,1)S(1)}, bf16[1040,256]{1,0:T(8,128)(2,1)S(1)}, u32[]{:S(2)}, u32[]{:S(2)}) collective-permute-start(bf16[1040,256]{1,0:T(8,128)(2,1)S(1)} %collective-permute-done.12.refs_1_), channel_id=1, source_target_pairs={{0,16},{1,3},{2,18},{3,5},{4,20},{5,7},{6,22},{7,9},{8,24},{9,11},... | collective-permute-start | bytes 1597448 | tf_op jit(solution)/shard_map/ppermute | solution.py:428
  99.5 11.3 %collective-permute-start.16 = (bf16[1040,256]{1,0:T(8,128)(2,1)S(1)}, bf16[1040,256]{1,0:T(8,128)(2,1)S(1)}, u32[]{:S(2)}, u32[]{:S(2)}) collective-permute-start(bf16[1040,256]{1,0:T(8,128)(2,1)S(1)} %collective-permute-done.13.refs_2_), channel_id=1, source_target_pairs={{0,112},{1,15},{2,114},{3,1},{4,116},{5,3},{6,118},{7,5},{8,120},{... | collective-permute-start | bytes 1597448 | tf_op jit(solution)/shard_map/ppermute | solution.py:428
  110.8 11.6 %collective-permute-start.17 = (bf16[1040,256]{1,0:T(8,128)(2,1)S(1)}, bf16[1040,256]{1,0:T(8,128)(2,1)S(1)}, u32[]{:S(2)}, u32[]{:S(2)}) collective-permute-start(bf16[1040,256]{1,0:T(8,128)(2,1)S(1)} %collective-permute-done.16.refs_2_), channel_id=1, source_target_pairs={{0,112},{1,15},{2,114},{3,1},{4,116},{5,3},{6,118},{7,5},{8,120},{... | collective-permute-start | bytes 1597448 | tf_op jit(solution)/shard_map/ppermute | solution.py:428
  113.2 9.2 %collective-permute-start.14 = (bf16[1024,256]{1,0:T(8,128)(2,1)S(1)}, bf16[1024,256]{1,0:T(8,128)(2,1)S(1)}, u32[]{:S(2)}, u32[]{:S(2)}) collective-permute-start(bf16[1024,256]{1,0:T(8,128)(2,1)S(1)} %collective-permute-done.10.refs_1_), channel_id=1, source_target_pairs={{0,16},{1,3},{2,18},{3,5},{4,20},{5,7},{6,22},{7,9},{8,24},{9,11},... | collective-permute-start | bytes 1572872 | tf_op jit(solution)/shard_map/ppermute | solution.py:428
  122.4 12.7 %copy-start.5 = (f32[144]{0:T(256)S(1)}, f32[144]{0:T(256)}, u32[]{:S(2)}) copy-start(f32[144]{0:T(256)} %param.11) | copy-start | bytes 1732
  124.5 22.6 %all-to-all-start.1 = ((bf16[16,32,256]{2,1,0:T(8,128)(2,1)}), bf16[16,32,256]{2,1,0:T(8,128)(2,1)S(1)}, u32[]{:S(2)}, u32[]{:S(2)}) async-start(bf16[16,32,256]{2,1,0:T(8,128)(2,1)} %get-tuple-element.180), calls=%async_computation.1 | async-start | bytes 524288 | tf_op jit(solution)/shard_map/all_to_all | solution.py:562
  135.1 4.2 %copy-start.1 = (bf16[512,128]{1,0:T(8,128)(2,1)S(1)}, bf16[512,128]{1,0:T(8,128)(2,1)}, u32[]{:S(2)}) copy-start(bf16[512,128]{1,0:T(8,128)(2,1)} %r_4_.1) | copy-start | bytes 393220
  135.1 4.2 %copy-start.3 = (f32[128]{0:T(128)S(1)}, f32[128]{0:T(128)}, u32[]{:S(2)}) copy-start(f32[128]{0:T(128)} %param.7) | copy-start | bytes 1540
  137.5 1.8 %collective-permute-start.18 = (f32[264,128]{1,0:T(8,128)S(1)}, f32[264,128]{1,0:T(8,128)S(1)}, u32[]{:S(2)}, u32[]{:S(2)}) collective-permute-start(f32[264,128]{1,0:T(8,128)S(1)} %get-tuple-element.175), channel_id=1, source_target_pairs={{0,1},{1,0},{2,3},{3,2},{4,5},{5,4},{6,7},{7,6},{8,9},{9,8},{10,11... | collective-permute-start | bytes 405512 | tf_op jit(solution)/shard_map/ppermute | solution.py:431

commit v4 on v2

--- a/solution.py
+++ b/solution.py
@@ -15,7 +15,7 @@
 rope_base = 500000.0
 
 VMEM = 24 * 2**20
-RING_VMEM = 48 * 2**20
+RING_VMEM = 24 * 2**20
 
 F32 = jnp.float32
 BF16 = jnp.bfloat16
@@ -68,51 +68,6 @@
 
 def block_at(core, i, side):
     return jnp.where(core == 0, i, (i % side) * side + i // side)
-
-
-def weights_kernel(core, wq, wo, w_all, w_buf, sems):
-    n = w_buf.shape[0]
-    side = math.isqrt(n)
-
-    def fetches(i):
-        b = block_at(core[0], i, side)
-        return (
-            pltpu.make_async_copy(wq.at[b], w_buf.at[i, 0], sems.at[0, i]),
-            pltpu.make_async_copy(wo.at[b], w_buf.at[i, 1], sems.at[1, i]),
-        )
-
-    def store(i):
-        return pltpu.make_async_copy(w_buf.at[i], w_all.at[i], sems.at[2, i])
-
-    @pl.loop(0, n)
-    def _(i):
-        for c in fetches(i):
-            c.start()
-
-    @pl.loop(0, n)
-    def _(i):
-        for c in fetches(i):
-            c.wait()
-        store(i).start()
-
-    @pl.loop(0, n)
-    def _(i):
-        store(i).wait()
-
-
-def arrange_weights(core, wq, wo):
-    n, kb, hw = wq.shape
-    hbm = pl.BlockSpec(memory_space=pltpu.HBM)
-    out = jax.ShapeDtypeStruct((n, 2, kb, hw), BF16)
-    return pl.pallas_call(
-        weights_kernel,
-        out_shape=out,
-        in_specs=[pl.BlockSpec(memory_space=pltpu.SMEM), hbm, hbm],
-        out_specs=hbm,
-        scratch_shapes=[pltpu.VMEM(out.shape, out.dtype), pltpu.SemaphoreType.DMA((3, n))],
-        compiler_params=pltpu.CompilerParams(vmem_limit_bytes=60 * 2**20),
-        cost_estimate=pl.CostEstimate(flops=10**9, bytes_accessed=2 * 10**7, transcendentals=0),
-    )(core, wq, wo)
 
 
 def kv_weights_kernel(core, kv, ko, kv_all, kvscale):
@@ -187,23 +142,46 @@
     return total
 
 
-def fetch(table, m, pairs, sems):
+def fetch(info, shifts, sems, xs, x_buf, weights=None, kv=None):
     copies = []
-    for i in range(m):
-        for j, (whole, buf) in enumerate(pairs):
-            n = buf.shape[1]
-            at = pl.ds(pl.multiple_of(table[i] * n, n), n)
-            copies.append(pltpu.make_async_copy(whole.at[at], buf.at[i], sems.at[j, i]))
+    used = iter(range(sems.shape[0]))
+
+    def add(src, dst):
+        copies.append(pltpu.make_async_copy(src, dst, sems.at[next(used)]))
+
+    for i, (x, (s, k)) in enumerate(zip(xs, shifts)):
+        add(x, x_buf.at[i, pl.ds(0, x.shape[0])])
+        if kv is not None:
+            whole, buf = kv
+            n, side = buf.shape[1], math.isqrt(whole.shape[0])
+            place = lax.rem(info[1] + (side - s % side), side)
+            add(whole.at[pl.ds(place * side + k * n, n)], buf.at[i])
+        if weights is not None:
+            wq, wo, buf = weights
+            n, side = buf.shape[1], math.isqrt(wq.shape[0])
+            place = lax.rem(info[1] + (side - s % side), side)
+            for j in range(n):
+                b = jnp.where(info[0] == 0, place * side + k * n + j, (k * n + j) * side + place)
+                add(wq.at[b], buf.at[i, j, 0])
+                add(wo.at[b], buf.at[i, j, 1])
     for c in copies:
         c.start()
     for c in copies:
         c.wait()
-
-
-def matmul_kernel(m, table, *refs):
-    xs, w_all, kv_all = refs[:m], refs[m], refs[m + 1]
-    q_in, kv_in, st_in, q_out, kv_out, st_out, w_buf, kv_buf, sems = refs[m + 2 :]
-    fetch(table, m, ((w_all, w_buf), (kv_all, kv_buf)), sems)
+    return [x_buf.at[i, pl.ds(0, x.shape[0])] for i, x in enumerate(xs)]
+
+
+def matmul_kernel(shifts, info, *refs):
+    m = len(shifts)
+    xs, wq, wo, kv_all = refs[:m], *refs[m : m + 3]
+    q_out, kv_out, st_out, x_buf, w_buf, kv_buf, sems = refs[-7:]
+    if len(refs) == m + 10:
+        q_in, kv_in, st_in = q_out, kv_out, st_out
+        for out in (q_out, kv_out, st_out):
+            out[...] = jnp.zeros_like(out)
+    else:
+        q_in, kv_in, st_in = refs[m + 3 : m + 6]
+    xs = fetch(info, shifts, sems, xs, x_buf, (wq, wo, w_buf), (kv_all, kv_buf))
     ws, kvs = [w_buf.at[i] for i in range(m)], [kv_buf.at[i] for i in range(m)]
     q_out[...] = q_sum(xs, ws, q_in)
     total, squares, largest = kv_rows(xs, kvs, kv_in, st_in)
@@ -212,51 +190,61 @@
     st_out[1:2, :] = largest
 
 
-def arrivals_call(kernel, out_shape, table, xs, weights, rest, flops, aliases=None):
+def arrivals_call(kernel, out_shape, info, xs, weights, kv, rest, flops, aliases=None):
     m = len(xs)
     n = xs[0].shape[0] // xs[0].shape[1]
+    big = [*weights, *kv]
     hbm = pl.BlockSpec(memory_space=pltpu.HBM)
     vmem = pl.BlockSpec(memory_space=pltpu.VMEM)
     smem = pl.BlockSpec(memory_space=pltpu.SMEM)
-    specs = [smem] + [vmem] * m + [hbm] * len(weights)
-    specs += [smem if a.dtype == jnp.int32 else vmem for a in rest]
+    scratch = [pltpu.VMEM((m, max(x.shape[0] for x in xs), xs[0].shape[1]), BF16)]
+    if weights:
+        scratch.append(pltpu.VMEM((m, n, 2) + weights[0].shape[1:], BF16))
+    if kv:
+        scratch.append(pltpu.VMEM((m, n) + kv[0].shape[1:], BF16))
+    count = m * (1 + len(kv) + n * len(weights))
     return pl.pallas_call(
         kernel,
         out_shape=out_shape,
-        in_specs=specs,
+        in_specs=[smem] + [hbm] * (m + len(big)) + [vmem] * len(rest),
         out_specs=tuple(vmem for _ in out_shape),
-        scratch_shapes=[pltpu.VMEM((m, n) + w.shape[1:], w.dtype) for w in weights]
-        + [pltpu.SemaphoreType.DMA((len(weights), m))],
+        scratch_shapes=scratch + [pltpu.SemaphoreType.DMA((count,))],
         input_output_aliases=aliases or {},
         compiler_params=pltpu.CompilerParams(vmem_limit_bytes=RING_VMEM),
         cost_estimate=pl.CostEstimate(flops=flops, bytes_accessed=10**6, transcendentals=0),
-    )(table, *xs, *weights, *rest)
-
-
-def matmul(table, xs, w_all, kv_all, acc):
+    )(info, *xs, *big, *rest)
+
+
+def matmul(half, info, shifts, xs, wq, wo, kv_all, acc):
     m = len(xs)
-    out_shape = tuple(jax.ShapeDtypeStruct(a.shape, a.dtype) for a in acc)
+    out_shape = (
+        jax.ShapeDtypeStruct((half, 2 * wq.shape[2]), F32),
+        jax.ShapeDtypeStruct((kv_all.shape[1], half), F32),
+        jax.ShapeDtypeStruct((8, half), F32),
+    )
     return arrivals_call(
-        lambda *refs: matmul_kernel(m, *refs),
+        lambda *refs: matmul_kernel(shifts, *refs),
         out_shape,
-        table,
+        info,
         xs,
-        (w_all, kv_all),
+        (wq, wo),
+        (kv_all,),
         acc,
         2 * m * xs[0].shape[0] * xs[0].shape[1] * 288,
-        {3 + m + i: i for i in range(3)},
-    )
-
-
-def last_kv_kernel(d, m, table, *refs):
+        {4 + m + i: i for i in range(len(acc))},
+    )
+
+
+def last_kv_kernel(d, shifts, info, *refs):
+    m = len(shifts)
     xs, kv_all = refs[:m], refs[m]
-    core, kv_in, st_in, kvscale, kcos, ksin, kvt, st_out, kv_buf, sems = refs[m + 1 :]
-    fetch(table, m, ((kv_all, kv_buf),), sems)
+    kv_in, st_in, kvscale, kcos, ksin, kvt, st_out, x_buf, kv_buf, sems = refs[m + 1 :]
+    xs = fetch(info, shifts, sems, xs, x_buf, kv=(kv_all, kv_buf))
     t, squares, largest = kv_rows(xs, [kv_buf.at[i] for i in range(m)], kv_in, st_in)
     st_out[0:1, :] = squares
     st_out[1:2, :] = largest
     t = t * (1.0 / jnp.sqrt(squares / d + norm_eps))
-    first = core[0] == 0
+    first = info[0] == 0
     mk, mv, ok, ov = t[0:8], t[8:16], t[16:24], t[24:32]
     a = jnp.concatenate([jnp.where(first, mk, ok), jnp.where(first, ok, mk)], axis=0)
     b = jnp.concatenate([jnp.where(first, mv, ov), jnp.where(first, ov, mv)], axis=0)
@@ -270,27 +258,28 @@
         kvt[s] = both
 
 
-def last_kv(d, copies, table, core, xs, kv_all, kv, st, kvscale, kcos, ksin):
-    m = len(xs)
+def last_kv(d, copies, info, shifts, xs, kv_all, kv, st, kvscale, kcos, ksin):
     out_shape = (
         jax.ShapeDtypeStruct((copies,) + kv.shape, BF16),
         jax.ShapeDtypeStruct(st.shape, F32),
     )
     return arrivals_call(
-        lambda *refs: last_kv_kernel(d, m, *refs),
+        lambda *refs: last_kv_kernel(d, shifts, *refs),
         out_shape,
-        table,
+        info,
         xs,
+        (),
         (kv_all,),
-        [core, kv, st, kvscale, kcos, ksin],
+        [kv, st, kvscale, kcos, ksin],
         10**9,
     )
 
 
-def last_q_kernel(d, m, table, *refs):
-    xs, w_all = refs[:m], refs[m]
-    q_in, st, wscale, cosine, sine, mine, msg, w_buf, sems = refs[m + 1 :]
-    fetch(table, m, ((w_all, w_buf),), sems)
+def last_q_kernel(d, shifts, info, *refs):
+    m = len(shifts)
+    xs, wq, wo = refs[:m], refs[m], refs[m + 1]
+    q_in, st, wscale, cosine, sine, mine, msg, x_buf, w_buf, sems = refs[m + 2 :]
+    xs = fetch(info, shifts, sems, xs, x_buf, weights=(wq, wo, w_buf))
     q = q_sum(xs, [w_buf.at[i] for i in range(m)], q_in)
     half = q.shape[0]
     squares, largest = st[0:1, :], st[1:2, :]
@@ -309,19 +298,19 @@
     )
 
 
-def last_q(d, table, xs, w_all, q, st, wscale, cosine, sine):
-    m = len(xs)
+def last_q(d, info, shifts, xs, wq, wo, q, st, wscale, cosine, sine):
     half = q.shape[0]
     out_shape = (
         jax.ShapeDtypeStruct((half, HD), BF16),
         jax.ShapeDtypeStruct((half + 8, HD), F32),
     )
     return arrivals_call(
-        lambda *refs: last_q_kernel(d, m, *refs),
+        lambda *refs: last_q_kernel(d, shifts, *refs),
         out_shape,
-        table,
+        info,
         xs,
-        (w_all,),
+        (wq, wo),
+        (),
         [q, st, wscale, cosine, sine],
         10**9,
     )
@@ -463,10 +452,6 @@
         gathered = lax.all_to_all(
             slots, "tp", split_axis=0, concat_axis=0, tiled=False, axis_index_groups=first_groups
         )
-        w_all = arrange_weights(
-            core1, w_query.reshape(-1, 2 * width, HD), wq_other.reshape(-1, 2 * width, HD)
-        )
-
         positions = (prefix[0] + jnp.arange(count, dtype=jnp.int32)).astype(F32)
         pos_own = lax.dynamic_slice_in_dim(positions, core * half, half)
         pos_far = lax.dynamic_slice_in_dim(positions, (1 - core) * half, half)
@@ -492,20 +477,13 @@
             jnp.cos(ang_k),
             jnp.sin(ang_k),
         )
-        zeros = (
-            jnp.zeros((half, 2 * HD), F32),
-            jnp.zeros((4 * KV_COLS_DEV, half), F32),
-            jnp.zeros((8, half), F32),
-        )
         coord = jnp.where(core == 0, y, x)
 
-        def table_of(items):
-            return jnp.stack([(coord - s) % side * 2 + k for s, k, _ in items]).astype(jnp.int32)
-
-        shifts = [(s, k) for s in range(side) for k in range(2)]
-        places = {sk: table_of([(*sk, None)]) for sk in shifts}
-        gathered, w_all, tables, zeros, places, order = lax.optimization_barrier(
-            (gathered, w_all, tables, zeros, places, order)
+        info = jnp.stack([core, coord]).astype(jnp.int32)
+        wq = w_query.reshape(-1, 2 * width, HD)
+        wo = wq_other.reshape(-1, 2 * width, HD)
+        gathered, wo, tables, info, order, qscale = lax.optimization_barrier(
+            (gathered, wo, tables, info, order, qscale)
         )
         cos_own, sin_own, cos_far, sin_far, cos_k, sin_k = tables
 
@@ -519,11 +497,12 @@
         )(gathered)
 
         def mm(acc, items):
-            table = jnp.concatenate([places[s % side, k] for s, k, _ in items])
-            return matmul(table, [v for _, _, v in items], w_all, kv_all, acc)
-
-        up = [second(low, 1), second(high, 1)]
-        down = [second(low, -1), second(high, -1)]
+            shifts = [(s, k) for s, k, _ in items]
+            return matmul(half, info, shifts, [v for _, _, v in items], wq, wo, kv_all, acc)
+
+        up, down = [second(low, 1)], [second(low, -1)]
+        up.append(second(high, 1))
+        down.append(second(high, -1))
         kv_other = swap(kv_mine)
         kv_all, kvscale = call(
             kv_weights_kernel,
@@ -531,11 +510,11 @@
                 jax.ShapeDtypeStruct((d // (2 * width), 4 * KV_COLS_DEV, 2 * width), BF16),
                 jax.ShapeDtypeStruct((4 * KV_COLS_DEV, half), F32),
             ),
-            core1,
+            info,
             kv_mine,
             kv_other,
         )
-        acc = mm(zeros, [(0, 0, low), (0, 1, high)])
+        acc = mm((), [(0, 0, low), (0, 1, high)])
         last_round = side // 2
         for r in range(1, last_round):
             for k in range(2):
@@ -550,20 +529,20 @@
                 acc = mm(acc, items)
         items = [(last_round, 0, up[0]), (-last_round, 1, down[1])]
         xs = [v for _, _, v in items]
-        table = jnp.concatenate([places[s % side, k] for s, k, _ in items])
+        shifts = [(s, k) for s, k, _ in items]
         kvt, st = last_kv(
-            d, row, table, core1, xs, kv_all, acc[1], acc[2], kvscale, cos_k, sin_k
+            d, row, info, shifts, xs, kv_all, acc[1], acc[2], kvscale, cos_k, sin_k
         )
         kvr = lax.all_to_all(
             kvt, "tp", split_axis=0, concat_axis=0, tiled=False, axis_index_groups=rows
         )
-        mine, msg = last_q(d, table, xs, w_all, acc[0], st, qscale, cos_own, sin_own)
+        mine, msg = last_q(d, info, shifts, xs, wq, wo, acc[0], st, qscale, cos_own, sin_own)
         far = swap(msg)
         out = jax.ShapeDtypeStruct((count, HD), BF16)
         queries, payload, scale = call(
             lambda *r: token_kernel(d, *r),
             (out, out, jax.ShapeDtypeStruct((count // HD, HD), F32)),
-            core1,
+            info,
             mine,
             far,
             st,

time: 149 us -> 142 us (0.953)
  waiting for transfers between devices: 51.1 us -> 42.5 us
  local copies, waits for them, and re-layouts: 2.5 us -> 6.84 us
    ppermute x14, waiting for transfers between devices: 12.5 us -> 7.21 us  [second(): return lax.ppermute(v, 'tp', pairs)]
    unnamed x12 -> x18, local copies, waits for them, and re-layouts: 1.58 us -> 5.94 us
    all_to_all x1, waiting for transfers between devices: 6.9 us -> 3.61 us  [body(): lax.all_to_all(kvt, 'tp', split_axis=0, concat_axis=0, tiled=False, axis_...]
    ppermute x14, starting transfers between devices: 18.7 us -> 16.1 us  [second(): return lax.ppermute(v, 'tp', pairs)]
    pallas_call x10 -> x9, Pallas kernels: 30 us -> 27.7 us  [arrivals_call(): pl.pallas_call(kernel, out_shape=out_shape, in_specs=[smem] + [hbm] * (m...]
  transfers between devices with their start and end apart: 21 -> 21, of which waited for: 11 -> 7; matrix products, arithmetic and copies ran while one was open for 2% -> 2% of each run, Pallas kernels for 21% -> 21%
where the time goes in v4:
time: 142 us; the launch traced here: 141 us
  starting transfers between devices  55 us (39%)
  waiting for transfers between devices  42.5 us (30%)
  Pallas kernels  32.8 us (23%)
  local copies, waits for them, and re-layouts  6.84 us (5%)
  other arithmetic  2.02 us (1%)
  between operations  1.7 us (1%)
    pallas_call x9, Pallas kernels, arrivals_call(): pl.pallas_call(kernel, out_shape=out_shape, in_specs=[smem] + [hbm] * (m...  27.7 us
    ppermute x1, waiting for transfers between devices, body(): lax.ppermute(jnp.concatenate([w_kv, scales], axis=1), 'tp', to_row)  26.9 us
    ppermute x4, starting transfers between devices, swap(): return lax.ppermute(v, 'tp', to_partner)  23.2 us
    ppermute x14, starting transfers between devices, second(): return lax.ppermute(v, 'tp', pairs)  16.1 us
    all_to_all x1, starting transfers between devices, body(): lax.all_to_all(kvt, 'tp', split_axis=0, concat_axis=0, tiled=False, axis_...  11.7 us
    ppermute x14, waiting for transfers between devices, second(): return lax.ppermute(v, 'tp', pairs)  7.21 us
    unnamed x18, local copies, waits for them, and re-layouts  5.94 us
    pallas_call x5, Pallas kernels, call(): pl.pallas_call(kernel, out_shape=out_shape, in_specs=[pl.BlockSpec(memory...  5.01 us
  transfers between devices with their start and end apart: 21, of which 7 were waited for; matrix products, arithmetic and copies ran while one was open for 2% of the time, Pallas kernels for 21%

profile of v4, /device:TPU:513, one launch (start us, length us, event | category | flops | bytes accessed | tf_op | source)
XLA Modules:
  0.0 140.9 jit_solution(12770413541726790417)
XLA Ops:
  0.6 20.5 %collective-permute-start.1 = (bf16[16384,128]{1,0:T(8,128)(2,1)}, bf16[16384,128]{1,0:T(8,128)(2,1)}, u32[]{:S(2)}, u32[]{:S(2)}) collective-permute-start(bf16[16384,128]{1,0:T(8,128)(2,1)} %param.9), channel_id=1, source_target_pairs={{0,1},{1,0},{2,3},{3,2},{4,5},{5,4},{6,7},{7,6},{8,9},{9,8},{10,11... | collective-permute-start | bytes 12582920 | tf_op jit(solution)/shard_map/ppermute | solution.py:415
  21.2 0.9 copy-done.3
  22.1 0.7 copy-done.5
  22.7 0.2 shard_map.101
  22.9 0.2 collective-permute-start
  23.1 0.7 convert_bitcast_fusion.2
  23.8 0.7 convert_bitcast_fusion.1
  24.5 0.1 copy.32
  24.6 3.7 %collective-permute-done.recv = bf16[272,128]{1,0:T(8,128)(2,1)S(1)} collective-permute-done((bf16[272,128]{1,0:T(8,128)(2,1)S(1)}, bf16[272,128]{1,0:T(8,128)(2,1)S(1)}, u32[]{:S(2)}, u32[]{:S(2)}) %collective-permute-start) | collective-permute-done | bytes 69664 | tf_op jit(solution)/shard_map/ppermute | solution.py:415
  28.3 1.2 shard_map.102
  29.5 3.9 %all-to-all-start = ((bf16[8,272,256]{2,1,0:T(8,128)(2,1)}), bf16[8,272,256]{2,1,0:T(8,128)(2,1)S(1)}, u32[]{:S(2)}, u32[]{:S(2)}) async-start(bf16[8,272,256]{2,1,0:T(8,128)(2,1)} %shard_map.102), calls=%async_computation | async-start | bytes 2228224 | tf_op jit(solution)/shard_map/all_to_all | solution.py:452
  33.4 0.0 copy-start.8
  33.4 0.1 collective-permute-start.4
  34.4 0.1 fusion.17
  34.5 0.1 multiply_sine_fusion.2
  34.7 1.0 multiply_sine_fusion
  35.7 26.9 %collective-permute-done.4.kv = bf16[16,16512]{1,0:T(8,128)(2,1)S(1)} collective-permute-done((bf16[16,16512]{1,0:T(8,128)(2,1)S(1)}, bf16[16,16512]{1,0:T(8,128)(2,1)S(1)}, u32[]{:S(2)}, u32[]{:S(2)}) %collective-permute-start.4) | collective-permute-done | bytes 528416 | tf_op jit(solution)/shard_map/ppermute | solution.py:443
  62.6 1.7 %collective-permute-start.5 = (bf16[16,16512]{1,0:T(8,128)(2,1)S(1)}, bf16[16,16512]{1,0:T(8,128)(2,1)S(1)}, u32[]{:S(2)}, u32[]{:S(2)}) collective-permute-start(bf16[16,16512]{1,0:T(8,128)(2,1)S(1)} %collective-permute-done.4.kv), channel_id=1, source_target_pairs={{0,1},{1,0},{2,3},{3,2},{4,5},{5,4},{6,7},{7,6},{8,9},{9,8},{10,11... | collective-permute-start | bytes 1585160 | tf_op jit(solution)/shard_map/ppermute | solution.py:415
  64.3 0.1 pad_add_fusion.core.refs_0_.r_0_
  64.4 0.0 all-to-all-done.gathered
  64.4 0.0 collective-permute-done.1
  64.5 0.1 collective-permute-start.3
  64.6 1.4 %collective-permute-start.2 = (bf16[1024,256]{1,0:T(8,128)(2,1)S(1)}, bf16[1024,256]{1,0:T(8,128)(2,1)S(1)}, u32[]{:S(2)}, u32[]{:S(2)}) collective-permute-start(bf16[1024,256]{1,0:T(8,128)(2,1)S(1)} %bitcast.26), channel_id=1, source_target_pairs={{0,16},{1,3},{2,18},{3,5},{4,20},{5,7},{6,22},{7,9},{8,24},{9,11},... | collective-permute-start | bytes 1572872 | tf_op jit(solution)/shard_map/ppermute | solution.py:412
  66.0 0.1 shard_map.103.refs_2_
  66.1 1.5 %collective-permute-start.9 = (bf16[1040,256]{1,0:T(8,128)(2,1)S(1)}, bf16[1040,256]{1,0:T(8,128)(2,1)S(1)}, u32[]{:S(2)}, u32[]{:S(2)}) collective-permute-start(bf16[1040,256]{1,0:T(8,128)(2,1)S(1)} %shard_map.103.refs_2_), channel_id=1, source_target_pairs={{0,112},{1,15},{2,114},{3,1},{4,116},{5,3},{6,118},{7,5},{8,120},{... | collective-permute-start | bytes 1597448 | tf_op jit(solution)/shard_map/ppermute | solution.py:412
  67.6 0.1 collective-permute-start.8
  67.7 0.0 collective-permute-done.5.ko
  67.7 0.7 shard_map.104
  68.4 0.0 copy-start
  68.4 2.2 %copy-done = bf16[16384,128]{1,0:T(8,128)(2,1)S(1)} copy-done((bf16[16384,128]{1,0:T(8,128)(2,1)S(1)}, bf16[16384,128]{1,0:T(8,128)(2,1)}, u32[]{:S(2)}) %copy-start) | copy-done | bytes 4194328
  70.6 3.3 %shard_map.105 = (f32[256,256]{1,0:T(8,128)S(1)}, f32[32,256]{1,0:T(8,128)S(1)}, f32[8,256]{1,0:T(8,128)S(1)}) custom-call(s32[2]{0:T(128)S(1)} %pad_add_fusion.core.refs_0_.r_0_, bf16[1024,256]{1,0:T(8,128)(2,1)S(1)} %bitcast.27, bf16[1040,256]{1,0:T(8,128)(2,1)S(1)} %shard_map.103.refs_2_, bf16[64,256,128]{2,1,0:T(8,128)(2,1)S(1)} %bitcast.17, ...), custom_call_target="tpu_custom_call" | custom-call | flops 301989888 | bytes 1000000 | tf_op jit(solution)/shard_map/pallas_call | solution.py:206
  73.9 0.4 collective-permute-done.2.refs_1_
  74.3 0.1 collective-permute-start.6
  74.4 2.6 %collective-permute-start.7 = (bf16[1024,256]{1,0:T(8,128)(2,1)S(1)}, bf16[1024,256]{1,0:T(8,128)(2,1)S(1)}, u32[]{:S(2)}, u32[]{:S(2)}) collective-permute-start(bf16[1024,256]{1,0:T(8,128)(2,1)S(1)} %collective-permute-done.3.refs_2_), channel_id=1, source_target_pairs={{0,112},{1,15},{2,114},{3,1},{4,116},{5,3},{6,118},{7,5},{8,120},{... | collective-permute-start | bytes 1572872 | tf_op jit(solution)/shard_map/ppermute | solution.py:412
  76.9 3.3 %shard_map.106 = (f32[256,256]{1,0:T(8,128)S(1)}, f32[32,256]{1,0:T(8,128)S(1)}, f32[8,256]{1,0:T(8,128)S(1)}) custom-call(s32[2]{0:T(128)S(1)} %pad_add_fusion.core.refs_0_.r_0_, bf16[1024,256]{1,0:T(8,128)(2,1)S(1)} %collective-permute-done.2.refs_1_, ...), custom_call_target="tpu_custom_call", output_to_operand_aliasing={{0}: (6, {}), {1}: (7, {}), {2}: (8, {})} | custom-call | flops 301989888 | bytes 1000000 | tf_op jit(solution)/shard_map/pallas_call | solution.py:206
  80.2 0.0 collective-permute-done.9.refs_2_
  80.2 0.1 collective-permute-start.12
  80.4 2.7 %collective-permute-start.13 = (bf16[1040,256]{1,0:T(8,128)(2,1)S(1)}, bf16[1040,256]{1,0:T(8,128)(2,1)S(1)}, u32[]{:S(2)}, u32[]{:S(2)}) collective-permute-start(bf16[1040,256]{1,0:T(8,128)(2,1)S(1)} %collective-permute-done.9.refs_2_), channel_id=1, source_target_pairs={{0,112},{1,15},{2,114},{3,1},{4,116},{5,3},{6,118},{7,5},{8,120},{... | collective-permute-start | bytes 1597448 | tf_op jit(solution)/shard_map/ppermute | solution.py:412
  83.0 3.3 %shard_map.107 = (f32[256,256]{1,0:T(8,128)S(1)}, f32[32,256]{1,0:T(8,128)S(1)}, f32[8,256]{1,0:T(8,128)S(1)}) custom-call(s32[2]{0:T(128)S(1)} %pad_add_fusion.core.refs_0_.r_0_, bf16[1040,256]{1,0:T(8,128)(2,1)S(1)} %collective-permute-done.8.refs_1_, ...), custom_call_target="tpu_custom_call", output_to_operand_aliasing={{0}: (6, {}), {1}: (7, {}), {2}: (8, {})} | custom-call | flops 306708480 | bytes 1000000 | tf_op jit(solution)/shard_map/pallas_call | solution.py:206
  86.3 0.0 collective-permute-done.6.refs_1_
  86.3 0.1 collective-permute-start.10
  86.5 2.6 %collective-permute-start.11 = (bf16[1024,256]{1,0:T(8,128)(2,1)S(1)}, bf16[1024,256]{1,0:T(8,128)(2,1)S(1)}, u32[]{:S(2)}, u32[]{:S(2)}) collective-permute-start(bf16[1024,256]{1,0:T(8,128)(2,1)S(1)} %collective-permute-done.7.refs_2_), channel_id=1, source_target_pairs={{0,112},{1,15},{2,114},{3,1},{4,116},{5,3},{6,118},{7,5},{8,120},{... | collective-permute-start | bytes 1572872 | tf_op jit(solution)/shard_map/ppermute | solution.py:412
  89.1 3.3 %shard_map.108 = (f32[256,256]{1,0:T(8,128)S(1)}, f32[32,256]{1,0:T(8,128)S(1)}, f32[8,256]{1,0:T(8,128)S(1)}) custom-call(s32[2]{0:T(128)S(1)} %pad_add_fusion.core.refs_0_.r_0_, bf16[1024,256]{1,0:T(8,128)(2,1)S(1)} %collective-permute-done.6.refs_1_, ...), custom_call_target="tpu_custom_call", output_to_operand_aliasing={{0}: (6, {}), {1}: (7, {}), {2}: (8, {})} | custom-call | flops 301989888 | bytes 1000000 | tf_op jit(solution)/shard_map/pallas_call | solution.py:206
  92.4 0.0 collective-permute-done.13.refs_2_
  92.4 0.1 collective-permute-start.15
  92.5 2.6 %collective-permute-start.16 = (bf16[1040,256]{1,0:T(8,128)(2,1)S(1)}, bf16[1040,256]{1,0:T(8,128)(2,1)S(1)}, u32[]{:S(2)}, u32[]{:S(2)}) collective-permute-start(bf16[1040,256]{1,0:T(8,128)(2,1)S(1)} %collective-permute-done.13.refs_2_), channel_id=1, source_target_pairs={{0,112},{1,15},{2,114},{3,1},{4,116},{5,3},{6,118},{7,5},{8,120},{... | collective-permute-start | bytes 1597448 | tf_op jit(solution)/shard_map/ppermute | solution.py:412
  95.2 3.3 %shard_map.109 = (f32[256,256]{1,0:T(8,128)S(1)}, f32[32,256]{1,0:T(8,128)S(1)}, f32[8,256]{1,0:T(8,128)S(1)}) custom-call(s32[2]{0:T(128)S(1)} %pad_add_fusion.core.refs_0_.r_0_, bf16[1040,256]{1,0:T(8,128)(2,1)S(1)} %collective-permute-done.12.refs_1_, ...), custom_call_target="tpu_custom_call", output_to_operand_aliasing={{0}: (6, {}), {1}: (7, {}), {2}: (8, {})} | custom-call | flops 306708480 | bytes 1000000 | tf_op jit(solution)/shard_map/pallas_call | solution.py:206
  98.5 0.0 collective-permute-done.10.refs_1_
  98.5 3.3 %shard_map.110 = (f32[256,256]{1,0:T(8,128)S(1)}, f32[32,256]{1,0:T(8,128)S(1)}, f32[8,256]{1,0:T(8,128)S(1)}) custom-call(s32[2]{0:T(128)S(1)} %pad_add_fusion.core.refs_0_.r_0_, bf16[1024,256]{1,0:T(8,128)(2,1)S(1)} %collective-permute-done.10.refs_1_, ...), custom_call_target="tpu_custom_call", output_to_operand_aliasing={{0}: (6, {}), {1}: (7, {}), {2}: (8, {})} | custom-call | flops 301989888 | bytes 1000000 | tf_op jit(solution)/shard_map/pallas_call | solution.py:206
  101.8 0.8 collective-permute-done.15.refs_1_
  102.6 0.0 collective-permute-done.16.refs_2_
  102.6 1.9 %collective-permute-start.17 = (bf16[1040,256]{1,0:T(8,128)(2,1)S(1)}, bf16[1040,256]{1,0:T(8,128)(2,1)S(1)}, u32[]{:S(2)}, u32[]{:S(2)}) collective-permute-start(bf16[1040,256]{1,0:T(8,128)(2,1)S(1)} %collective-permute-done.16.refs_2_), channel_id=1, source_target_pairs={{0,112},{1,15},{2,114},{3,1},{4,116},{5,3},{6,118},{7,5},{8,120},{... | collective-permute-start | bytes 1597448 | tf_op jit(solution)/shard_map/ppermute | solution.py:412
  104.5 0.0 collective-permute-start.14
  104.5 3.3 %shard_map.111 = (f32[256,256]{1,0:T(8,128)S(1)}, f32[32,256]{1,0:T(8,128)S(1)}, f32[8,256]{1,0:T(8,128)S(1)}) custom-call(s32[2]{0:T(128)S(1)} %pad_add_fusion.core.refs_0_.r_0_, bf16[1040,256]{1,0:T(8,128)(2,1)S(1)} %collective-permute-done.15.refs_1_, ...), custom_call_target="tpu_custom_call", output_to_operand_aliasing={{0}: (6, {}), {1}: (7, {}), {2}: (8, {})} | custom-call | flops 306708480 | bytes 1000000 | tf_op jit(solution)/shard_map/pallas_call | solution.py:206
  107.8 6.0 %collective-permute-done.14.refs_1_ = bf16[1024,256]{1,0:T(8,128)(2,1)S(1)} collective-permute-done((bf16[1024,256]{1,0:T(8,128)(2,1)S(1)}, bf16[1024,256]{1,0:T(8,128)(2,1)S(1)}, u32[]{:S(2)}, u32[]{:S(2)}) %collective-permute-start.14) | collective-permute-done | bytes 524320 | tf_op jit(solution)/shard_map/ppermute | solution.py:412
  113.8 2.0 %shard_map.112 = (bf16[16,32,256]{2,1,0:T(8,128)(2,1)}, f32[8,256]{1,0:T(8,128)S(1)}) custom-call(s32[2]{0:T(128)S(1)} %pad_add_fusion.core.refs_0_.r_0_, bf16[1024,256]{1,0:T(8,128)(2,1)S(1)} %collective-permute-done.14.refs_1_, bf16[1040,256]{1,0:T(8,128)(2,1)S(1)} %collective-permute-done.17.refs_2_, ...), custom_call_target="tpu_custom_call" | custom-call | flops 1000000000 | bytes 1000000 | tf_op jit(solution)/shard_map/pallas_call | solution.py:206
  115.8 11.7 %all-to-all-start.1 = ((bf16[16,32,256]{2,1,0:T(8,128)(2,1)}), bf16[16,32,256]{2,1,0:T(8,128)(2,1)S(1)}, u32[]{:S(2)}, u32[]{:S(2)}) async-start(bf16[16,32,256]{2,1,0:T(8,128)(2,1)} %get-tuple-element.146), calls=%async_computation.1 | async-start | bytes 524288 | tf_op jit(solution)/shard_map/all_to_all | solution.py:536
  127.5 2.2 %copy-done.2 = bf16[16384,128]{1,0:T(8,128)(2,1)S(1)} copy-done((bf16[16384,128]{1,0:T(8,128)(2,1)S(1)}, bf16[16384,128]{1,0:T(8,128)(2,1)}, u32[]{:S(2)}) %copy-start.2) | copy-done | bytes 4194328
  129.7 2.9 %shard_map.113 = (bf16[256,128]{1,0:T(8,128)(2,1)S(1)}, f32[264,128]{1,0:T(8,128)S(1)}) custom-call(s32[2]{0:T(128)S(1)} %pad_add_fusion.core.refs_0_.r_0_, bf16[1024,256]{1,0:T(8,128)(2,1)S(1)} %collective-permute-done.14.refs_1_, bf16[1040,256]{1,0:T(8,128)(2,1)S(1)} %collective-permute-done.17.refs_2_, bf16[64,256,128]{2,1,0:T(8,128)(2,1)S(1)} %bitcast.24, ...), custom_call_target="tpu_custom_call" | custom-call | flops 1000000000 | bytes 1000000 | tf_op jit(solution)/shard_map/pallas_call | solution.py:206
  132.6 0.8 collective-permute-start.18
  133.4 1.0 collective-permute-done.18.r_2_
  134.4 1.5 %shard_map.114 = (bf16[512,128]{1,0:T(8,128)(2,1)}, bf16[512,128]{1,0:T(8,128)(2,1)}, f32[4,128]{1,0:T(4,128)}) custom-call(s32[2]{0:T(128)S(1)} %pad_add_fusion.core.refs_0_.r_0_, bf16[256,128]{1,0:T(8,128)(2,1)S(1)} %get-tuple-element.140.r_1_, f32[264,128]{1,0:T(8,128)S(1)} %collective-permute-done.18.r_2_, f32[8,256]{1,0:T(8,128)S(1)} %get-tuple-element.136.refs_6_.r_3_, ...), custom_call_target="tpu_custom_call" | custom-call | flops 100000000 | bytes 1000000 | tf_op jit(solution)/shard_map/pallas_call | solution.py:374
  135.9 3.6 %all-to-all-done.1.kvr = bf16[16,32,256]{2,1,0:T(8,128)(2,1)S(1)} async-done(((bf16[16,32,256]{2,1,0:T(8,128)(2,1)}), bf16[16,32,256]{2,1,0:T(8,128)(2,1)S(1)}, u32[]{:S(2)}, u32[]{:S(2)}) %all-to-all-start.1) | async-done | bytes 262176 | tf_op jit(solution)/shard_map/all_to_all | solution.py:536
  139.5 1.4 shard_map.115
  (26 shorter events, 0.2 us)
Async XLA Ops:
  0.6 63.8 %collective-permute-start.1 = (bf16[16384,128]{1,0:T(8,128)(2,1)}, bf16[16384,128]{1,0:T(8,128)(2,1)}, u32[]{:S(2)}, u32[]{:S(2)}) collective-permute-start(bf16[16384,128]{1,0:T(8,128)(2,1)} %param.9), channel_id=1, source_target_pairs={{0,1},{1,0},{2,3},{3,2},{4,5},{5,4},{6,7},{7,6},{8,9},{9,8},{10,11... | collective-permute-start | bytes 12582920 | tf_op jit(solution)/shard_map/ppermute | solution.py:415
  21.2 0.9 copy-start.3
  22.1 0.7 copy-start.5
  22.9 5.3 %collective-permute-start = (bf16[272,128]{1,0:T(8,128)(2,1)S(1)}, bf16[272,128]{1,0:T(8,128)(2,1)S(1)}, u32[]{:S(2)}, u32[]{:S(2)}) collective-permute-start(bf16[272,128]{1,0:T(8,128)(2,1)S(1)} %get-tuple-element.79), channel_id=1, source_target_pairs={{0,1},{1,0},{2,3},{3,2},{4,5},{5,4},{6,7},{7,6},{8,9},{9,8},{10,11... | collective-permute-start | bytes 208904 | tf_op jit(solution)/shard_map/ppermute | solution.py:415
  29.5 3.9 %copy-start.7 = (bf16[16,16384]{1,0:T(8,128)(2,1)S(1)}, bf16[16,16384]{1,0:T(8,128)(2,1)}, u32[]{:S(2)}) copy-start(bf16[16,16384]{1,0:T(8,128)(2,1)} %param.10) | copy-start | bytes 1572868
  29.5 35.0 %all-to-all-start = ((bf16[8,272,256]{2,1,0:T(8,128)(2,1)}), bf16[8,272,256]{2,1,0:T(8,128)(2,1)S(1)}, u32[]{:S(2)}, u32[]{:S(2)}) async-start(bf16[8,272,256]{2,1,0:T(8,128)(2,1)} %shard_map.102), calls=%async_computation | async-start | bytes 2228224 | tf_op jit(solution)/shard_map/all_to_all | solution.py:452
  33.4 1.1 copy-start.8
  33.4 29.2 %collective-permute-start.4 = (bf16[16,16512]{1,0:T(8,128)(2,1)S(1)}, bf16[16,16512]{1,0:T(8,128)(2,1)S(1)}, u32[]{:S(2)}, u32[]{:S(2)}) collective-permute-start(bf16[16,16512]{1,0:T(8,128)(2,1)S(1)} %fusion.1), channel_id=1, source_target_pairs={{0,14},{1,30},{2,34},{3,50},{4,70},{5,86},{6,106},{7,122},{8,6},{9... | collective-permute-start | bytes 1585160 | tf_op jit(solution)/shard_map/ppermute | solution.py:443
  62.6 5.1 %collective-permute-start.5 = (bf16[16,16512]{1,0:T(8,128)(2,1)S(1)}, bf16[16,16512]{1,0:T(8,128)(2,1)S(1)}, u32[]{:S(2)}, u32[]{:S(2)}) collective-permute-start(bf16[16,16512]{1,0:T(8,128)(2,1)S(1)} %collective-permute-done.4.kv), channel_id=1, source_target_pairs={{0,1},{1,0},{2,3},{3,2},{4,5},{5,4},{6,7},{7,6},{8,9},{9,8},{10,11... | collective-permute-start | bytes 1585160 | tf_op jit(solution)/shard_map/ppermute | solution.py:415
  64.5 9.4 %collective-permute-start.3 = (bf16[1024,256]{1,0:T(8,128)(2,1)S(1)}, bf16[1024,256]{1,0:T(8,128)(2,1)S(1)}, u32[]{:S(2)}, u32[]{:S(2)}) collective-permute-start(bf16[1024,256]{1,0:T(8,128)(2,1)S(1)} %bitcast.25), channel_id=1, source_target_pairs={{0,112},{1,15},{2,114},{3,1},{4,116},{5,3},{6,118},{7,5},{8,120},{... | collective-permute-start | bytes 1572872 | tf_op jit(solution)/shard_map/ppermute | solution.py:412
  64.6 9.7 %collective-permute-start.2 = (bf16[1024,256]{1,0:T(8,128)(2,1)S(1)}, bf16[1024,256]{1,0:T(8,128)(2,1)S(1)}, u32[]{:S(2)}, u32[]{:S(2)}) collective-permute-start(bf16[1024,256]{1,0:T(8,128)(2,1)S(1)} %bitcast.26), channel_id=1, source_target_pairs={{0,16},{1,3},{2,18},{3,5},{4,20},{5,7},{6,22},{7,9},{8,24},{9,11},... | collective-permute-start | bytes 1572872 | tf_op jit(solution)/shard_map/ppermute | solution.py:412
  66.1 14.1 %collective-permute-start.9 = (bf16[1040,256]{1,0:T(8,128)(2,1)S(1)}, bf16[1040,256]{1,0:T(8,128)(2,1)S(1)}, u32[]{:S(2)}, u32[]{:S(2)}) collective-permute-start(bf16[1040,256]{1,0:T(8,128)(2,1)S(1)} %shard_map.103.refs_2_), channel_id=1, source_target_pairs={{0,112},{1,15},{2,114},{3,1},{4,116},{5,3},{6,118},{7,5},{8,120},{... | collective-permute-start | bytes 1597448 | tf_op jit(solution)/shard_map/ppermute | solution.py:412
  67.6 12.6 %collective-permute-start.8 = (bf16[1040,256]{1,0:T(8,128)(2,1)S(1)}, bf16[1040,256]{1,0:T(8,128)(2,1)S(1)}, u32[]{:S(2)}, u32[]{:S(2)}) collective-permute-start(bf16[1040,256]{1,0:T(8,128)(2,1)S(1)} %shard_map.103.refs_2_), channel_id=1, source_target_pairs={{0,16},{1,3},{2,18},{3,5},{4,20},{5,7},{6,22},{7,9},{8,24},{9,11},... | collective-permute-start | bytes 1597448 | tf_op jit(solution)/shard_map/ppermute | solution.py:412
  68.4 2.2 %copy-start = (bf16[16384,128]{1,0:T(8,128)(2,1)S(1)}, bf16[16384,128]{1,0:T(8,128)(2,1)}, u32[]{:S(2)}) copy-start(bf16[16384,128]{1,0:T(8,128)(2,1)} %param.9) | copy-start | bytes 12582916
  70.6 6.3 %copy-start.1 = (bf16[16384,128]{1,0:T(8,128)(2,1)S(1)}, bf16[16384,128]{1,0:T(8,128)(2,1)}, u32[]{:S(2)}) copy-start(bf16[16384,128]{1,0:T(8,128)(2,1)} %param.9) | copy-start | bytes 12582916
  74.3 12.0 %collective-permute-start.6 = (bf16[1024,256]{1,0:T(8,128)(2,1)S(1)}, bf16[1024,256]{1,0:T(8,128)(2,1)S(1)}, u32[]{:S(2)}, u32[]{:S(2)}) collective-permute-start(bf16[1024,256]{1,0:T(8,128)(2,1)S(1)} %collective-permute-done.2.refs_1_), channel_id=1, source_target_pairs={{0,16},{1,3},{2,18},{3,5},{4,20},{5,7},{6,22},{7,9},{8,24},{9,11},... | collective-permute-start | bytes 1572872 | tf_op jit(solution)/shard_map/ppermute | solution.py:412
  74.4 11.9 %collective-permute-start.7 = (bf16[1024,256]{1,0:T(8,128)(2,1)S(1)}, bf16[1024,256]{1,0:T(8,128)(2,1)S(1)}, u32[]{:S(2)}, u32[]{:S(2)}) collective-permute-start(bf16[1024,256]{1,0:T(8,128)(2,1)S(1)} %collective-permute-done.3.refs_2_), channel_id=1, source_target_pairs={{0,112},{1,15},{2,114},{3,1},{4,116},{5,3},{6,118},{7,5},{8,120},{... | collective-permute-start | bytes 1572872 | tf_op jit(solution)/shard_map/ppermute | solution.py:412
  80.2 12.2 %collective-permute-start.12 = (bf16[1040,256]{1,0:T(8,128)(2,1)S(1)}, bf16[1040,256]{1,0:T(8,128)(2,1)S(1)}, u32[]{:S(2)}, u32[]{:S(2)}) collective-permute-start(bf16[1040,256]{1,0:T(8,128)(2,1)S(1)} %collective-permute-done.8.refs_1_), channel_id=1, source_target_pairs={{0,16},{1,3},{2,18},{3,5},{4,20},{5,7},{6,22},{7,9},{8,24},{9,11},... | collective-permute-start | bytes 1597448 | tf_op jit(solution)/shard_map/ppermute | solution.py:412
  80.4 12.0 %collective-permute-start.13 = (bf16[1040,256]{1,0:T(8,128)(2,1)S(1)}, bf16[1040,256]{1,0:T(8,128)(2,1)S(1)}, u32[]{:S(2)}, u32[]{:S(2)}) collective-permute-start(bf16[1040,256]{1,0:T(8,128)(2,1)S(1)} %collective-permute-done.9.refs_2_), channel_id=1, source_target_pairs={{0,112},{1,15},{2,114},{3,1},{4,116},{5,3},{6,118},{7,5},{8,120},{... | collective-permute-start | bytes 1597448 | tf_op jit(solution)/shard_map/ppermute | solution.py:412
  86.3 12.2 %collective-permute-start.10 = (bf16[1024,256]{1,0:T(8,128)(2,1)S(1)}, bf16[1024,256]{1,0:T(8,128)(2,1)S(1)}, u32[]{:S(2)}, u32[]{:S(2)}) collective-permute-start(bf16[1024,256]{1,0:T(8,128)(2,1)S(1)} %collective-permute-done.6.refs_1_), channel_id=1, source_target_pairs={{0,16},{1,3},{2,18},{3,5},{4,20},{5,7},{6,22},{7,9},{8,24},{9,11},... | collective-permute-start | bytes 1572872 | tf_op jit(solution)/shard_map/ppermute | solution.py:412
  86.5 12.0 %collective-permute-start.11 = (bf16[1024,256]{1,0:T(8,128)(2,1)S(1)}, bf16[1024,256]{1,0:T(8,128)(2,1)S(1)}, u32[]{:S(2)}, u32[]{:S(2)}) collective-permute-start(bf16[1024,256]{1,0:T(8,128)(2,1)S(1)} %collective-permute-done.7.refs_2_), channel_id=1, source_target_pairs={{0,112},{1,15},{2,114},{3,1},{4,116},{5,3},{6,118},{7,5},{8,120},{... | collective-permute-start | bytes 1572872 | tf_op jit(solution)/shard_map/ppermute | solution.py:412
  92.4 10.2 %collective-permute-start.15 = (bf16[1040,256]{1,0:T(8,128)(2,1)S(1)}, bf16[1040,256]{1,0:T(8,128)(2,1)S(1)}, u32[]{:S(2)}, u32[]{:S(2)}) collective-permute-start(bf16[1040,256]{1,0:T(8,128)(2,1)S(1)} %collective-permute-done.12.refs_1_), channel_id=1, source_target_pairs={{0,16},{1,3},{2,18},{3,5},{4,20},{5,7},{6,22},{7,9},{8,24},{9,11},... | collective-permute-start | bytes 1597448 | tf_op jit(solution)/shard_map/ppermute | solution.py:412
  92.5 10.1 %collective-permute-start.16 = (bf16[1040,256]{1,0:T(8,128)(2,1)S(1)}, bf16[1040,256]{1,0:T(8,128)(2,1)S(1)}, u32[]{:S(2)}, u32[]{:S(2)}) collective-permute-start(bf16[1040,256]{1,0:T(8,128)(2,1)S(1)} %collective-permute-done.13.refs_2_), channel_id=1, source_target_pairs={{0,112},{1,15},{2,114},{3,1},{4,116},{5,3},{6,118},{7,5},{8,120},{... | collective-permute-start | bytes 1597448 | tf_op jit(solution)/shard_map/ppermute | solution.py:412
  102.6 11.1 %collective-permute-start.17 = (bf16[1040,256]{1,0:T(8,128)(2,1)S(1)}, bf16[1040,256]{1,0:T(8,128)(2,1)S(1)}, u32[]{:S(2)}, u32[]{:S(2)}) collective-permute-start(bf16[1040,256]{1,0:T(8,128)(2,1)S(1)} %collective-permute-done.16.refs_2_), channel_id=1, source_target_pairs={{0,112},{1,15},{2,114},{3,1},{4,116},{5,3},{6,118},{7,5},{8,120},{... | collective-permute-start | bytes 1597448 | tf_op jit(solution)/shard_map/ppermute | solution.py:412
  104.5 9.2 %collective-permute-start.14 = (bf16[1024,256]{1,0:T(8,128)(2,1)S(1)}, bf16[1024,256]{1,0:T(8,128)(2,1)S(1)}, u32[]{:S(2)}, u32[]{:S(2)}) collective-permute-start(bf16[1024,256]{1,0:T(8,128)(2,1)S(1)} %collective-permute-done.10.refs_1_), channel_id=1, source_target_pairs={{0,16},{1,3},{2,18},{3,5},{4,20},{5,7},{6,22},{7,9},{8,24},{9,11},... | collective-permute-start | bytes 1572872 | tf_op jit(solution)/shard_map/ppermute | solution.py:412
  115.8 23.7 %all-to-all-start.1 = ((bf16[16,32,256]{2,1,0:T(8,128)(2,1)}), bf16[16,32,256]{2,1,0:T(8,128)(2,1)S(1)}, u32[]{:S(2)}, u32[]{:S(2)}) async-start(bf16[16,32,256]{2,1,0:T(8,128)(2,1)} %get-tuple-element.146), calls=%async_computation.1 | async-start | bytes 524288 | tf_op jit(solution)/shard_map/all_to_all | solution.py:536
  127.5 2.2 %copy-start.2 = (bf16[16384,128]{1,0:T(8,128)(2,1)S(1)}, bf16[16384,128]{1,0:T(8,128)(2,1)}, u32[]{:S(2)}) copy-start(bf16[16384,128]{1,0:T(8,128)(2,1)} %param.9) | copy-start | bytes 12582916
  129.7 4.7 %copy-start.4 = (bf16[512,128]{1,0:T(8,128)(2,1)S(1)}, bf16[512,128]{1,0:T(8,128)(2,1)}, u32[]{:S(2)}) copy-start(bf16[512,128]{1,0:T(8,128)(2,1)} %r_4_.1) | copy-start | bytes 393220
  129.7 4.7 %copy-start.6 = (f32[128]{0:T(128)S(1)}, f32[128]{0:T(128)}, u32[]{:S(2)}) copy-start(f32[128]{0:T(128)} %param.7) | copy-start | bytes 1540
  132.6 1.8 %collective-permute-start.18 = (f32[264,128]{1,0:T(8,128)S(1)}, f32[264,128]{1,0:T(8,128)S(1)}, u32[]{:S(2)}, u32[]{:S(2)}) collective-permute-start(f32[264,128]{1,0:T(8,128)S(1)} %get-tuple-element.141), channel_id=1, source_target_pairs={{0,1},{1,0},{2,3},{3,2},{4,5},{5,4},{6,7},{7,6},{8,9},{9,8},{10,11... | collective-permute-start | bytes 405512 | tf_op jit(solution)/shard_map/ppermute | solution.py:415

commit v5 on v4

--- a/solution.py
+++ b/solution.py
@@ -15,7 +15,7 @@
 rope_base = 500000.0
 
 VMEM = 24 * 2**20
-RING_VMEM = 24 * 2**20
+RING_VMEM = 48 * 2**20
 
 F32 = jnp.float32
 BF16 = jnp.bfloat16
@@ -68,6 +68,52 @@
 
 def block_at(core, i, side):
     return jnp.where(core == 0, i, (i % side) * side + i // side)
+
+
+def weights_kernel(info, wq, wo, w_all, w_buf, sems):
+    n = w_buf.shape[0]
+    hw = wq.shape[2]
+    side = math.isqrt(n)
+
+    def fetches(i):
+        b = block_at(info[0], i, side)
+        return (
+            pltpu.make_async_copy(wq.at[b], w_buf.at[i, :, pl.ds(0, hw)], sems.at[0, i]),
+            pltpu.make_async_copy(wo.at[b], w_buf.at[i, :, pl.ds(hw, hw)], sems.at[1, i]),
+        )
+
+    def store(i):
+        return pltpu.make_async_copy(w_buf.at[i], w_all.at[i], sems.at[2, i])
+
+    @pl.loop(0, n)
+    def _(i):
+        for c in fetches(i):
+            c.start()
+
+    @pl.loop(0, n)
+    def _(i):
+        for c in fetches(i):
+            c.wait()
+        store(i).start()
+
+    @pl.loop(0, n)
+    def _(i):
+        store(i).wait()
+
+
+def arrange_weights(info, wq, wo):
+    n, kb, hw = wq.shape
+    hbm = pl.BlockSpec(memory_space=pltpu.HBM)
+    out = jax.ShapeDtypeStruct((n, kb, 2 * hw), BF16)
+    return pl.pallas_call(
+        weights_kernel,
+        out_shape=out,
+        in_specs=[pl.BlockSpec(memory_space=pltpu.SMEM), hbm, hbm],
+        out_specs=hbm,
+        scratch_shapes=[pltpu.VMEM(out.shape, out.dtype), pltpu.SemaphoreType.DMA((3, n))],
+        compiler_params=pltpu.CompilerParams(vmem_limit_bytes=60 * 2**20),
+        cost_estimate=pl.CostEstimate(flops=10**9, bytes_accessed=2 * 10**7, transcendentals=0),
+    )(info, wq, wo)
 
 
 def kv_weights_kernel(core, kv, ko, kv_all, kvscale):
@@ -136,13 +182,13 @@
         for i in range(w.shape[0]):
             total = total + jnp.dot(
                 x[i * half : (i + 1) * half, :],
-                jnp.concatenate([w[i, 0], w[i, 1]], axis=1),
+                w[i],
                 preferred_element_type=F32,
             )
     return total
 
 
-def fetch(info, shifts, sems, xs, x_buf, weights=None, kv=None):
+def fetch(info, shifts, sems, xs, x_buf, *pairs):
     copies = []
     used = iter(range(sems.shape[0]))
 
@@ -151,19 +197,10 @@
 
     for i, (x, (s, k)) in enumerate(zip(xs, shifts)):
         add(x, x_buf.at[i, pl.ds(0, x.shape[0])])
-        if kv is not None:
-            whole, buf = kv
+        for whole, buf in pairs:
             n, side = buf.shape[1], math.isqrt(whole.shape[0])
             place = lax.rem(info[1] + (side - s % side), side)
             add(whole.at[pl.ds(place * side + k * n, n)], buf.at[i])
-        if weights is not None:
-            wq, wo, buf = weights
-            n, side = buf.shape[1], math.isqrt(wq.shape[0])
-            place = lax.rem(info[1] + (side - s % side), side)
-            for j in range(n):
-                b = jnp.where(info[0] == 0, place * side + k * n + j, (k * n + j) * side + place)
-                add(wq.at[b], buf.at[i, j, 0])
-                add(wo.at[b], buf.at[i, j, 1])
     for c in copies:
         c.start()
     for c in copies:
@@ -173,15 +210,15 @@
 
 def matmul_kernel(shifts, info, *refs):
     m = len(shifts)
-    xs, wq, wo, kv_all = refs[:m], *refs[m : m + 3]
+    xs, w_all, kv_all = refs[:m], refs[m], refs[m + 1]
     q_out, kv_out, st_out, x_buf, w_buf, kv_buf, sems = refs[-7:]
-    if len(refs) == m + 10:
+    if len(refs) == m + 9:
         q_in, kv_in, st_in = q_out, kv_out, st_out
         for out in (q_out, kv_out, st_out):
             out[...] = jnp.zeros_like(out)
     else:
-        q_in, kv_in, st_in = refs[m + 3 : m + 6]
-    xs = fetch(info, shifts, sems, xs, x_buf, (wq, wo, w_buf), (kv_all, kv_buf))
+        q_in, kv_in, st_in = refs[m + 2 : m + 5]
+    xs = fetch(info, shifts, sems, xs, x_buf, (w_all, w_buf), (kv_all, kv_buf))
     ws, kvs = [w_buf.at[i] for i in range(m)], [kv_buf.at[i] for i in range(m)]
     q_out[...] = q_sum(xs, ws, q_in)
     total, squares, largest = kv_rows(xs, kvs, kv_in, st_in)
@@ -190,19 +227,15 @@
     st_out[1:2, :] = largest
 
 
-def arrivals_call(kernel, out_shape, info, xs, weights, kv, rest, flops, aliases=None):
+def arrivals_call(kernel, out_shape, info, xs, big, rest, flops, aliases=None):
     m = len(xs)
     n = xs[0].shape[0] // xs[0].shape[1]
-    big = [*weights, *kv]
     hbm = pl.BlockSpec(memory_space=pltpu.HBM)
     vmem = pl.BlockSpec(memory_space=pltpu.VMEM)
     smem = pl.BlockSpec(memory_space=pltpu.SMEM)
     scratch = [pltpu.VMEM((m, max(x.shape[0] for x in xs), xs[0].shape[1]), BF16)]
-    if weights:
-        scratch.append(pltpu.VMEM((m, n, 2) + weights[0].shape[1:], BF16))
-    if kv:
-        scratch.append(pltpu.VMEM((m, n) + kv[0].shape[1:], BF16))
-    count = m * (1 + len(kv) + n * len(weights))
+    scratch += [pltpu.VMEM((m, n) + w.shape[1:], BF16) for w in big]
+    count = m * (1 + len(big))
     return pl.pallas_call(
         kernel,
         out_shape=out_shape,
@@ -215,10 +248,10 @@
     )(info, *xs, *big, *rest)
 
 
-def matmul(half, info, shifts, xs, wq, wo, kv_all, acc):
+def matmul(half, info, shifts, xs, w_all, kv_all, acc):
     m = len(xs)
     out_shape = (
-        jax.ShapeDtypeStruct((half, 2 * wq.shape[2]), F32),
+        jax.ShapeDtypeStruct((half, w_all.shape[2]), F32),
         jax.ShapeDtypeStruct((kv_all.shape[1], half), F32),
         jax.ShapeDtypeStruct((8, half), F32),
     )
@@ -227,11 +260,10 @@
         out_shape,
         info,
         xs,
-        (wq, wo),
-        (kv_all,),
+        (w_all, kv_all),
         acc,
         2 * m * xs[0].shape[0] * xs[0].shape[1] * 288,
-        {4 + m + i: i for i in range(len(acc))},
+        {3 + m + i: i for i in range(len(acc))},
     )
 
 
@@ -239,7 +271,7 @@
     m = len(shifts)
     xs, kv_all = refs[:m], refs[m]
     kv_in, st_in, kvscale, kcos, ksin, kvt, st_out, x_buf, kv_buf, sems = refs[m + 1 :]
-    xs = fetch(info, shifts, sems, xs, x_buf, kv=(kv_all, kv_buf))
+    xs = fetch(info, shifts, sems, xs, x_buf, (kv_all, kv_buf))
     t, squares, largest = kv_rows(xs, [kv_buf.at[i] for i in range(m)], kv_in, st_in)
     st_out[0:1, :] = squares
     st_out[1:2, :] = largest
@@ -268,7 +300,6 @@
         out_shape,
         info,
         xs,
-        (),
         (kv_all,),
         [kv, st, kvscale, kcos, ksin],
         10**9,
@@ -277,9 +308,9 @@
 
 def last_q_kernel(d, shifts, info, *refs):
     m = len(shifts)
-    xs, wq, wo = refs[:m], refs[m], refs[m + 1]
-    q_in, st, wscale, cosine, sine, mine, msg, x_buf, w_buf, sems = refs[m + 2 :]
-    xs = fetch(info, shifts, sems, xs, x_buf, weights=(wq, wo, w_buf))
+    xs, w_all = refs[:m], refs[m]
+    q_in, st, wscale, cosine, sine, mine, msg, x_buf, w_buf, sems = refs[m + 1 :]
+    xs = fetch(info, shifts, sems, xs, x_buf, (w_all, w_buf))
     q = q_sum(xs, [w_buf.at[i] for i in range(m)], q_in)
     half = q.shape[0]
     squares, largest = st[0:1, :], st[1:2, :]
@@ -298,7 +329,7 @@
     )
 
 
-def last_q(d, info, shifts, xs, wq, wo, q, st, wscale, cosine, sine):
+def last_q(d, info, shifts, xs, w_all, q, st, wscale, cosine, sine):
     half = q.shape[0]
     out_shape = (
         jax.ShapeDtypeStruct((half, HD), BF16),
@@ -309,8 +340,7 @@
         out_shape,
         info,
         xs,
-        (wq, wo),
-        (),
+        (w_all,),
         [q, st, wscale, cosine, sine],
         10**9,
     )
@@ -480,10 +510,11 @@
         coord = jnp.where(core == 0, y, x)
 
         info = jnp.stack([core, coord]).astype(jnp.int32)
-        wq = w_query.reshape(-1, 2 * width, HD)
-        wo = wq_other.reshape(-1, 2 * width, HD)
-        gathered, wo, tables, info, order, qscale = lax.optimization_barrier(
-            (gathered, wo, tables, info, order, qscale)
+        w_all = arrange_weights(
+            info, w_query.reshape(-1, 2 * width, HD), wq_other.reshape(-1, 2 * width, HD)
+        )
+        gathered, w_all, tables, info, order, qscale = lax.optimization_barrier(
+            (gathered, w_all, tables, info, order, qscale)
         )
         cos_own, sin_own, cos_far, sin_far, cos_k, sin_k = tables
 
@@ -498,7 +529,7 @@
 
         def mm(acc, items):
             shifts = [(s, k) for s, k, _ in items]
-            return matmul(half, info, shifts, [v for _, _, v in items], wq, wo, kv_all, acc)
+            return matmul(half, info, shifts, [v for _, _, v in items], w_all, kv_all, acc)
 
         up, down = [second(low, 1)], [second(low, -1)]
         up.append(second(high, 1))
@@ -536,7 +567,7 @@
         kvr = lax.all_to_all(
             kvt, "tp", split_axis=0, concat_axis=0, tiled=False, axis_index_groups=rows
         )
-        mine, msg = last_q(d, info, shifts, xs, wq, wo, acc[0], st, qscale, cos_own, sin_own)
+        mine, msg = last_q(d, info, shifts, xs, w_all, acc[0], st, qscale, cos_own, sin_own)
         far = swap(msg)
         out = jax.ShapeDtypeStruct((count, HD), BF16)
         queries, payload, scale = call(

time: 142 us -> 149 us (1.049)
  waiting for transfers between devices: 42.5 us -> 49.5 us
  local copies, waits for them, and re-layouts: 6.84 us -> 2.48 us
  Pallas kernels: 32.8 us -> 36.2 us
    pallas_call x0 -> x1, Pallas kernels: none -> 8.77 us  [arrange_weights(): pl.pallas_call(weights_kernel, out_shape=out, in_specs=[pl.BlockSpec(memo...]
    pallas_call x9, Pallas kernels: 27.7 us -> 22.4 us  [arrivals_call(): pl.pallas_call(kernel, out_shape=out_shape, in_specs=[smem] + [hbm] * (m...]
    ppermute x14, waiting for transfers between devices: 7.21 us -> 12.1 us  [second(): return lax.ppermute(v, 'tp', pairs)]
    unnamed x18 -> x14, local copies, waits for them, and re-layouts: 5.94 us -> 1.58 us
    all_to_all x1, waiting for transfers between devices: 3.61 us -> 6.33 us  [body(): lax.all_to_all(kvt, 'tp', split_axis=0, concat_axis=0, tiled=False, axis_...]
    ppermute x14, starting transfers between devices: 16.1 us -> 18.7 us  [second(): return lax.ppermute(v, 'tp', pairs)]
  transfers between devices with their start and end apart: 21 -> 21, of which waited for: 7 -> 11; matrix products, arithmetic and copies ran while one was open for 2% -> 2% of each run, Pallas kernels for 21% -> 22%
where the time goes in v5:
time: 149 us
  starting transfers between devices  56.4 us (38%)
  waiting for transfers between devices  49.5 us (33%)
  Pallas kernels  36.2 us (24%)
  other arithmetic  2.53 us (2%)
  local copies, waits for them, and re-layouts  2.48 us (2%)
  between operations  1.65 us (1%)
    ppermute x1, waiting for transfers between devices, body(): lax.ppermute(jnp.concatenate([w_kv, scales], axis=1), 'tp', to_row)  26.4 us
    ppermute x4, starting transfers between devices, swap(): return lax.ppermute(v, 'tp', to_partner)  23.2 us
    pallas_call x9, Pallas kernels, arrivals_call(): pl.pallas_call(kernel, out_shape=out_shape, in_specs=[smem] + [hbm] * (m...  22.4 us
    ppermute x14, starting transfers between devices, second(): return lax.ppermute(v, 'tp', pairs)  18.7 us
    ppermute x14, waiting for transfers between devices, second(): return lax.ppermute(v, 'tp', pairs)  12.1 us
    all_to_all x1, starting transfers between devices, body(): lax.all_to_all(kvt, 'tp', split_axis=0, concat_axis=0, tiled=False, axis_...  10.5 us
    pallas_call x1, Pallas kernels, arrange_weights(): pl.pallas_call(weights_kernel, out_shape=out, in_specs=[pl.BlockSpec(memo...  8.77 us
    all_to_all x1, waiting for transfers between devices, body(): lax.all_to_all(kvt, 'tp', split_axis=0, concat_axis=0, tiled=False, axis_...  6.33 us
  transfers between devices with their start and end apart: 21, of which 11 were waited for; matrix products, arithmetic and copies ran while one was open for 2% of the time, Pallas kernels for 22%

profile of v5, /device:TPU:513, one launch (start us, length us, event | category | flops | bytes accessed | tf_op | source)
XLA Modules:
  0.0 148.7 jit_solution(18357521574043198361)
XLA Ops:
  0.6 20.5 %collective-permute-start.1 = (bf16[16384,128]{1,0:T(8,128)(2,1)}, bf16[16384,128]{1,0:T(8,128)(2,1)}, u32[]{:S(2)}, u32[]{:S(2)}) collective-permute-start(bf16[16384,128]{1,0:T(8,128)(2,1)} %param.9), channel_id=1, source_target_pairs={{0,1},{1,0},{2,3},{3,2},{4,5},{5,4},{6,7},{7,6},{8,9},{9,8},{10,11... | collective-permute-start | bytes 12582920 | tf_op jit(solution)/shard_map/ppermute | solution.py:445
  21.2 0.9 copy-done
  22.1 0.7 copy-done.3
  22.7 0.2 shard_map.101
  22.9 0.2 collective-permute-start
  23.1 0.7 convert_bitcast_fusion.2
  23.8 0.7 convert_bitcast_fusion.1
  24.5 0.1 copy.32
  24.6 3.7 %collective-permute-done.recv = bf16[272,128]{1,0:T(8,128)(2,1)S(1)} collective-permute-done((bf16[272,128]{1,0:T(8,128)(2,1)S(1)}, bf16[272,128]{1,0:T(8,128)(2,1)S(1)}, u32[]{:S(2)}, u32[]{:S(2)}) %collective-permute-start) | collective-permute-done | bytes 69664 | tf_op jit(solution)/shard_map/ppermute | solution.py:445
  28.3 1.1 shard_map.102
  29.4 3.9 %all-to-all-start = ((bf16[8,272,256]{2,1,0:T(8,128)(2,1)}), bf16[8,272,256]{2,1,0:T(8,128)(2,1)S(1)}, u32[]{:S(2)}, u32[]{:S(2)}) async-start(bf16[8,272,256]{2,1,0:T(8,128)(2,1)} %shard_map.102), calls=%async_computation | async-start | bytes 2228224 | tf_op jit(solution)/shard_map/all_to_all | solution.py:482
  33.4 0.0 copy-start.6
  33.4 0.1 collective-permute-start.4
  34.4 0.1 fusion.17
  34.5 0.6 pad_add_fusion.info.core.refs_0_.r_0_
  35.1 0.1 multiply_sine_fusion.2
  35.3 1.0 multiply_sine_fusion
  36.2 26.4 %collective-permute-done.4.kv = bf16[16,16512]{1,0:T(8,128)(2,1)S(1)} collective-permute-done((bf16[16,16512]{1,0:T(8,128)(2,1)S(1)}, bf16[16,16512]{1,0:T(8,128)(2,1)S(1)}, u32[]{:S(2)}, u32[]{:S(2)}) %collective-permute-start.4) | collective-permute-done | bytes 528416 | tf_op jit(solution)/shard_map/ppermute | solution.py:473
  62.6 1.7 %collective-permute-start.5 = (bf16[16,16512]{1,0:T(8,128)(2,1)S(1)}, bf16[16,16512]{1,0:T(8,128)(2,1)S(1)}, u32[]{:S(2)}, u32[]{:S(2)}) collective-permute-start(bf16[16,16512]{1,0:T(8,128)(2,1)S(1)} %collective-permute-done.4.kv), channel_id=1, source_target_pairs={{0,1},{1,0},{2,3},{3,2},{4,5},{5,4},{6,7},{7,6},{8,9},{9,8},{10,11... | collective-permute-start | bytes 1585160 | tf_op jit(solution)/shard_map/ppermute | solution.py:445
  64.3 0.0 collective-permute-done.1
  64.3 8.8 %shard_map.103.refs_3_ = bf16[64,256,256]{2,1,0:T(8,128)(2,1)} custom-call(s32[2]{0:T(128)} %pad_add_fusion.info.core.refs_0_.r_0_, bf16[64,256,128]{2,1,0:T(8,128)(2,1)} %bitcast.22, bf16[64,256,128]{2,1,0:T(8,128)(2,1)} %bitcast.4.wo), custom_call_target="tpu_custom_call" | custom-call | flops 1000000000 | bytes 20000000 | tf_op jit(solution)/shard_map/pallas_call | solution.py:108
  73.1 0.0 all-to-all-done.gathered
  73.1 0.0 copy-start.2
  73.2 0.1 collective-permute-start.2
  73.3 2.6 %collective-permute-start.3 = (bf16[1024,256]{1,0:T(8,128)(2,1)S(1)}, bf16[1024,256]{1,0:T(8,128)(2,1)S(1)}, u32[]{:S(2)}, u32[]{:S(2)}) collective-permute-start(bf16[1024,256]{1,0:T(8,128)(2,1)S(1)} %bitcast.18), channel_id=1, source_target_pairs={{0,112},{1,15},{2,114},{3,1},{4,116},{5,3},{6,118},{7,5},{8,120},{... | collective-permute-start | bytes 1572872 | tf_op jit(solution)/shard_map/ppermute | solution.py:442
  76.0 0.1 shard_map.104.refs_2_
  76.0 0.1 collective-permute-start.8
  76.2 2.6 %collective-permute-start.9 = (bf16[1040,256]{1,0:T(8,128)(2,1)S(1)}, bf16[1040,256]{1,0:T(8,128)(2,1)S(1)}, u32[]{:S(2)}, u32[]{:S(2)}) collective-permute-start(bf16[1040,256]{1,0:T(8,128)(2,1)S(1)} %shard_map.104.refs_2_), channel_id=1, source_target_pairs={{0,112},{1,15},{2,114},{3,1},{4,116},{5,3},{6,118},{7,5},{8,120},{... | collective-permute-start | bytes 1597448 | tf_op jit(solution)/shard_map/ppermute | solution.py:442
  78.8 0.0 collective-permute-done.5.ko
  78.8 0.7 shard_map.105
  79.5 2.6 %shard_map.106 = (f32[256,256]{1,0:T(8,128)S(1)}, f32[32,256]{1,0:T(8,128)S(1)}, f32[8,256]{1,0:T(8,128)S(1)}) custom-call(s32[2]{0:T(128)S(1)} %copy-done.2, bf16[1024,256]{1,0:T(8,128)(2,1)S(1)} %bitcast.19, bf16[1040,256]{1,0:T(8,128)(2,1)S(1)} %shard_map.104.refs_2_, bf16[64,256,256]{2,1,0:T(8,128)(2,1)} %shard_map.103.refs_3_, ...), custom_call_target="tpu_custom_call" | custom-call | flops 301989888 | bytes 1000000 | tf_op jit(solution)/shard_map/pallas_call | solution.py:239
  82.1 0.7 collective-permute-done.2.refs_1_
  82.8 0.0 collective-permute-start.6
  82.8 2.7 %collective-permute-start.7 = (bf16[1024,256]{1,0:T(8,128)(2,1)S(1)}, bf16[1024,256]{1,0:T(8,128)(2,1)S(1)}, u32[]{:S(2)}, u32[]{:S(2)}) collective-permute-start(bf16[1024,256]{1,0:T(8,128)(2,1)S(1)} %collective-permute-done.3.refs_2_), channel_id=1, source_target_pairs={{0,112},{1,15},{2,114},{3,1},{4,116},{5,3},{6,118},{7,5},{8,120},{... | collective-permute-start | bytes 1572872 | tf_op jit(solution)/shard_map/ppermute | solution.py:442
  85.5 2.6 %shard_map.107 = (f32[256,256]{1,0:T(8,128)S(1)}, f32[32,256]{1,0:T(8,128)S(1)}, f32[8,256]{1,0:T(8,128)S(1)}) custom-call(s32[2]{0:T(128)S(1)} %copy-done.2, bf16[1024,256]{1,0:T(8,128)(2,1)S(1)} %collective-permute-done.2.refs_1_, bf16[1024,256]{1,0:T(8,128)(2,1)S(1)} %collective-permute-done.3.refs_2_, ...), custom_call_target="tpu_custom_call", output_to_operand_aliasing={{0}: (5, {}), {1}: (6, {}), {2}: (7, {})} | custom-call | flops 301989888 | bytes 1000000 | tf_op jit(solution)/shard_map/pallas_call | solution.py:239
  88.1 0.4 collective-permute-done.8.refs_1_
  88.5 0.0 collective-permute-done.9.refs_2_
  88.5 0.0 collective-permute-start.12
  88.5 2.7 %collective-permute-start.13 = (bf16[1040,256]{1,0:T(8,128)(2,1)S(1)}, bf16[1040,256]{1,0:T(8,128)(2,1)S(1)}, u32[]{:S(2)}, u32[]{:S(2)}) collective-permute-start(bf16[1040,256]{1,0:T(8,128)(2,1)S(1)} %collective-permute-done.9.refs_2_), channel_id=1, source_target_pairs={{0,112},{1,15},{2,114},{3,1},{4,116},{5,3},{6,118},{7,5},{8,120},{... | collective-permute-start | bytes 1597448 | tf_op jit(solution)/shard_map/ppermute | solution.py:442
  91.2 2.6 %shard_map.108 = (f32[256,256]{1,0:T(8,128)S(1)}, f32[32,256]{1,0:T(8,128)S(1)}, f32[8,256]{1,0:T(8,128)S(1)}) custom-call(s32[2]{0:T(128)S(1)} %copy-done.2, bf16[1040,256]{1,0:T(8,128)(2,1)S(1)} %collective-permute-done.8.refs_1_, bf16[1040,256]{1,0:T(8,128)(2,1)S(1)} %collective-permute-done.9.refs_2_, ...), custom_call_target="tpu_custom_call", output_to_operand_aliasing={{0}: (5, {}), {1}: (6, {}), {2}: (7, {})} | custom-call | flops 306708480 | bytes 1000000 | tf_op jit(solution)/shard_map/pallas_call | solution.py:239
  93.8 0.3 collective-permute-done.6.refs_1_
  94.1 0.0 collective-permute-done.7.refs_2_
  94.1 0.0 collective-permute-start.10
  94.1 2.7 %collective-permute-start.11 = (bf16[1024,256]{1,0:T(8,128)(2,1)S(1)}, bf16[1024,256]{1,0:T(8,128)(2,1)S(1)}, u32[]{:S(2)}, u32[]{:S(2)}) collective-permute-start(bf16[1024,256]{1,0:T(8,128)(2,1)S(1)} %collective-permute-done.7.refs_2_), channel_id=1, source_target_pairs={{0,112},{1,15},{2,114},{3,1},{4,116},{5,3},{6,118},{7,5},{8,120},{... | collective-permute-start | bytes 1572872 | tf_op jit(solution)/shard_map/ppermute | solution.py:442
  96.8 2.6 %shard_map.109 = (f32[256,256]{1,0:T(8,128)S(1)}, f32[32,256]{1,0:T(8,128)S(1)}, f32[8,256]{1,0:T(8,128)S(1)}) custom-call(s32[2]{0:T(128)S(1)} %copy-done.2, bf16[1024,256]{1,0:T(8,128)(2,1)S(1)} %collective-permute-done.6.refs_1_, bf16[1024,256]{1,0:T(8,128)(2,1)S(1)} %collective-permute-done.7.refs_2_, ...), custom_call_target="tpu_custom_call", output_to_operand_aliasing={{0}: (5, {}), {1}: (6, {}), {2}: (7, {})} | custom-call | flops 301989888 | bytes 1000000 | tf_op jit(solution)/shard_map/pallas_call | solution.py:239
  99.4 0.4 collective-permute-done.12.refs_1_
  99.9 2.7 %collective-permute-start.16 = (bf16[1040,256]{1,0:T(8,128)(2,1)S(1)}, bf16[1040,256]{1,0:T(8,128)(2,1)S(1)}, u32[]{:S(2)}, u32[]{:S(2)}) collective-permute-start(bf16[1040,256]{1,0:T(8,128)(2,1)S(1)} %collective-permute-done.13.refs_2_), channel_id=1, source_target_pairs={{0,112},{1,15},{2,114},{3,1},{4,116},{5,3},{6,118},{7,5},{8,120},{... | collective-permute-start | bytes 1597448 | tf_op jit(solution)/shard_map/ppermute | solution.py:442
  102.5 2.6 %shard_map.110 = (f32[256,256]{1,0:T(8,128)S(1)}, f32[32,256]{1,0:T(8,128)S(1)}, f32[8,256]{1,0:T(8,128)S(1)}) custom-call(s32[2]{0:T(128)S(1)} %copy-done.2, bf16[1040,256]{1,0:T(8,128)(2,1)S(1)} %collective-permute-done.12.refs_1_, ...), custom_call_target="tpu_custom_call", output_to_operand_aliasing={{0}: (5, {}), {1}: (6, {}), {2}: (7, {})} | custom-call | flops 306708480 | bytes 1000000 | tf_op jit(solution)/shard_map/pallas_call | solution.py:239
  105.1 0.3 collective-permute-done.10.refs_1_
  105.5 0.0 collective-permute-done.11.refs_2_
  105.5 2.6 %shard_map.111 = (f32[256,256]{1,0:T(8,128)S(1)}, f32[32,256]{1,0:T(8,128)S(1)}, f32[8,256]{1,0:T(8,128)S(1)}) custom-call(s32[2]{0:T(128)S(1)} %copy-done.2, bf16[1024,256]{1,0:T(8,128)(2,1)S(1)} %collective-permute-done.10.refs_1_, ...), custom_call_target="tpu_custom_call", output_to_operand_aliasing={{0}: (5, {}), {1}: (6, {}), {2}: (7, {})} | custom-call | flops 301989888 | bytes 1000000 | tf_op jit(solution)/shard_map/pallas_call | solution.py:239
  108.0 3.1 %collective-permute-done.15.refs_1_ = bf16[1040,256]{1,0:T(8,128)(2,1)S(1)} collective-permute-done((bf16[1040,256]{1,0:T(8,128)(2,1)S(1)}, bf16[1040,256]{1,0:T(8,128)(2,1)S(1)}, u32[]{:S(2)}, u32[]{:S(2)}) %collective-permute-start.15) | collective-permute-done | bytes 532512 | tf_op jit(solution)/shard_map/ppermute | solution.py:442
  111.2 2.4 %collective-permute-start.17 = (bf16[1040,256]{1,0:T(8,128)(2,1)S(1)}, bf16[1040,256]{1,0:T(8,128)(2,1)S(1)}, u32[]{:S(2)}, u32[]{:S(2)}) collective-permute-start(bf16[1040,256]{1,0:T(8,128)(2,1)S(1)} %collective-permute-done.16.refs_2_), channel_id=1, source_target_pairs={{0,112},{1,15},{2,114},{3,1},{4,116},{5,3},{6,118},{7,5},{8,120},{... | collective-permute-start | bytes 1597448 | tf_op jit(solution)/shard_map/ppermute | solution.py:442
  113.6 2.6 %shard_map.112 = (f32[256,256]{1,0:T(8,128)S(1)}, f32[32,256]{1,0:T(8,128)S(1)}, f32[8,256]{1,0:T(8,128)S(1)}) custom-call(s32[2]{0:T(128)S(1)} %copy-done.2, bf16[1040,256]{1,0:T(8,128)(2,1)S(1)} %collective-permute-done.15.refs_1_, ...), custom_call_target="tpu_custom_call", output_to_operand_aliasing={{0}: (5, {}), {1}: (6, {}), {2}: (7, {})} | custom-call | flops 306708480 | bytes 1000000 | tf_op jit(solution)/shard_map/pallas_call | solution.py:239
  116.1 6.7 %collective-permute-done.14.refs_1_ = bf16[1024,256]{1,0:T(8,128)(2,1)S(1)} collective-permute-done((bf16[1024,256]{1,0:T(8,128)(2,1)S(1)}, bf16[1024,256]{1,0:T(8,128)(2,1)S(1)}, u32[]{:S(2)}, u32[]{:S(2)}) %collective-permute-start.14) | collective-permute-done | bytes 524320 | tf_op jit(solution)/shard_map/ppermute | solution.py:442
  122.8 2.0 %shard_map.113 = (bf16[16,32,256]{2,1,0:T(8,128)(2,1)}, f32[8,256]{1,0:T(8,128)S(1)}) custom-call(s32[2]{0:T(128)S(1)} %copy-done.2, bf16[1024,256]{1,0:T(8,128)(2,1)S(1)} %collective-permute-done.14.refs_1_, bf16[1040,256]{1,0:T(8,128)(2,1)S(1)} %collective-permute-done.17.refs_2_, bf16[64,32,256]{2,1,0:T(8,128)(2,1)S(1)} %get-tuple-element.83.refs_4_.refs_3_, ...), custom_call_target="tpu_custom_call" | custom-call | flops 1000000000 | bytes 1000000 | tf_op jit(solution)/shard_map/pallas_call | solution.py:239
  124.8 10.5 %all-to-all-start.1 = ((bf16[16,32,256]{2,1,0:T(8,128)(2,1)}), bf16[16,32,256]{2,1,0:T(8,128)(2,1)S(1)}, u32[]{:S(2)}, u32[]{:S(2)}) async-start(bf16[16,32,256]{2,1,0:T(8,128)(2,1)} %get-tuple-element.146), calls=%async_computation.1 | async-start | bytes 524288 | tf_op jit(solution)/shard_map/all_to_all | solution.py:567
  135.3 0.0 copy-start.4
  135.3 2.3 %shard_map.114 = (bf16[256,128]{1,0:T(8,128)(2,1)S(1)}, f32[264,128]{1,0:T(8,128)S(1)}) custom-call(s32[2]{0:T(128)S(1)} %copy-done.2, bf16[1024,256]{1,0:T(8,128)(2,1)S(1)} %collective-permute-done.14.refs_1_, bf16[1040,256]{1,0:T(8,128)(2,1)S(1)} %collective-permute-done.17.refs_2_, bf16[64,256,256]{2,1,0:T(8,128)(2,1)} %shard_map.103.refs_3_, ...), custom_call_target="tpu_custom_call" | custom-call | flops 1000000000 | bytes 1000000 | tf_op jit(solution)/shard_map/pallas_call | solution.py:239
  137.7 0.8 collective-permute-start.18
  138.5 1.0 collective-permute-done.18.r_2_
  139.4 1.5 %shard_map.115 = (bf16[512,128]{1,0:T(8,128)(2,1)}, bf16[512,128]{1,0:T(8,128)(2,1)}, f32[4,128]{1,0:T(4,128)}) custom-call(s32[2]{0:T(128)S(1)} %copy-done.2, bf16[256,128]{1,0:T(8,128)(2,1)S(1)} %get-tuple-element.140.r_1_, f32[264,128]{1,0:T(8,128)S(1)} %collective-permute-done.18.r_2_, f32[8,256]{1,0:T(8,128)S(1)} %get-tuple-element.136.refs_5_.r_3_, ...), custom_call_target="tpu_custom_call" | custom-call | flops 100000000 | bytes 1000000 | tf_op jit(solution)/shard_map/pallas_call | solution.py:404
  140.9 6.3 %all-to-all-done.1.kvr = bf16[16,32,256]{2,1,0:T(8,128)(2,1)S(1)} async-done(((bf16[16,32,256]{2,1,0:T(8,128)(2,1)}), bf16[16,32,256]{2,1,0:T(8,128)(2,1)S(1)}, u32[]{:S(2)}, u32[]{:S(2)}) %all-to-all-start.1) | async-done | bytes 262176 | tf_op jit(solution)/shard_map/all_to_all | solution.py:567
  147.3 1.4 shard_map.116
  (23 shorter events, 0.2 us)
Async XLA Ops:
  0.6 63.7 %collective-permute-start.1 = (bf16[16384,128]{1,0:T(8,128)(2,1)}, bf16[16384,128]{1,0:T(8,128)(2,1)}, u32[]{:S(2)}, u32[]{:S(2)}) collective-permute-start(bf16[16384,128]{1,0:T(8,128)(2,1)} %param.9), channel_id=1, source_target_pairs={{0,1},{1,0},{2,3},{3,2},{4,5},{5,4},{6,7},{7,6},{8,9},{9,8},{10,11... | collective-permute-start | bytes 12582920 | tf_op jit(solution)/shard_map/ppermute | solution.py:445
  21.2 0.9 copy-start
  22.1 0.7 copy-start.3
  22.9 5.3 %collective-permute-start = (bf16[272,128]{1,0:T(8,128)(2,1)S(1)}, bf16[272,128]{1,0:T(8,128)(2,1)S(1)}, u32[]{:S(2)}, u32[]{:S(2)}) collective-permute-start(bf16[272,128]{1,0:T(8,128)(2,1)S(1)} %get-tuple-element.79), channel_id=1, source_target_pairs={{0,1},{1,0},{2,3},{3,2},{4,5},{5,4},{6,7},{7,6},{8,9},{9,8},{10,11... | collective-permute-start | bytes 208904 | tf_op jit(solution)/shard_map/ppermute | solution.py:445
  29.4 3.9 %copy-start.5 = (bf16[16,16384]{1,0:T(8,128)(2,1)S(1)}, bf16[16,16384]{1,0:T(8,128)(2,1)}, u32[]{:S(2)}) copy-start(bf16[16,16384]{1,0:T(8,128)(2,1)} %param.10) | copy-start | bytes 1572868
  29.4 43.7 %all-to-all-start = ((bf16[8,272,256]{2,1,0:T(8,128)(2,1)}), bf16[8,272,256]{2,1,0:T(8,128)(2,1)S(1)}, u32[]{:S(2)}, u32[]{:S(2)}) async-start(bf16[8,272,256]{2,1,0:T(8,128)(2,1)} %shard_map.102), calls=%async_computation | async-start | bytes 2228224 | tf_op jit(solution)/shard_map/all_to_all | solution.py:482
  33.4 1.2 copy-start.6
  33.4 29.2 %collective-permute-start.4 = (bf16[16,16512]{1,0:T(8,128)(2,1)S(1)}, bf16[16,16512]{1,0:T(8,128)(2,1)S(1)}, u32[]{:S(2)}, u32[]{:S(2)}) collective-permute-start(bf16[16,16512]{1,0:T(8,128)(2,1)S(1)} %fusion.1), channel_id=1, source_target_pairs={{0,14},{1,30},{2,34},{3,50},{4,70},{5,86},{6,106},{7,122},{8,6},{9... | collective-permute-start | bytes 1585160 | tf_op jit(solution)/shard_map/ppermute | solution.py:473
  62.6 16.2 %collective-permute-start.5 = (bf16[16,16512]{1,0:T(8,128)(2,1)S(1)}, bf16[16,16512]{1,0:T(8,128)(2,1)S(1)}, u32[]{:S(2)}, u32[]{:S(2)}) collective-permute-start(bf16[16,16512]{1,0:T(8,128)(2,1)S(1)} %collective-permute-done.4.kv), channel_id=1, source_target_pairs={{0,1},{1,0},{2,3},{3,2},{4,5},{5,4},{6,7},{7,6},{8,9},{9,8},{10,11... | collective-permute-start | bytes 1585160 | tf_op jit(solution)/shard_map/ppermute | solution.py:445
  73.1 5.7 %copy-start.2 = (s32[2]{0:T(128)S(1)}, s32[2]{0:T(128)}, u32[]{:S(2)}) copy-start(s32[2]{0:T(128)} %pad_add_fusion.info.core.refs_0_.r_0_) | copy-start | bytes 28
  73.2 9.7 %collective-permute-start.2 = (bf16[1024,256]{1,0:T(8,128)(2,1)S(1)}, bf16[1024,256]{1,0:T(8,128)(2,1)S(1)}, u32[]{:S(2)}, u32[]{:S(2)}) collective-permute-start(bf16[1024,256]{1,0:T(8,128)(2,1)S(1)} %bitcast.17), channel_id=1, source_target_pairs={{0,16},{1,3},{2,18},{3,5},{4,20},{5,7},{6,22},{7,9},{8,24},{9,11},... | collective-permute-start | bytes 1572872 | tf_op jit(solution)/shard_map/ppermute | solution.py:442
  73.3 9.5 %collective-permute-start.3 = (bf16[1024,256]{1,0:T(8,128)(2,1)S(1)}, bf16[1024,256]{1,0:T(8,128)(2,1)S(1)}, u32[]{:S(2)}, u32[]{:S(2)}) collective-permute-start(bf16[1024,256]{1,0:T(8,128)(2,1)S(1)} %bitcast.18), channel_id=1, source_target_pairs={{0,112},{1,15},{2,114},{3,1},{4,116},{5,3},{6,118},{7,5},{8,120},{... | collective-permute-start | bytes 1572872 | tf_op jit(solution)/shard_map/ppermute | solution.py:442
  76.0 12.5 %collective-permute-start.8 = (bf16[1040,256]{1,0:T(8,128)(2,1)S(1)}, bf16[1040,256]{1,0:T(8,128)(2,1)S(1)}, u32[]{:S(2)}, u32[]{:S(2)}) collective-permute-start(bf16[1040,256]{1,0:T(8,128)(2,1)S(1)} %shard_map.104.refs_2_), channel_id=1, source_target_pairs={{0,16},{1,3},{2,18},{3,5},{4,20},{5,7},{6,22},{7,9},{8,24},{9,11},... | collective-permute-start | bytes 1597448 | tf_op jit(solution)/shard_map/ppermute | solution.py:442
  76.2 12.4 %collective-permute-start.9 = (bf16[1040,256]{1,0:T(8,128)(2,1)S(1)}, bf16[1040,256]{1,0:T(8,128)(2,1)S(1)}, u32[]{:S(2)}, u32[]{:S(2)}) collective-permute-start(bf16[1040,256]{1,0:T(8,128)(2,1)S(1)} %shard_map.104.refs_2_), channel_id=1, source_target_pairs={{0,112},{1,15},{2,114},{3,1},{4,116},{5,3},{6,118},{7,5},{8,120},{... | collective-permute-start | bytes 1597448 | tf_op jit(solution)/shard_map/ppermute | solution.py:442
  82.8 11.3 %collective-permute-start.6 = (bf16[1024,256]{1,0:T(8,128)(2,1)S(1)}, bf16[1024,256]{1,0:T(8,128)(2,1)S(1)}, u32[]{:S(2)}, u32[]{:S(2)}) collective-permute-start(bf16[1024,256]{1,0:T(8,128)(2,1)S(1)} %collective-permute-done.2.refs_1_), channel_id=1, source_target_pairs={{0,16},{1,3},{2,18},{3,5},{4,20},{5,7},{6,22},{7,9},{8,24},{9,11},... | collective-permute-start | bytes 1572872 | tf_op jit(solution)/shard_map/ppermute | solution.py:442
  82.8 11.3 %collective-permute-start.7 = (bf16[1024,256]{1,0:T(8,128)(2,1)S(1)}, bf16[1024,256]{1,0:T(8,128)(2,1)S(1)}, u32[]{:S(2)}, u32[]{:S(2)}) collective-permute-start(bf16[1024,256]{1,0:T(8,128)(2,1)S(1)} %collective-permute-done.3.refs_2_), channel_id=1, source_target_pairs={{0,112},{1,15},{2,114},{3,1},{4,116},{5,3},{6,118},{7,5},{8,120},{... | collective-permute-start | bytes 1572872 | tf_op jit(solution)/shard_map/ppermute | solution.py:442
  88.5 11.3 %collective-permute-start.12 = (bf16[1040,256]{1,0:T(8,128)(2,1)S(1)}, bf16[1040,256]{1,0:T(8,128)(2,1)S(1)}, u32[]{:S(2)}, u32[]{:S(2)}) collective-permute-start(bf16[1040,256]{1,0:T(8,128)(2,1)S(1)} %collective-permute-done.8.refs_1_), channel_id=1, source_target_pairs={{0,16},{1,3},{2,18},{3,5},{4,20},{5,7},{6,22},{7,9},{8,24},{9,11},... | collective-permute-start | bytes 1597448 | tf_op jit(solution)/shard_map/ppermute | solution.py:442
  88.5 11.3 %collective-permute-start.13 = (bf16[1040,256]{1,0:T(8,128)(2,1)S(1)}, bf16[1040,256]{1,0:T(8,128)(2,1)S(1)}, u32[]{:S(2)}, u32[]{:S(2)}) collective-permute-start(bf16[1040,256]{1,0:T(8,128)(2,1)S(1)} %collective-permute-done.9.refs_2_), channel_id=1, source_target_pairs={{0,112},{1,15},{2,114},{3,1},{4,116},{5,3},{6,118},{7,5},{8,120},{... | collective-permute-start | bytes 1597448 | tf_op jit(solution)/shard_map/ppermute | solution.py:442
  94.1 11.3 %collective-permute-start.10 = (bf16[1024,256]{1,0:T(8,128)(2,1)S(1)}, bf16[1024,256]{1,0:T(8,128)(2,1)S(1)}, u32[]{:S(2)}, u32[]{:S(2)}) collective-permute-start(bf16[1024,256]{1,0:T(8,128)(2,1)S(1)} %collective-permute-done.6.refs_1_), channel_id=1, source_target_pairs={{0,16},{1,3},{2,18},{3,5},{4,20},{5,7},{6,22},{7,9},{8,24},{9,11},... | collective-permute-start | bytes 1572872 | tf_op jit(solution)/shard_map/ppermute | solution.py:442
  94.1 11.3 %collective-permute-start.11 = (bf16[1024,256]{1,0:T(8,128)(2,1)S(1)}, bf16[1024,256]{1,0:T(8,128)(2,1)S(1)}, u32[]{:S(2)}, u32[]{:S(2)}) collective-permute-start(bf16[1024,256]{1,0:T(8,128)(2,1)S(1)} %collective-permute-done.7.refs_2_), channel_id=1, source_target_pairs={{0,112},{1,15},{2,114},{3,1},{4,116},{5,3},{6,118},{7,5},{8,120},{... | collective-permute-start | bytes 1572872 | tf_op jit(solution)/shard_map/ppermute | solution.py:442
  99.8 11.3 %collective-permute-start.15 = (bf16[1040,256]{1,0:T(8,128)(2,1)S(1)}, bf16[1040,256]{1,0:T(8,128)(2,1)S(1)}, u32[]{:S(2)}, u32[]{:S(2)}) collective-permute-start(bf16[1040,256]{1,0:T(8,128)(2,1)S(1)} %collective-permute-done.12.refs_1_), channel_id=1, source_target_pairs={{0,16},{1,3},{2,18},{3,5},{4,20},{5,7},{6,22},{7,9},{8,24},{9,11},... | collective-permute-start | bytes 1597448 | tf_op jit(solution)/shard_map/ppermute | solution.py:442
  99.9 11.3 %collective-permute-start.16 = (bf16[1040,256]{1,0:T(8,128)(2,1)S(1)}, bf16[1040,256]{1,0:T(8,128)(2,1)S(1)}, u32[]{:S(2)}, u32[]{:S(2)}) collective-permute-start(bf16[1040,256]{1,0:T(8,128)(2,1)S(1)} %collective-permute-done.13.refs_2_), channel_id=1, source_target_pairs={{0,112},{1,15},{2,114},{3,1},{4,116},{5,3},{6,118},{7,5},{8,120},{... | collective-permute-start | bytes 1597448 | tf_op jit(solution)/shard_map/ppermute | solution.py:442
  111.2 11.6 %collective-permute-start.17 = (bf16[1040,256]{1,0:T(8,128)(2,1)S(1)}, bf16[1040,256]{1,0:T(8,128)(2,1)S(1)}, u32[]{:S(2)}, u32[]{:S(2)}) collective-permute-start(bf16[1040,256]{1,0:T(8,128)(2,1)S(1)} %collective-permute-done.16.refs_2_), channel_id=1, source_target_pairs={{0,112},{1,15},{2,114},{3,1},{4,116},{5,3},{6,118},{7,5},{8,120},{... | collective-permute-start | bytes 1597448 | tf_op jit(solution)/shard_map/ppermute | solution.py:442
  113.5 9.2 %collective-permute-start.14 = (bf16[1024,256]{1,0:T(8,128)(2,1)S(1)}, bf16[1024,256]{1,0:T(8,128)(2,1)S(1)}, u32[]{:S(2)}, u32[]{:S(2)}) collective-permute-start(bf16[1024,256]{1,0:T(8,128)(2,1)S(1)} %collective-permute-done.10.refs_1_), channel_id=1, source_target_pairs={{0,16},{1,3},{2,18},{3,5},{4,20},{5,7},{6,22},{7,9},{8,24},{9,11},... | collective-permute-start | bytes 1572872 | tf_op jit(solution)/shard_map/ppermute | solution.py:442
  124.8 22.5 %all-to-all-start.1 = ((bf16[16,32,256]{2,1,0:T(8,128)(2,1)}), bf16[16,32,256]{2,1,0:T(8,128)(2,1)S(1)}, u32[]{:S(2)}, u32[]{:S(2)}) async-start(bf16[16,32,256]{2,1,0:T(8,128)(2,1)} %get-tuple-element.146), calls=%async_computation.1 | async-start | bytes 524288 | tf_op jit(solution)/shard_map/all_to_all | solution.py:567
  135.3 4.1 %copy-start.1 = (bf16[512,128]{1,0:T(8,128)(2,1)S(1)}, bf16[512,128]{1,0:T(8,128)(2,1)}, u32[]{:S(2)}) copy-start(bf16[512,128]{1,0:T(8,128)(2,1)} %r_4_.1) | copy-start | bytes 393220
  135.3 4.1 %copy-start.4 = (f32[128]{0:T(128)S(1)}, f32[128]{0:T(128)}, u32[]{:S(2)}) copy-start(f32[128]{0:T(128)} %param.7) | copy-start | bytes 1540
  137.7 1.8 %collective-permute-start.18 = (f32[264,128]{1,0:T(8,128)S(1)}, f32[264,128]{1,0:T(8,128)S(1)}, u32[]{:S(2)}, u32[]{:S(2)}) collective-permute-start(f32[264,128]{1,0:T(8,128)S(1)} %get-tuple-element.141), channel_id=1, source_target_pairs={{0,1},{1,0},{2,3},{3,2},{4,5},{5,4},{6,7},{7,6},{8,9},{9,8},{10,11... | collective-permute-start | bytes 405512 | tf_op jit(solution)/shard_map/ppermute | solution.py:445

commit v6 on v5

--- a/solution.py
+++ b/solution.py
@@ -160,7 +160,7 @@
     total = kv_in[...]
     squares, largest = st_in[0:1, :], st_in[1:2, :]
     for x, w in zip(xs, kvs):
-        n = w.shape[0]
+        n = len(w)
         for i in range(n):
             total = total + lax.dot_general(
                 w[i],
@@ -179,7 +179,7 @@
     half = q_in.shape[0]
     total = q_in[...]
     for x, w in zip(xs, ws):
-        for i in range(w.shape[0]):
+        for i in range(len(w)):
             total = total + jnp.dot(
                 x[i * half : (i + 1) * half, :],
                 w[i],
@@ -188,64 +188,72 @@
     return total
 
 
-def fetch(info, shifts, sems, xs, x_buf, *pairs):
-    copies = []
-    used = iter(range(sems.shape[0]))
-
-    def add(src, dst):
-        copies.append(pltpu.make_async_copy(src, dst, sems.at[next(used)]))
-
-    for i, (x, (s, k)) in enumerate(zip(xs, shifts)):
-        add(x, x_buf.at[i, pl.ds(0, x.shape[0])])
-        for whole, buf in pairs:
-            n, side = buf.shape[1], math.isqrt(whole.shape[0])
-            place = lax.rem(info[1] + (side - s % side), side)
-            add(whole.at[pl.ds(place * side + k * n, n)], buf.at[i])
+def places_of(info, shifts, whole, n):
+    side = math.isqrt(whole.shape[0])
+    return [lax.rem(info[1] + (side - s % side), side) * side + k * n for s, k in shifts]
+
+
+def blocks_from(info, shifts, whole, n):
+    return [[whole[p + j] for j in range(n)] for p in places_of(info, shifts, whole, n)]
+
+
+def fetch(info, shifts, w_all, w_buf, sems):
+    n = w_buf.shape[1]
+    copies = [
+        pltpu.make_async_copy(w_all.at[pl.ds(p, n)], w_buf.at[i], sems.at[i])
+        for i, p in enumerate(places_of(info, shifts, w_all, n))
+    ]
     for c in copies:
         c.start()
+    return copies
+
+
+def arrived(copies, w_buf):
     for c in copies:
         c.wait()
-    return [x_buf.at[i, pl.ds(0, x.shape[0])] for i, x in enumerate(xs)]
+    m, n = w_buf.shape[:2]
+    return [[w_buf[i, j] for j in range(n)] for i in range(m)]
 
 
 def matmul_kernel(shifts, info, *refs):
     m = len(shifts)
     xs, w_all, kv_all = refs[:m], refs[m], refs[m + 1]
-    q_out, kv_out, st_out, x_buf, w_buf, kv_buf, sems = refs[-7:]
-    if len(refs) == m + 9:
+    q_out, kv_out, st_out, w_buf, sems = refs[-5:]
+    copies = fetch(info, shifts, w_all, w_buf, sems)
+    if len(refs) == m + 7:
         q_in, kv_in, st_in = q_out, kv_out, st_out
         for out in (q_out, kv_out, st_out):
             out[...] = jnp.zeros_like(out)
     else:
         q_in, kv_in, st_in = refs[m + 2 : m + 5]
-    xs = fetch(info, shifts, sems, xs, x_buf, (w_all, w_buf), (kv_all, kv_buf))
-    ws, kvs = [w_buf.at[i] for i in range(m)], [kv_buf.at[i] for i in range(m)]
-    q_out[...] = q_sum(xs, ws, q_in)
+    n = xs[0].shape[0] // xs[0].shape[1]
+    kvs = blocks_from(info, shifts, kv_all, n)
     total, squares, largest = kv_rows(xs, kvs, kv_in, st_in)
     kv_out[...] = total
     st_out[0:1, :] = squares
     st_out[1:2, :] = largest
-
-
-def arrivals_call(kernel, out_shape, info, xs, big, rest, flops, aliases=None):
+    q_out[...] = q_sum(xs, arrived(copies, w_buf), q_in)
+
+
+def arrivals_call(kernel, out_shape, info, xs, w_all, rest, flops, aliases=None):
     m = len(xs)
     n = xs[0].shape[0] // xs[0].shape[1]
-    hbm = pl.BlockSpec(memory_space=pltpu.HBM)
     vmem = pl.BlockSpec(memory_space=pltpu.VMEM)
     smem = pl.BlockSpec(memory_space=pltpu.SMEM)
-    scratch = [pltpu.VMEM((m, max(x.shape[0] for x in xs), xs[0].shape[1]), BF16)]
-    scratch += [pltpu.VMEM((m, n) + w.shape[1:], BF16) for w in big]
-    count = m * (1 + len(big))
+    w, scratch = [], []
+    if w_all is not None:
+        w = [w_all]
+        scratch = [pltpu.VMEM((m, n) + w_all.shape[1:], BF16), pltpu.SemaphoreType.DMA((m,))]
     return pl.pallas_call(
         kernel,
         out_shape=out_shape,
-        in_specs=[smem] + [hbm] * (m + len(big)) + [vmem] * len(rest),
+        in_specs=[smem] + [vmem] * m + [pl.BlockSpec(memory_space=pltpu.HBM)] * len(w) + [vmem] * len(rest),
         out_specs=tuple(vmem for _ in out_shape),
-        scratch_shapes=scratch + [pltpu.SemaphoreType.DMA((count,))],
+        scratch_shapes=scratch,
         input_output_aliases=aliases or {},
         compiler_params=pltpu.CompilerParams(vmem_limit_bytes=RING_VMEM),
         cost_estimate=pl.CostEstimate(flops=flops, bytes_accessed=10**6, transcendentals=0),
-    )(info, *xs, *big, *rest)
+    )(info, *xs, *w, *rest)
 
 
 def matmul(half, info, shifts, xs, w_all, kv_all, acc):
@@ -260,8 +268,8 @@
         out_shape,
         info,
         xs,
-        (w_all, kv_all),
-        acc,
+        w_all,
+        [kv_all, *acc],
         2 * m * xs[0].shape[0] * xs[0].shape[1] * 288,
         {3 + m + i: i for i in range(len(acc))},
     )
@@ -270,9 +278,9 @@
 def last_kv_kernel(d, shifts, info, *refs):
     m = len(shifts)
     xs, kv_all = refs[:m], refs[m]
-    kv_in, st_in, kvscale, kcos, ksin, kvt, st_out, x_buf, kv_buf, sems = refs[m + 1 :]
-    xs = fetch(info, shifts, sems, xs, x_buf, (kv_all, kv_buf))
-    t, squares, largest = kv_rows(xs, [kv_buf.at[i] for i in range(m)], kv_in, st_in)
+    kv_in, st_in, kvscale, kcos, ksin, kvt, st_out = refs[m + 1 :]
+    kvs = blocks_from(info, shifts, kv_all, xs[0].shape[0] // xs[0].shape[1])
+    t, squares, largest = kv_rows(xs, kvs, kv_in, st_in)
     st_out[0:1, :] = squares
     st_out[1:2, :] = largest
     t = t * (1.0 / jnp.sqrt(squares / d + norm_eps))
@@ -300,8 +308,8 @@
         out_shape,
         info,
         xs,
-        (kv_all,),
-        [kv, st, kvscale, kcos, ksin],
+        None,
+        [kv_all, kv, st, kvscale, kcos, ksin],
         10**9,
     )
 
@@ -309,9 +317,8 @@
 def last_q_kernel(d, shifts, info, *refs):
     m = len(shifts)
     xs, w_all = refs[:m], refs[m]
-    q_in, st, wscale, cosine, sine, mine, msg, x_buf, w_buf, sems = refs[m + 1 :]
-    xs = fetch(info, shifts, sems, xs, x_buf, (w_all, w_buf))
-    q = q_sum(xs, [w_buf.at[i] for i in range(m)], q_in)
+    q_in, st, wscale, cosine, sine, mine, msg, w_buf, sems = refs[m + 1 :]
+    q = q_sum(xs, arrived(fetch(info, shifts, w_all, w_buf, sems), w_buf), q_in)
     half = q.shape[0]
     squares, largest = st[0:1, :], st[1:2, :]
     inv = columns_of(1.0 / jnp.sqrt(squares / d + norm_eps), 128)
@@ -340,7 +347,7 @@
         out_shape,
         info,
         xs,
-        (w_all,),
+        w_all,
         [q, st, wscale, cosine, sine],
         10**9,
     )

time: 149 us -> 150 us (level)
  waiting for transfers between devices: 49.5 us -> 46.5 us
  Pallas kernels: 36.2 us -> 38.1 us
  starting transfers between devices: 56.4 us -> 58 us
    ppermute x14, waiting for transfers between devices: 12.1 us -> 9.09 us  [second(): return lax.ppermute(v, 'tp', pairs)]
    pallas_call x9, Pallas kernels: 22.4 us -> 24.3 us  [arrivals_call(): pl.pallas_call(kernel, out_shape=out_shape, in_specs=[smem] + [vmem] * m...]
  transfers between devices with their start and end apart: 21 -> 21, of which waited for: 11 -> 8; matrix products, arithmetic and copies ran while one was open for 2% -> 2% of each run, Pallas kernels for 22% -> 23%
where the time goes in v6:
time: 150 us; the launch traced here: 149 us
  starting transfers between devices  58 us (39%)
  waiting for transfers between devices  46.5 us (31%)
  Pallas kernels  38.1 us (25%)
  other arithmetic  2.53 us (2%)
  local copies, waits for them, and re-layouts  2.48 us (2%)
  between operations  1.71 us (1%)
    ppermute x1, waiting for transfers between devices, body(): lax.ppermute(jnp.concatenate([w_kv, scales], axis=1), 'tp', to_row)  26.4 us
    pallas_call x9, Pallas kernels, arrivals_call(): pl.pallas_call(kernel, out_shape=out_shape, in_specs=[smem] + [vmem] * m...  24.3 us
    ppermute x4, starting transfers between devices, swap(): return lax.ppermute(v, 'tp', to_partner)  23.2 us
    ppermute x14, starting transfers between devices, second(): return lax.ppermute(v, 'tp', pairs)  19.3 us
    all_to_all x1, starting transfers between devices, body(): lax.all_to_all(kvt, 'tp', split_axis=0, concat_axis=0, tiled=False, axis_...  11.4 us
    ppermute x14, waiting for transfers between devices, second(): return lax.ppermute(v, 'tp', pairs)  9.09 us
    pallas_call x1, Pallas kernels, arrange_weights(): pl.pallas_call(weights_kernel, out_shape=out, in_specs=[pl.BlockSpec(memo...  8.77 us
    all_to_all x1, waiting for transfers between devices, body(): lax.all_to_all(kvt, 'tp', split_axis=0, concat_axis=0, tiled=False, axis_...  6.39 us
  transfers between devices with their start and end apart: 21, of which 8 were waited for; matrix products, arithmetic and copies ran while one was open for 2% of the time, Pallas kernels for 23%

profile of v6, /device:TPU:513, one launch (start us, length us, event | category | flops | bytes accessed | tf_op | source)
XLA Modules:
  0.0 149.3 jit_solution(12793672933254895073)
XLA Ops:
  0.6 20.5 %collective-permute-start.1 = (bf16[16384,128]{1,0:T(8,128)(2,1)}, bf16[16384,128]{1,0:T(8,128)(2,1)}, u32[]{:S(2)}, u32[]{:S(2)}) collective-permute-start(bf16[16384,128]{1,0:T(8,128)(2,1)} %param.9), channel_id=1, source_target_pairs={{0,1},{1,0},{2,3},{3,2},{4,5},{5,4},{6,7},{7,6},{8,9},{9,8},{10,11... | collective-permute-start | bytes 12582920 | tf_op jit(solution)/shard_map/ppermute | solution.py:452
  21.2 0.9 copy-done
  22.1 0.7 copy-done.3
  22.7 0.2 shard_map.101
  22.9 0.2 collective-permute-start
  23.1 0.7 convert_bitcast_fusion.2
  23.8 0.7 convert_bitcast_fusion.1
  24.5 0.1 copy.32
  24.6 3.7 %collective-permute-done.recv = bf16[272,128]{1,0:T(8,128)(2,1)S(1)} collective-permute-done((bf16[272,128]{1,0:T(8,128)(2,1)S(1)}, bf16[272,128]{1,0:T(8,128)(2,1)S(1)}, u32[]{:S(2)}, u32[]{:S(2)}) %collective-permute-start) | collective-permute-done | bytes 69664 | tf_op jit(solution)/shard_map/ppermute | solution.py:452
  28.3 1.1 shard_map.102
  29.4 3.9 %all-to-all-start = ((bf16[8,272,256]{2,1,0:T(8,128)(2,1)}), bf16[8,272,256]{2,1,0:T(8,128)(2,1)S(1)}, u32[]{:S(2)}, u32[]{:S(2)}) async-start(bf16[8,272,256]{2,1,0:T(8,128)(2,1)} %shard_map.102), calls=%async_computation | async-start | bytes 2228224 | tf_op jit(solution)/shard_map/all_to_all | solution.py:489
  33.4 0.0 copy-start.6
  33.4 0.1 collective-permute-start.4
  34.4 0.1 fusion.17
  34.5 0.6 pad_add_fusion.info.core.refs_0_.r_0_
  35.1 0.1 multiply_sine_fusion.2
  35.3 1.0 multiply_sine_fusion
  36.2 26.4 %collective-permute-done.4.kv = bf16[16,16512]{1,0:T(8,128)(2,1)S(1)} collective-permute-done((bf16[16,16512]{1,0:T(8,128)(2,1)S(1)}, bf16[16,16512]{1,0:T(8,128)(2,1)S(1)}, u32[]{:S(2)}, u32[]{:S(2)}) %collective-permute-start.4) | collective-permute-done | bytes 528416 | tf_op jit(solution)/shard_map/ppermute | solution.py:480
  62.6 1.7 %collective-permute-start.5 = (bf16[16,16512]{1,0:T(8,128)(2,1)S(1)}, bf16[16,16512]{1,0:T(8,128)(2,1)S(1)}, u32[]{:S(2)}, u32[]{:S(2)}) collective-permute-start(bf16[16,16512]{1,0:T(8,128)(2,1)S(1)} %collective-permute-done.4.kv), channel_id=1, source_target_pairs={{0,1},{1,0},{2,3},{3,2},{4,5},{5,4},{6,7},{7,6},{8,9},{9,8},{10,11... | collective-permute-start | bytes 1585160 | tf_op jit(solution)/shard_map/ppermute | solution.py:452
  64.3 0.0 collective-permute-done.1
  64.3 8.8 %shard_map.103.refs_3_ = bf16[64,256,256]{2,1,0:T(8,128)(2,1)} custom-call(s32[2]{0:T(128)} %pad_add_fusion.info.core.refs_0_.r_0_, bf16[64,256,128]{2,1,0:T(8,128)(2,1)} %bitcast.22, bf16[64,256,128]{2,1,0:T(8,128)(2,1)} %bitcast.4.wo), custom_call_target="tpu_custom_call" | custom-call | flops 1000000000 | bytes 20000000 | tf_op jit(solution)/shard_map/pallas_call | solution.py:108
  73.1 0.0 all-to-all-done.gathered
  73.1 0.0 copy-start.2
  73.2 0.1 collective-permute-start.2
  73.3 2.6 %collective-permute-start.3 = (bf16[1024,256]{1,0:T(8,128)(2,1)S(1)}, bf16[1024,256]{1,0:T(8,128)(2,1)S(1)}, u32[]{:S(2)}, u32[]{:S(2)}) collective-permute-start(bf16[1024,256]{1,0:T(8,128)(2,1)S(1)} %bitcast.18), channel_id=1, source_target_pairs={{0,112},{1,15},{2,114},{3,1},{4,116},{5,3},{6,118},{7,5},{8,120},{... | collective-permute-start | bytes 1572872 | tf_op jit(solution)/shard_map/ppermute | solution.py:449
  76.0 0.1 shard_map.104.refs_2_
  76.0 0.1 collective-permute-start.8
  76.2 2.6 %collective-permute-start.9 = (bf16[1040,256]{1,0:T(8,128)(2,1)S(1)}, bf16[1040,256]{1,0:T(8,128)(2,1)S(1)}, u32[]{:S(2)}, u32[]{:S(2)}) collective-permute-start(bf16[1040,256]{1,0:T(8,128)(2,1)S(1)} %shard_map.104.refs_2_), channel_id=1, source_target_pairs={{0,112},{1,15},{2,114},{3,1},{4,116},{5,3},{6,118},{7,5},{8,120},{... | collective-permute-start | bytes 1597448 | tf_op jit(solution)/shard_map/ppermute | solution.py:449
  78.8 0.0 collective-permute-done.5.ko
  78.8 0.7 shard_map.105
  79.5 2.9 %shard_map.106 = (f32[256,256]{1,0:T(8,128)S(1)}, f32[32,256]{1,0:T(8,128)S(1)}, f32[8,256]{1,0:T(8,128)S(1)}) custom-call(s32[2]{0:T(128)S(1)} %copy-done.2, bf16[1024,256]{1,0:T(8,128)(2,1)S(1)} %bitcast.19, bf16[1040,256]{1,0:T(8,128)(2,1)S(1)} %shard_map.104.refs_2_, bf16[64,256,256]{2,1,0:T(8,128)(2,1)} %shard_map.103.refs_3_, ...), custom_call_target="tpu_custom_call" | custom-call | flops 301989888 | bytes 1000000 | tf_op jit(solution)/shard_map/pallas_call | solution.py:247
  82.4 0.4 collective-permute-done.2.refs_1_
  82.8 0.0 collective-permute-start.6
  82.8 2.7 %collective-permute-start.7 = (bf16[1024,256]{1,0:T(8,128)(2,1)S(1)}, bf16[1024,256]{1,0:T(8,128)(2,1)S(1)}, u32[]{:S(2)}, u32[]{:S(2)}) collective-permute-start(bf16[1024,256]{1,0:T(8,128)(2,1)S(1)} %collective-permute-done.3.refs_2_), channel_id=1, source_target_pairs={{0,112},{1,15},{2,114},{3,1},{4,116},{5,3},{6,118},{7,5},{8,120},{... | collective-permute-start | bytes 1572872 | tf_op jit(solution)/shard_map/ppermute | solution.py:449
  85.5 2.9 %shard_map.107 = (f32[256,256]{1,0:T(8,128)S(1)}, f32[32,256]{1,0:T(8,128)S(1)}, f32[8,256]{1,0:T(8,128)S(1)}) custom-call(s32[2]{0:T(128)S(1)} %copy-done.2, bf16[1024,256]{1,0:T(8,128)(2,1)S(1)} %collective-permute-done.2.refs_1_, bf16[1024,256]{1,0:T(8,128)(2,1)S(1)} %collective-permute-done.3.refs_2_, ...), custom_call_target="tpu_custom_call", output_to_operand_aliasing={{0}: (5, {}), {1}: (6, {}), {2}: (7, {})} | custom-call | flops 301989888 | bytes 1000000 | tf_op jit(solution)/shard_map/pallas_call | solution.py:247
  88.4 0.1 collective-permute-done.8.refs_1_
  88.5 0.0 collective-permute-done.9.refs_2_
  88.5 0.2 collective-permute-start.12
  88.7 2.6 %collective-permute-start.13 = (bf16[1040,256]{1,0:T(8,128)(2,1)S(1)}, bf16[1040,256]{1,0:T(8,128)(2,1)S(1)}, u32[]{:S(2)}, u32[]{:S(2)}) collective-permute-start(bf16[1040,256]{1,0:T(8,128)(2,1)S(1)} %collective-permute-done.9.refs_2_), channel_id=1, source_target_pairs={{0,112},{1,15},{2,114},{3,1},{4,116},{5,3},{6,118},{7,5},{8,120},{... | collective-permute-start | bytes 1597448 | tf_op jit(solution)/shard_map/ppermute | solution.py:449
  91.4 2.9 %shard_map.108 = (f32[256,256]{1,0:T(8,128)S(1)}, f32[32,256]{1,0:T(8,128)S(1)}, f32[8,256]{1,0:T(8,128)S(1)}) custom-call(s32[2]{0:T(128)S(1)} %copy-done.2, bf16[1040,256]{1,0:T(8,128)(2,1)S(1)} %collective-permute-done.8.refs_1_, bf16[1040,256]{1,0:T(8,128)(2,1)S(1)} %collective-permute-done.9.refs_2_, ...), custom_call_target="tpu_custom_call", output_to_operand_aliasing={{0}: (5, {}), {1}: (6, {}), {2}: (7, {})} | custom-call | flops 306708480 | bytes 1000000 | tf_op jit(solution)/shard_map/pallas_call | solution.py:247
  94.3 0.0 collective-permute-done.6.refs_1_
  94.3 0.1 collective-permute-start.10
  94.5 2.6 %collective-permute-start.11 = (bf16[1024,256]{1,0:T(8,128)(2,1)S(1)}, bf16[1024,256]{1,0:T(8,128)(2,1)S(1)}, u32[]{:S(2)}, u32[]{:S(2)}) collective-permute-start(bf16[1024,256]{1,0:T(8,128)(2,1)S(1)} %collective-permute-done.7.refs_2_), channel_id=1, source_target_pairs={{0,112},{1,15},{2,114},{3,1},{4,116},{5,3},{6,118},{7,5},{8,120},{... | collective-permute-start | bytes 1572872 | tf_op jit(solution)/shard_map/ppermute | solution.py:449
  97.1 2.9 %shard_map.109 = (f32[256,256]{1,0:T(8,128)S(1)}, f32[32,256]{1,0:T(8,128)S(1)}, f32[8,256]{1,0:T(8,128)S(1)}) custom-call(s32[2]{0:T(128)S(1)} %copy-done.2, bf16[1024,256]{1,0:T(8,128)(2,1)S(1)} %collective-permute-done.6.refs_1_, bf16[1024,256]{1,0:T(8,128)(2,1)S(1)} %collective-permute-done.7.refs_2_, ...), custom_call_target="tpu_custom_call", output_to_operand_aliasing={{0}: (5, {}), {1}: (6, {}), {2}: (7, {})} | custom-call | flops 301989888 | bytes 1000000 | tf_op jit(solution)/shard_map/pallas_call | solution.py:247
  100.0 0.0 collective-permute-done.12.refs_1_
  100.0 0.1 collective-permute-start.15
  100.2 2.6 %collective-permute-start.16 = (bf16[1040,256]{1,0:T(8,128)(2,1)S(1)}, bf16[1040,256]{1,0:T(8,128)(2,1)S(1)}, u32[]{:S(2)}, u32[]{:S(2)}) collective-permute-start(bf16[1040,256]{1,0:T(8,128)(2,1)S(1)} %collective-permute-done.13.refs_2_), channel_id=1, source_target_pairs={{0,112},{1,15},{2,114},{3,1},{4,116},{5,3},{6,118},{7,5},{8,120},{... | collective-permute-start | bytes 1597448 | tf_op jit(solution)/shard_map/ppermute | solution.py:449
  102.8 2.9 %shard_map.110 = (f32[256,256]{1,0:T(8,128)S(1)}, f32[32,256]{1,0:T(8,128)S(1)}, f32[8,256]{1,0:T(8,128)S(1)}) custom-call(s32[2]{0:T(128)S(1)} %copy-done.2, bf16[1040,256]{1,0:T(8,128)(2,1)S(1)} %collective-permute-done.12.refs_1_, ...), custom_call_target="tpu_custom_call", output_to_operand_aliasing={{0}: (5, {}), {1}: (6, {}), {2}: (7, {})} | custom-call | flops 306708480 | bytes 1000000 | tf_op jit(solution)/shard_map/pallas_call | solution.py:247
  105.8 0.0 collective-permute-done.10.refs_1_
  105.8 2.9 %shard_map.111 = (f32[256,256]{1,0:T(8,128)S(1)}, f32[32,256]{1,0:T(8,128)S(1)}, f32[8,256]{1,0:T(8,128)S(1)}) custom-call(s32[2]{0:T(128)S(1)} %copy-done.2, bf16[1024,256]{1,0:T(8,128)(2,1)S(1)} %collective-permute-done.10.refs_1_, ...), custom_call_target="tpu_custom_call", output_to_operand_aliasing={{0}: (5, {}), {1}: (6, {}), {2}: (7, {})} | custom-call | flops 301989888 | bytes 1000000 | tf_op jit(solution)/shard_map/pallas_call | solution.py:247
  108.7 2.2 %collective-permute-done.15.refs_1_ = bf16[1040,256]{1,0:T(8,128)(2,1)S(1)} collective-permute-done((bf16[1040,256]{1,0:T(8,128)(2,1)S(1)}, bf16[1040,256]{1,0:T(8,128)(2,1)S(1)}, u32[]{:S(2)}, u32[]{:S(2)}) %collective-permute-start.15) | collective-permute-done | bytes 532512 | tf_op jit(solution)/shard_map/ppermute | solution.py:449
  110.9 0.0 collective-permute-done.16.refs_2_
  110.9 2.7 %collective-permute-start.17 = (bf16[1040,256]{1,0:T(8,128)(2,1)S(1)}, bf16[1040,256]{1,0:T(8,128)(2,1)S(1)}, u32[]{:S(2)}, u32[]{:S(2)}) collective-permute-start(bf16[1040,256]{1,0:T(8,128)(2,1)S(1)} %collective-permute-done.16.refs_2_), channel_id=1, source_target_pairs={{0,112},{1,15},{2,114},{3,1},{4,116},{5,3},{6,118},{7,5},{8,120},{... | collective-permute-start | bytes 1597448 | tf_op jit(solution)/shard_map/ppermute | solution.py:449
  113.6 2.9 %shard_map.112 = (f32[256,256]{1,0:T(8,128)S(1)}, f32[32,256]{1,0:T(8,128)S(1)}, f32[8,256]{1,0:T(8,128)S(1)}) custom-call(s32[2]{0:T(128)S(1)} %copy-done.2, bf16[1040,256]{1,0:T(8,128)(2,1)S(1)} %collective-permute-done.15.refs_1_, ...), custom_call_target="tpu_custom_call", output_to_operand_aliasing={{0}: (5, {}), {1}: (6, {}), {2}: (7, {})} | custom-call | flops 306708480 | bytes 1000000 | tf_op jit(solution)/shard_map/pallas_call | solution.py:247
  116.5 6.3 %collective-permute-done.14.refs_1_ = bf16[1024,256]{1,0:T(8,128)(2,1)S(1)} collective-permute-done((bf16[1024,256]{1,0:T(8,128)(2,1)S(1)}, bf16[1024,256]{1,0:T(8,128)(2,1)S(1)}, u32[]{:S(2)}, u32[]{:S(2)}) %collective-permute-start.14) | collective-permute-done | bytes 524320 | tf_op jit(solution)/shard_map/ppermute | solution.py:449
  122.8 1.7 %shard_map.113 = (bf16[16,32,256]{2,1,0:T(8,128)(2,1)}, f32[8,256]{1,0:T(8,128)S(1)}) custom-call(s32[2]{0:T(128)S(1)} %copy-done.2, bf16[1024,256]{1,0:T(8,128)(2,1)S(1)} %collective-permute-done.14.refs_1_, bf16[1040,256]{1,0:T(8,128)(2,1)S(1)} %collective-permute-done.17.refs_2_, bf16[64,32,256]{2,1,0:T(8,128)(2,1)S(1)} %get-tuple-element.83.refs_4_.refs_3_, ...), custom_call_target="tpu_custom_call" | custom-call | flops 1000000000 | bytes 1000000 | tf_op jit(solution)/shard_map/pallas_call | solution.py:247
  124.5 11.4 %all-to-all-start.1 = ((bf16[16,32,256]{2,1,0:T(8,128)(2,1)}), bf16[16,32,256]{2,1,0:T(8,128)(2,1)S(1)}, u32[]{:S(2)}, u32[]{:S(2)}) async-start(bf16[16,32,256]{2,1,0:T(8,128)(2,1)} %get-tuple-element.146), calls=%async_computation.1 | async-start | bytes 524288 | tf_op jit(solution)/shard_map/all_to_all | solution.py:574
  136.0 0.0 copy-start.4
  136.0 2.3 %shard_map.114 = (bf16[256,128]{1,0:T(8,128)(2,1)S(1)}, f32[264,128]{1,0:T(8,128)S(1)}) custom-call(s32[2]{0:T(128)S(1)} %copy-done.2, bf16[1024,256]{1,0:T(8,128)(2,1)S(1)} %collective-permute-done.14.refs_1_, bf16[1040,256]{1,0:T(8,128)(2,1)S(1)} %collective-permute-done.17.refs_2_, bf16[64,256,256]{2,1,0:T(8,128)(2,1)} %shard_map.103.refs_3_, ...), custom_call_target="tpu_custom_call" | custom-call | flops 1000000000 | bytes 1000000 | tf_op jit(solution)/shard_map/pallas_call | solution.py:247
  138.3 0.8 collective-permute-start.18
  139.1 1.0 collective-permute-done.18.r_2_
  140.0 1.5 %shard_map.115 = (bf16[512,128]{1,0:T(8,128)(2,1)}, bf16[512,128]{1,0:T(8,128)(2,1)}, f32[4,128]{1,0:T(4,128)}) custom-call(s32[2]{0:T(128)S(1)} %copy-done.2, bf16[256,128]{1,0:T(8,128)(2,1)S(1)} %get-tuple-element.140.r_1_, f32[264,128]{1,0:T(8,128)S(1)} %collective-permute-done.18.r_2_, f32[8,256]{1,0:T(8,128)S(1)} %get-tuple-element.136.refs_5_.r_3_, ...), custom_call_target="tpu_custom_call" | custom-call | flops 100000000 | bytes 1000000 | tf_op jit(solution)/shard_map/pallas_call | solution.py:411
  141.5 6.4 %all-to-all-done.1.kvr = bf16[16,32,256]{2,1,0:T(8,128)(2,1)S(1)} async-done(((bf16[16,32,256]{2,1,0:T(8,128)(2,1)}), bf16[16,32,256]{2,1,0:T(8,128)(2,1)S(1)}, u32[]{:S(2)}, u32[]{:S(2)}) %all-to-all-start.1) | async-done | bytes 262176 | tf_op jit(solution)/shard_map/all_to_all | solution.py:574
  147.9 1.4 shard_map.116
  (23 shorter events, 0.2 us)
Async XLA Ops:
  0.6 63.7 %collective-permute-start.1 = (bf16[16384,128]{1,0:T(8,128)(2,1)}, bf16[16384,128]{1,0:T(8,128)(2,1)}, u32[]{:S(2)}, u32[]{:S(2)}) collective-permute-start(bf16[16384,128]{1,0:T(8,128)(2,1)} %param.9), channel_id=1, source_target_pairs={{0,1},{1,0},{2,3},{3,2},{4,5},{5,4},{6,7},{7,6},{8,9},{9,8},{10,11... | collective-permute-start | bytes 12582920 | tf_op jit(solution)/shard_map/ppermute | solution.py:452
  21.2 0.9 copy-start
  22.1 0.7 copy-start.3
  22.9 5.3 %collective-permute-start = (bf16[272,128]{1,0:T(8,128)(2,1)S(1)}, bf16[272,128]{1,0:T(8,128)(2,1)S(1)}, u32[]{:S(2)}, u32[]{:S(2)}) collective-permute-start(bf16[272,128]{1,0:T(8,128)(2,1)S(1)} %get-tuple-element.79), channel_id=1, source_target_pairs={{0,1},{1,0},{2,3},{3,2},{4,5},{5,4},{6,7},{7,6},{8,9},{9,8},{10,11... | collective-permute-start | bytes 208904 | tf_op jit(solution)/shard_map/ppermute | solution.py:452
  29.4 3.9 %copy-start.5 = (bf16[16,16384]{1,0:T(8,128)(2,1)S(1)}, bf16[16,16384]{1,0:T(8,128)(2,1)}, u32[]{:S(2)}) copy-start(bf16[16,16384]{1,0:T(8,128)(2,1)} %param.10) | copy-start | bytes 1572868
  29.4 43.7 %all-to-all-start = ((bf16[8,272,256]{2,1,0:T(8,128)(2,1)}), bf16[8,272,256]{2,1,0:T(8,128)(2,1)S(1)}, u32[]{:S(2)}, u32[]{:S(2)}) async-start(bf16[8,272,256]{2,1,0:T(8,128)(2,1)} %shard_map.102), calls=%async_computation | async-start | bytes 2228224 | tf_op jit(solution)/shard_map/all_to_all | solution.py:489
  33.4 1.2 copy-start.6
  33.4 29.2 %collective-permute-start.4 = (bf16[16,16512]{1,0:T(8,128)(2,1)S(1)}, bf16[16,16512]{1,0:T(8,128)(2,1)S(1)}, u32[]{:S(2)}, u32[]{:S(2)}) collective-permute-start(bf16[16,16512]{1,0:T(8,128)(2,1)S(1)} %fusion.1), channel_id=1, source_target_pairs={{0,14},{1,30},{2,34},{3,50},{4,70},{5,86},{6,106},{7,122},{8,6},{9... | collective-permute-start | bytes 1585160 | tf_op jit(solution)/shard_map/ppermute | solution.py:480
  62.6 16.2 %collective-permute-start.5 = (bf16[16,16512]{1,0:T(8,128)(2,1)S(1)}, bf16[16,16512]{1,0:T(8,128)(2,1)S(1)}, u32[]{:S(2)}, u32[]{:S(2)}) collective-permute-start(bf16[16,16512]{1,0:T(8,128)(2,1)S(1)} %collective-permute-done.4.kv), channel_id=1, source_target_pairs={{0,1},{1,0},{2,3},{3,2},{4,5},{5,4},{6,7},{7,6},{8,9},{9,8},{10,11... | collective-permute-start | bytes 1585160 | tf_op jit(solution)/shard_map/ppermute | solution.py:452
  73.1 5.7 %copy-start.2 = (s32[2]{0:T(128)S(1)}, s32[2]{0:T(128)}, u32[]{:S(2)}) copy-start(s32[2]{0:T(128)} %pad_add_fusion.info.core.refs_0_.r_0_) | copy-start | bytes 28
  73.2 9.7 %collective-permute-start.2 = (bf16[1024,256]{1,0:T(8,128)(2,1)S(1)}, bf16[1024,256]{1,0:T(8,128)(2,1)S(1)}, u32[]{:S(2)}, u32[]{:S(2)}) collective-permute-start(bf16[1024,256]{1,0:T(8,128)(2,1)S(1)} %bitcast.17), channel_id=1, source_target_pairs={{0,16},{1,3},{2,18},{3,5},{4,20},{5,7},{6,22},{7,9},{8,24},{9,11},... | collective-permute-start | bytes 1572872 | tf_op jit(solution)/shard_map/ppermute | solution.py:449
  73.3 9.5 %collective-permute-start.3 = (bf16[1024,256]{1,0:T(8,128)(2,1)S(1)}, bf16[1024,256]{1,0:T(8,128)(2,1)S(1)}, u32[]{:S(2)}, u32[]{:S(2)}) collective-permute-start(bf16[1024,256]{1,0:T(8,128)(2,1)S(1)} %bitcast.18), channel_id=1, source_target_pairs={{0,112},{1,15},{2,114},{3,1},{4,116},{5,3},{6,118},{7,5},{8,120},{... | collective-permute-start | bytes 1572872 | tf_op jit(solution)/shard_map/ppermute | solution.py:449
  76.0 12.5 %collective-permute-start.8 = (bf16[1040,256]{1,0:T(8,128)(2,1)S(1)}, bf16[1040,256]{1,0:T(8,128)(2,1)S(1)}, u32[]{:S(2)}, u32[]{:S(2)}) collective-permute-start(bf16[1040,256]{1,0:T(8,128)(2,1)S(1)} %shard_map.104.refs_2_), channel_id=1, source_target_pairs={{0,16},{1,3},{2,18},{3,5},{4,20},{5,7},{6,22},{7,9},{8,24},{9,11},... | collective-permute-start | bytes 1597448 | tf_op jit(solution)/shard_map/ppermute | solution.py:449
  76.2 12.4 %collective-permute-start.9 = (bf16[1040,256]{1,0:T(8,128)(2,1)S(1)}, bf16[1040,256]{1,0:T(8,128)(2,1)S(1)}, u32[]{:S(2)}, u32[]{:S(2)}) collective-permute-start(bf16[1040,256]{1,0:T(8,128)(2,1)S(1)} %shard_map.104.refs_2_), channel_id=1, source_target_pairs={{0,112},{1,15},{2,114},{3,1},{4,116},{5,3},{6,118},{7,5},{8,120},{... | collective-permute-start | bytes 1597448 | tf_op jit(solution)/shard_map/ppermute | solution.py:449
  82.8 11.5 %collective-permute-start.6 = (bf16[1024,256]{1,0:T(8,128)(2,1)S(1)}, bf16[1024,256]{1,0:T(8,128)(2,1)S(1)}, u32[]{:S(2)}, u32[]{:S(2)}) collective-permute-start(bf16[1024,256]{1,0:T(8,128)(2,1)S(1)} %collective-permute-done.2.refs_1_), channel_id=1, source_target_pairs={{0,16},{1,3},{2,18},{3,5},{4,20},{5,7},{6,22},{7,9},{8,24},{9,11},... | collective-permute-start | bytes 1572872 | tf_op jit(solution)/shard_map/ppermute | solution.py:449
  82.8 11.5 %collective-permute-start.7 = (bf16[1024,256]{1,0:T(8,128)(2,1)S(1)}, bf16[1024,256]{1,0:T(8,128)(2,1)S(1)}, u32[]{:S(2)}, u32[]{:S(2)}) collective-permute-start(bf16[1024,256]{1,0:T(8,128)(2,1)S(1)} %collective-permute-done.3.refs_2_), channel_id=1, source_target_pairs={{0,112},{1,15},{2,114},{3,1},{4,116},{5,3},{6,118},{7,5},{8,120},{... | collective-permute-start | bytes 1572872 | tf_op jit(solution)/shard_map/ppermute | solution.py:449
  88.5 11.5 %collective-permute-start.12 = (bf16[1040,256]{1,0:T(8,128)(2,1)S(1)}, bf16[1040,256]{1,0:T(8,128)(2,1)S(1)}, u32[]{:S(2)}, u32[]{:S(2)}) collective-permute-start(bf16[1040,256]{1,0:T(8,128)(2,1)S(1)} %collective-permute-done.8.refs_1_), channel_id=1, source_target_pairs={{0,16},{1,3},{2,18},{3,5},{4,20},{5,7},{6,22},{7,9},{8,24},{9,11},... | collective-permute-start | bytes 1597448 | tf_op jit(solution)/shard_map/ppermute | solution.py:449
  88.7 11.3 %collective-permute-start.13 = (bf16[1040,256]{1,0:T(8,128)(2,1)S(1)}, bf16[1040,256]{1,0:T(8,128)(2,1)S(1)}, u32[]{:S(2)}, u32[]{:S(2)}) collective-permute-start(bf16[1040,256]{1,0:T(8,128)(2,1)S(1)} %collective-permute-done.9.refs_2_), channel_id=1, source_target_pairs={{0,112},{1,15},{2,114},{3,1},{4,116},{5,3},{6,118},{7,5},{8,120},{... | collective-permute-start | bytes 1597448 | tf_op jit(solution)/shard_map/ppermute | solution.py:449
  94.3 11.4 %collective-permute-start.10 = (bf16[1024,256]{1,0:T(8,128)(2,1)S(1)}, bf16[1024,256]{1,0:T(8,128)(2,1)S(1)}, u32[]{:S(2)}, u32[]{:S(2)}) collective-permute-start(bf16[1024,256]{1,0:T(8,128)(2,1)S(1)} %collective-permute-done.6.refs_1_), channel_id=1, source_target_pairs={{0,16},{1,3},{2,18},{3,5},{4,20},{5,7},{6,22},{7,9},{8,24},{9,11},... | collective-permute-start | bytes 1572872 | tf_op jit(solution)/shard_map/ppermute | solution.py:449
  94.5 11.3 %collective-permute-start.11 = (bf16[1024,256]{1,0:T(8,128)(2,1)S(1)}, bf16[1024,256]{1,0:T(8,128)(2,1)S(1)}, u32[]{:S(2)}, u32[]{:S(2)}) collective-permute-start(bf16[1024,256]{1,0:T(8,128)(2,1)S(1)} %collective-permute-done.7.refs_2_), channel_id=1, source_target_pairs={{0,112},{1,15},{2,114},{3,1},{4,116},{5,3},{6,118},{7,5},{8,120},{... | collective-permute-start | bytes 1572872 | tf_op jit(solution)/shard_map/ppermute | solution.py:449
  100.0 10.9 %collective-permute-start.15 = (bf16[1040,256]{1,0:T(8,128)(2,1)S(1)}, bf16[1040,256]{1,0:T(8,128)(2,1)S(1)}, u32[]{:S(2)}, u32[]{:S(2)}) collective-permute-start(bf16[1040,256]{1,0:T(8,128)(2,1)S(1)} %collective-permute-done.12.refs_1_), channel_id=1, source_target_pairs={{0,16},{1,3},{2,18},{3,5},{4,20},{5,7},{6,22},{7,9},{8,24},{9,11},... | collective-permute-start | bytes 1597448 | tf_op jit(solution)/shard_map/ppermute | solution.py:449
  100.2 10.7 %collective-permute-start.16 = (bf16[1040,256]{1,0:T(8,128)(2,1)S(1)}, bf16[1040,256]{1,0:T(8,128)(2,1)S(1)}, u32[]{:S(2)}, u32[]{:S(2)}) collective-permute-start(bf16[1040,256]{1,0:T(8,128)(2,1)S(1)} %collective-permute-done.13.refs_2_), channel_id=1, source_target_pairs={{0,112},{1,15},{2,114},{3,1},{4,116},{5,3},{6,118},{7,5},{8,120},{... | collective-permute-start | bytes 1597448 | tf_op jit(solution)/shard_map/ppermute | solution.py:449
  110.9 11.9 %collective-permute-start.17 = (bf16[1040,256]{1,0:T(8,128)(2,1)S(1)}, bf16[1040,256]{1,0:T(8,128)(2,1)S(1)}, u32[]{:S(2)}, u32[]{:S(2)}) collective-permute-start(bf16[1040,256]{1,0:T(8,128)(2,1)S(1)} %collective-permute-done.16.refs_2_), channel_id=1, source_target_pairs={{0,112},{1,15},{2,114},{3,1},{4,116},{5,3},{6,118},{7,5},{8,120},{... | collective-permute-start | bytes 1597448 | tf_op jit(solution)/shard_map/ppermute | solution.py:449
  113.5 9.2 %collective-permute-start.14 = (bf16[1024,256]{1,0:T(8,128)(2,1)S(1)}, bf16[1024,256]{1,0:T(8,128)(2,1)S(1)}, u32[]{:S(2)}, u32[]{:S(2)}) collective-permute-start(bf16[1024,256]{1,0:T(8,128)(2,1)S(1)} %collective-permute-done.10.refs_1_), channel_id=1, source_target_pairs={{0,16},{1,3},{2,18},{3,5},{4,20},{5,7},{6,22},{7,9},{8,24},{9,11},... | collective-permute-start | bytes 1572872 | tf_op jit(solution)/shard_map/ppermute | solution.py:449
  124.5 23.4 %all-to-all-start.1 = ((bf16[16,32,256]{2,1,0:T(8,128)(2,1)}), bf16[16,32,256]{2,1,0:T(8,128)(2,1)S(1)}, u32[]{:S(2)}, u32[]{:S(2)}) async-start(bf16[16,32,256]{2,1,0:T(8,128)(2,1)} %get-tuple-element.146), calls=%async_computation.1 | async-start | bytes 524288 | tf_op jit(solution)/shard_map/all_to_all | solution.py:574
  136.0 4.1 %copy-start.1 = (bf16[512,128]{1,0:T(8,128)(2,1)S(1)}, bf16[512,128]{1,0:T(8,128)(2,1)}, u32[]{:S(2)}) copy-start(bf16[512,128]{1,0:T(8,128)(2,1)} %r_4_.1) | copy-start | bytes 393220
  136.0 4.1 %copy-start.4 = (f32[128]{0:T(128)S(1)}, f32[128]{0:T(128)}, u32[]{:S(2)}) copy-start(f32[128]{0:T(128)} %param.7) | copy-start | bytes 1540
  138.3 1.8 %collective-permute-start.18 = (f32[264,128]{1,0:T(8,128)S(1)}, f32[264,128]{1,0:T(8,128)S(1)}, u32[]{:S(2)}, u32[]{:S(2)}) collective-permute-start(f32[264,128]{1,0:T(8,128)S(1)} %get-tuple-element.141), channel_id=1, source_target_pairs={{0,1},{1,0},{2,3},{3,2},{4,5},{5,4},{6,7},{7,6},{8,9},{9,8},{10,11... | collective-permute-start | bytes 405512 | tf_op jit(solution)/shard_map/ppermute | solution.py:452
